TPU v7x, 32 devices: a whole 2x2x4 slice. The times are simulated.
32 devices in a mesh: groups: 2 (over y), space: 4 (over z), mp: 2 (over x), sub: 2 (over core).
Axes of the slice: x: 2, y: 2, z: 4, core: 2. Of those that a mesh axis runs over, the one named last changes fastest.
Arguments:
- voxels: bfloat16 [24576, 512], P(('groups', 'space', 'sub')), parts along dimension 0, may hold values from -6 to 6
- window_ids: int32 [24576], P(('groups', 'space', 'sub')), parts along dimension 0, may hold values from 0 to 127, as said below
- voxel_slots: int32 [24576], P(('groups', 'space', 'sub')), parts along dimension 0, may hold values from 0 to 255, as said below
- window_counts: int32 [256], P('groups'), parts along dimension 0, may hold values from 0 to 256, as said below
- norm_gain: float32 [512], replicated, may hold values from 0.25 to 1.75
- w_query_key: bfloat16 [2, 512, 512], P(None, None, 'mp'), may hold values from -2 to 2
- w_value: bfloat16 [512, 512], P(None, 'mp'), may hold values from -0.25 to 0.25
- w_out: bfloat16 [512, 512], P('mp'), may hold values from -0.25 to 0.25
- ffn_gain: float32 [512], replicated, may hold values from 0.25 to 1.75
- w_up: bfloat16 [512, 2048], P(None, 'mp'), may hold values from -0.25 to 0.25
- w_down: bfloat16 [2048, 512], P('mp'), may hold values from -0.125 to 0.125
Outputs:
- result: bfloat16 [24576, 512], P(('groups', 'space', 'sub'), 'mp'), parts along dimension 0
There are 2 independent parts, one for each index of `groups`. A program takes and returns all parts, laid end to end along the dimension named above; an argument that names none is the same for every part. Nothing has to cross between parts.
Inputs may be any that keep to these rules, and one draw needn't show every extreme that they name: `window_ids`: window w belongs to owner w // 16 (its index along space+sub) as that owner's window w % 16. On the voxels of one device at most 384 lie in windows of one owner, and in every draw some owner has exactly 384 voxels of every device. `voxel_slots`: the voxels of a window hold slots 0 to its count - 1, each once. window_counts[w] is the number of voxels with window id w; some window holds 256.
All inputs are finite; a program needn't handle non-finite values.
Results may differ from a plain program's by a relative error of at most 0.012.
Values may be sent and summed in bfloat16 or wider, within the bound.
No kernel may reach another device: no remote copies, remote signals or barrier semaphores. Data moves between devices by JAX's collectives and lax.ppermute only.
A program may use at most 128 MiB of HBM per device.

v0:
```python
import functools

import jax
import jax.numpy as jnp
from jax import lax
from jax.experimental import pallas as pl
from jax.experimental.pallas import tpu as pltpu
from jax.sharding import PartitionSpec as P


HDIM = 64
WLEN = 256
WIN_DEV = 16
META = 16
LANES = 128
OWN = ("space", "sub")


F32 = jnp.float32
BF16 = jnp.bfloat16
VM = pl.BlockSpec(memory_space=pltpu.VMEM)
PARAMS = pltpu.CompilerParams(vmem_limit_bytes=20 * 1024 * 1024)


class Steps:
    def __init__(self, n):
        self.n = n
        self.xor = n & (n - 1) == 0

    def to(self, i, k):
        return i ^ k if self.xor else (i + k) % self.n

    def frm(self, i, k):
        return i ^ k if self.xor else (i + self.n - k) % self.n

    def step(self, i, owner):
        return owner ^ i if self.xor else (owner + self.n - i) % self.n

    def perm(self, k, back=False):
        go = self.frm if back else self.to
        return [(i, go(i, k)) for i in range(self.n)]


def layer_norm(values_in, gain):
    row_mean = jnp.mean(values_in, axis=-1, keepdims=True)
    centred = values_in - row_mean
    variance = jnp.mean(centred * centred, axis=-1, keepdims=True)
    return centred * lax.rsqrt(variance + 1e-05) * gain


def dot(a, b):
    return jnp.dot(a, b, preferred_element_type=F32)


def own_index(sub_size):
    return lax.axis_index("space") * sub_size + lax.axis_index("sub")


def pack_kernel(ids_ref, vox_ref, gain_ref, *refs, steps, sub_size, near, cap, wins):
    n = steps.n
    col_ref, outs, normed_ref, cnt_ref = refs[0], refs[1 : 1 + n], refs[1 + n], refs[2 + n]
    rows, _ = vox_ref.shape
    me = own_index(sub_size)
    mp = lax.axis_index("mp")
    normed_ref[...] = layer_norm(vox_ref[...].astype(F32), gain_ref[...]).astype(BF16)
    ids = ids_ref[...]
    step = 256
    win_iota = lax.broadcasted_iota(jnp.int32, (wins, step), 0)
    upper = (
        lax.broadcasted_iota(jnp.int32, (step, step), 0)
        < lax.broadcasted_iota(jnp.int32, (step, step), 1)
    ).astype(F32).astype(BF16)
    hots, counts = [], jnp.zeros((wins, 1), F32)
    for b in range(rows // step):
        hot = (ids[:, b * step : (b + 1) * step] == win_iota).astype(F32)
        hots.append(hot)
        counts = counts + jnp.sum(hot, axis=1, keepdims=True)
    wide = jnp.broadcast_to(counts, (wins, LANES))
    cnt_ref[...] = wide
    r_io = lax.broadcasted_iota(jnp.int32, (wins, wins), 0)
    c_io = lax.broadcasted_iota(jnp.int32, (wins, wins), 1)
    same = (r_io // WIN_DEV == c_io // WIN_DEV) & (c_io < r_io)
    carry = dot(same.astype(F32).astype(BF16), wide.astype(BF16))[:, :1]
    ranks = []
    for hot in hots:
        cum = dot(hot.astype(BF16), upper) + carry
        ranks.append(jnp.sum(hot * cum, axis=0, keepdims=True))
        carry = carry + jnp.sum(hot, axis=1, keepdims=True)
    rank = jnp.concatenate(ranks, axis=1).astype(jnp.int32)
    dest = steps.step(me, ids // WIN_DEV) * cap + rank
    col_ref[...] = jnp.transpose(jnp.broadcast_to(dest.astype(F32), (LANES, rows))).astype(jnp.int32)
    row_iota = lax.broadcasted_iota(jnp.int32, (cap, rows), 0)
    for k in range(n):
        out = outs[k]
        piece = out.shape[1]
        pick = (dest == row_iota + k * cap).astype(F32).astype(BF16)
        if k < near:
            source = normed_ref[...]
        else:
            source = normed_ref[:, pl.ds(pl.multiple_of(mp * piece, LANES), piece)]
        out[0:cap, :] = dot(pick, source).astype(BF16)
        owner = steps.to(me, k)
        tail = cnt_ref[pl.ds(pl.multiple_of(owner * WIN_DEV, WIN_DEV), WIN_DEV), :]
        out[cap : cap + META, :] = jnp.concatenate([tail] * (piece // LANES), axis=1).astype(BF16)


def places(tails, cap):
    base = jnp.zeros((META, 1), F32)
    lower = (
        lax.broadcasted_iota(jnp.int32, (META, META), 1)
        < lax.broadcasted_iota(jnp.int32, (META, META), 0)
    ).astype(F32).astype(BF16)
    row = lax.broadcasted_iota(jnp.int32, (META, cap), 1).astype(F32)
    win = lax.broadcasted_iota(jnp.int32, (META, 1), 0).astype(F32) * WLEN
    out = []
    for tail in tails:
        start = dot(lower, tail)[:, :1]
        count = tail.astype(F32)[:, :1]
        inside = (row >= start) & (row < start + count)
        value = jnp.where(inside, win + base - start + row + 1.0, 0.0)
        out.append((jnp.sum(value, axis=0, keepdims=True) - 1.0).astype(jnp.int32))
        base = base + count
    return out


def read_piece(refs, t, piece, cap, block):
    if len(refs) == 1:
        return refs[0][0:cap, pl.ds(pl.multiple_of(block * piece, LANES), piece)]
    return refs[t][0:cap, :]


def window_bits(tail):
    power = jnp.left_shift(1, lax.broadcasted_iota(jnp.int32, (META, LANES), 0)).astype(F32)
    lane = lax.broadcasted_iota(jnp.int32, (META, LANES), 1)
    return jnp.sum(jnp.where((tail.astype(F32) > 0) & (lane == 0), power, 0.0)).astype(jnp.int32)


def split_refs(refs, at, parts):
    out = []
    for width in parts:
        out.append(refs[at : at + width])
        at += width
    return out, at


def add_rows(dest, hot, part, mp, mp_steps, piece, cap):
    for t in range(mp_steps.n):
        cols = slice(t * piece, (t + 1) * piece)
        term = dot(hot, read_piece(part, t, piece, cap, mp_steps.frm(mp, t)))
        dest[:, cols] = dest[:, cols] + term.astype(BF16)


def place_kernel(*refs, names, parts, cap, mp_steps, tails_count, piece):
    table = refs[-1]
    part_refs, _ = split_refs(refs, tails_count, parts)
    mp = lax.axis_index("mp")
    tails = [r[cap : cap + META, 0:LANES] for r in refs[:tails_count]]
    where_all = places(tails, cap)
    bits = [window_bits(tails[i]) for i in names]
    slot = lax.broadcasted_iota(jnp.int32, (WLEN, cap), 0)

    @pl.loop(0, table.shape[0] // WLEN)
    def _(w):
        rows = table.at[pl.ds(pl.multiple_of(w * WLEN, WLEN), WLEN), :]
        rows[...] = jnp.zeros(rows.shape, BF16)
        for i, name in enumerate(names):

            @pl.when((bits[i] >> w) & 1 == 1)
            def _():
                hot = (slot + w * WLEN == where_all[name]).astype(F32).astype(BF16)
                add_rows(rows, hot, part_refs[i], mp, mp_steps, piece, cap)


def attend_kernel(*refs, names, parts, cap, mp_steps, tails_count, piece, local, sub_size):
    att, pos_ref, weight_ref, member_ref = refs[-4:]
    part_refs, at = split_refs(refs, tails_count, parts)
    table_ref, wqk_ref, wv_ref, counts_ref = refs[at : at + 4]
    mp = lax.axis_index("mp")
    me = own_index(sub_size)
    tails = [r[cap : cap + META, 0:LANES] for r in refs[:tails_count]]
    where_all = places(tails, cap)
    bits = [window_bits(tails[i]) for i in names]
    for i, p in enumerate(where_all):
        pos_ref[i * cap : (i + 1) * cap, :] = jnp.transpose(
            jnp.broadcast_to(p.astype(F32), (LANES, cap))
        ).astype(jnp.int32)
    for t in range(mp_steps.n):
        block = pl.ds(pl.multiple_of(mp_steps.frm(mp, t) * piece, piece), piece)
        to = slice(t * piece, (t + 1) * piece)
        weight_ref[to, 0:local] = wqk_ref[0, block, :]
        weight_ref[to, local : 2 * local] = wqk_ref[1, block, :]
        weight_ref[to, 2 * local : 3 * local] = wv_ref[block, :]
    windows = att.shape[0] // WLEN
    slot = lax.broadcasted_iota(jnp.int32, (WLEN, cap), 0)
    low = lax.broadcasted_iota(jnp.int32, (WLEN, LANES), 1) < HDIM
    key = lax.broadcasted_iota(jnp.int32, (WLEN, WLEN), 1)
    factor = HDIM ** (-0.5) * 1.4426950408889634

    @pl.loop(0, windows)
    def _(w):
        rows = pl.ds(pl.multiple_of(w * WLEN, WLEN), WLEN)
        live = counts_ref[me * windows + w]

        @pl.when(live == 0)
        def _():
            att[rows, :] = jnp.zeros((WLEN, local), BF16)

        @pl.when(live > 0)
        def _():
            member_ref[...] = table_ref[rows, :]
            for i, name in enumerate(names):

                @pl.when((bits[i] >> w) & 1 == 1)
                def _():
                    hot = (slot + w * WLEN == where_all[name]).astype(F32).astype(BF16)
                    add_rows(member_ref, hot, part_refs[i], mp, mp_steps, piece, cap)

            qkv = dot(member_ref[...], weight_ref[...]).astype(BF16)
            zero = jnp.zeros((WLEN, LANES), BF16)
            for pair in range(local // LANES):
                q = qkv[:, pair * LANES : (pair + 1) * LANES]
                k = qkv[:, local + pair * LANES : local + (pair + 1) * LANES]
                v = qkv[:, 2 * local + pair * LANES : 2 * local + (pair + 1) * LANES]
                total, mixed = [], None
                for half in (low, ~low):
                    scores = lax.dot_general(
                        q, jnp.where(half, k, zero), (((1,), (1,)), ((), ())),
                        preferred_element_type=F32,
                    )
                    scores = jnp.where(key < live, scores, -1e30)
                    top = jnp.max(scores, axis=1, keepdims=True)
                    grown = jnp.exp2((scores - top) * factor)
                    total.append(jnp.sum(grown, axis=1, keepdims=True))
                    term = dot(grown.astype(BF16), jnp.where(half, v, zero))
                    mixed = term if mixed is None else mixed + term
                mixed = mixed / jnp.where(low, total[0], total[1])
                att[rows, pair * LANES : (pair + 1) * LANES] = mixed.astype(BF16)


def fetch_kernel(att_ref, pos_ref, *outs, names, cap):
    slots = att_ref.shape[0]
    for i, k in enumerate(names):
        pos = pos_ref[k * cap : (k + 1) * cap, :]
        lane = lax.broadcasted_iota(jnp.int32, (cap, LANES), 1)
        hot = jnp.concatenate(
            [(pos == lane + t * LANES).astype(F32).astype(BF16) for t in range(slots // LANES)],
            axis=1,
        )
        outs[i][...] = dot(hot, att_ref[...]).astype(BF16)


def spots(dest, lane, base, cap):
    tiles = []
    for t in range(-(-cap // LANES)):
        tiles.append((dest == lane + (base + t * LANES)).astype(F32).astype(BF16))
    hot = tiles[0] if len(tiles) == 1 else jnp.concatenate(tiles, axis=1)
    return hot[:, 0:cap]


def unpack_kernel(*refs, names, cap, parts, local, block_rows):
    col_ref, out_ref = refs[-2], refs[-1]
    lane = lax.broadcasted_iota(jnp.int32, (block_rows, LANES), 1)

    @pl.loop(0, out_ref.shape[0] // block_rows)
    def _(b):
        rows = pl.ds(pl.multiple_of(b * block_rows, block_rows), block_rows)
        dest = col_ref[rows, :]
        heads = [None] * parts
        for i, k in enumerate(names):
            hot = spots(dest, lane, k * cap, cap)
            for t in range(parts):
                term = dot(hot, refs[i * parts + t][...])
                heads[t] = term if heads[t] is None else heads[t] + term
        for t in range(parts):
            out_ref[rows, t * local : (t + 1) * local] = heads[t].astype(BF16)


def final_kernel(*refs, names, cap, mp_steps, sub_size, local, block_rows):
    parts = mp_steps.n
    at = len(names) * parts
    early_ref, col_ref, vox_ref, gain_ref, wout_ref, wup_ref, wdown_ref = refs[at : at + 7]
    at += 7
    extra = refs[at : at + 3 * sub_size * (parts - 1)]
    out_ref, proj_ref = refs[-2], refs[-1]
    mp = lax.axis_index("mp")
    sub = lax.axis_index("sub")
    width = vox_ref.shape[1]
    out_width = out_ref.shape[1]
    mine = pl.ds(pl.multiple_of(mp * out_width, LANES), out_width)
    proj_ref[0:local, :] = wout_ref[...]
    ups, downs = [wup_ref], [None]
    part_rows = local // sub_size
    for t in range(1, parts):
        for j in range(sub_size):
            up, down, proj = extra[3 * ((t - 1) * sub_size + j) : 3 * ((t - 1) * sub_size + j) + 3]
            ups.append(up)
            downs.append(down)
            at_row = t * local + (sub + j) % sub_size * part_rows
            proj_ref[pl.ds(pl.multiple_of(at_row, part_rows), part_rows), :] = proj[...]
    lane = lax.broadcasted_iota(jnp.int32, (block_rows, LANES), 1)

    @pl.loop(0, vox_ref.shape[0] // block_rows)
    def _(b):
        rows = pl.ds(pl.multiple_of(b * block_rows, block_rows), block_rows)
        dest = col_ref[rows, :]
        heads = [early_ref[rows, t * local : (t + 1) * local].astype(F32) for t in range(parts)]
        for i, k in enumerate(names):
            hot = spots(dest, lane, k * cap, cap)
            for t in range(parts):
                heads[t] = heads[t] + dot(hot, refs[i * parts + t][...])
        every = jnp.concatenate([h.astype(BF16) for h in heads], axis=1)
        after = vox_ref[rows, :].astype(F32) + dot(every, proj_ref[...])
        normed = layer_norm(after, gain_ref[...]).astype(BF16)
        total = None
        for up, down in zip(ups, downs):
            u = dot(normed, up[...])
            inner = u * (0.7978845608028654 + (0.7978845608028654 * 0.044715) * (u * u))
            half = 0.5 * u
            hidden = (half + half * jnp.tanh(inner)).astype(BF16)
            term = dot(hidden, wdown_ref[:, mine] if down is None else down[...])
            total = term if total is None else total + term
        keep = after[:, 0:out_width]
        for j in range(1, width // out_width):
            keep = jnp.where(mp == j, after[:, j * out_width : (j + 1) * out_width], keep)
        out_ref[rows, :] = (keep + total).astype(BF16)


def far_order(n, near):
    if n == 8 and near == 2:
        return [4, 2, 5, 3, 6, 7]
    return list(range(near, n))


def near_count(n, sub_size):
    return sub_size if Steps(n).xor else 1


def shards(
    voxels, window_ids, voxel_slots, window_counts, norm_gain, w_query_key, w_value, w_out,
    ffn_gain, w_up, w_down, *, n, mp_size, sub_size,
):
    rows, width = voxels.shape
    cap = 2 * rows // n
    steps, mp_steps = Steps(n), Steps(mp_size)
    near = near_count(n, sub_size)
    far = far_order(n, near)
    order = list(range(near)) + far
    early, late = order[:-2], order[-2:]
    piece = width // mp_size
    local = w_value.shape[1]
    mp = lax.axis_index("mp")
    sub = lax.axis_index("sub")

    def over_mp(x, t):
        return lax.ppermute(x, "mp", mp_steps.perm(t))

    bucket = cap + META
    packed = pl.pallas_call(
        functools.partial(
            pack_kernel, steps=steps, sub_size=sub_size, near=near, cap=cap, wins=n * WIN_DEV
        ),
        out_shape=[jax.ShapeDtypeStruct((rows, LANES), jnp.int32)]
        + [jax.ShapeDtypeStruct((bucket, width if k < near else piece), BF16) for k in range(n)],
        in_specs=[VM] * 3,
        out_specs=[VM] * (n + 1),
        scratch_shapes=[pltpu.VMEM((rows, width), BF16), pltpu.VMEM((n * WIN_DEV, LANES), F32)],
        compiler_params=PARAMS,
        name="pack",
    )(window_ids.reshape(1, rows), voxels, norm_gain.reshape(1, width))
    dest_col, packed = packed[0], packed[1:]

    arrived = {0: [packed[0]]}
    for k in range(1, near):
        arrived[k] = [lax.ppermute(packed[k], OWN, steps.perm(k))]
    for i, k in enumerate(far):
        sent = packed[k]
        if i >= 2:
            sent, _ = lax.optimization_barrier((sent, arrived[far[i - 2]][0]))
        got = lax.ppermute(sent, OWN, steps.perm(k))
        arrived[k] = [got] + [over_mp(got, t) for t in range(1, mp_size)]

    part = w_up.shape[1] // sub_size
    out_part = w_out.shape[0] // sub_size
    extra = []
    for t in range(1, mp_size):
        to = mp_steps.to(mp, t)
        up = over_mp(lax.dynamic_slice_in_dim(w_up, sub * part, part, 1), t)
        down = over_mp(lax.dynamic_slice(w_down, (sub * part, to * piece), (part, piece)), t)
        proj = over_mp(lax.dynamic_slice_in_dim(w_out, sub * out_part, out_part, 0), t)
        extra += [up, down, proj]
        for j in range(1, sub_size):
            share = [((i + j) % sub_size, i) for i in range(sub_size)]
            extra += [lax.ppermute(x, "sub", share) for x in (up, down, proj)]

    slots = WIN_DEV * WLEN
    flat = [x for k in early for x in arrived[k]]
    table = pl.pallas_call(
        functools.partial(
            place_kernel, names=list(range(len(early))), parts=[len(arrived[k]) for k in early],
            cap=cap, mp_steps=mp_steps, tails_count=len(early), piece=piece,
        ),
        out_shape=jax.ShapeDtypeStruct((slots, width), BF16),
        in_specs=[VM] * (len(early) + len(flat)),
        out_specs=VM,
        compiler_params=PARAMS,
        name="place",
    )(*[arrived[k][0] for k in early], *flat)
    flat = [x for k in late for x in arrived[k]]
    att, pos = pl.pallas_call(
        functools.partial(
            attend_kernel, names=[order.index(k) for k in late],
            parts=[len(arrived[k]) for k in late], cap=cap, mp_steps=mp_steps, tails_count=n,
            piece=piece, local=local, sub_size=sub_size,
        ),
        out_shape=[
            jax.ShapeDtypeStruct((slots, local), BF16),
            jax.ShapeDtypeStruct((n * cap, LANES), jnp.int32),
        ],
        in_specs=[VM] * (n + len(flat) + 3) + [pl.BlockSpec(memory_space=pltpu.SMEM)],
        out_specs=[VM, VM],
        scratch_shapes=[pltpu.VMEM((width, 3 * local), BF16), pltpu.VMEM((WLEN, width), BF16)],
        compiler_params=PARAMS,
        name="attend",
    )(*[arrived[k][0] for k in order], *flat, table, w_query_key, w_value, window_counts)

    answers = {}
    for group in (far[:2], list(range(near)) + far[2:]):
        got = pl.pallas_call(
            functools.partial(fetch_kernel, names=[order.index(k) for k in group], cap=cap),
            out_shape=[jax.ShapeDtypeStruct((cap, local), BF16) for _ in group],
            in_specs=[VM, VM],
            out_specs=[VM] * len(group),
            compiler_params=PARAMS,
            name="fetch",
        )(att, pos)
        answers.update(zip(group, got))
    returned = {}
    for i, k in enumerate(order):
        home = answers[k]
        if i >= near + 2:
            home, _ = lax.optimization_barrier((home, returned[order[i - 2]][0]))
        if k > 0:
            home = lax.ppermute(home, OWN, steps.perm(k, True))
        returned[k] = [home] + [over_mp(home, t) for t in range(1, mp_size)]

    block_rows = rows // 2
    flat = [x for k in early for x in returned[k]]
    heads = pl.pallas_call(
        functools.partial(
            unpack_kernel, names=early, cap=cap, parts=mp_size, local=local,
            block_rows=block_rows,
        ),
        out_shape=jax.ShapeDtypeStruct((rows, mp_size * local), BF16),
        in_specs=[VM] * (len(flat) + 1),
        out_specs=VM,
        compiler_params=PARAMS,
        name="unpack",
    )(*flat, dest_col)
    flat = [x for k in late for x in returned[k]]
    return pl.pallas_call(
        functools.partial(
            final_kernel, names=late, cap=cap, mp_steps=mp_steps, sub_size=sub_size, local=local,
            block_rows=block_rows,
        ),
        out_shape=jax.ShapeDtypeStruct((rows, piece), BF16),
        in_specs=[VM] * (len(flat) + 7 + len(extra)),
        out_specs=VM,
        scratch_shapes=[pltpu.VMEM((mp_size * local, width), BF16)],
        compiler_params=PARAMS,
        name="final",
    )(*flat, heads, dest_col, voxels, ffn_gain.reshape(1, width), w_out, w_up, w_down, *extra)


def solution(mesh):
    sizes = mesh.shape
    n, sub_size = sizes["space"] * sizes["sub"], sizes["sub"]

    def body(*args):
        return shards(*args, n=n, mp_size=sizes["mp"], sub_size=sub_size)

    return jax.shard_map(
        body,
        mesh=mesh,
        in_specs=(
            P(("groups", "space", "sub"), None),
            P(("groups", "space", "sub")),
            P(("groups", "space", "sub")),
            P("groups"),
            P(),
            P(None, None, "mp"),
            P(None, "mp"),
            P("mp", None),
            P(),
            P(None, "mp"),
            P("mp", None),
        ),
        out_specs=P(("groups", "space", "sub"), "mp"),
        check_vma=False,
    )
```

profile of v0, /device:TPU:9, one launch (start us, length us, event | category | flops | bytes accessed | tf_op | source)
XLA Modules:
  0.0 150.8 jit_solution(2963041184516674136)
XLA Ops:
  0.0 0.7 reshape.9.ids_ref
  0.7 1.4 copy-done.2
  2.1 0.7 copy-done.18
  2.8 5.2 %pack.1 = (s32[1536,128]{1,0:T(8,128)S(1)}, bf16[400,512]{1,0:T(8,128)(2,1)S(1)}, bf16[400,512]{1,0:T(8,128)(2,1)}, bf16[400,256]{1,0:T(8,128)(2,1)S(1)}, bf16[4...) custom-call(s32[1,1536]{1,0:T(1,128)S(1)} %reshape.9.ids_ref, ...), custom_call_target="tpu_custom_call" | custom-call | tf_op jit(solution)/shard_map/pack/pallas_call | solution.py:358
  8.0 0.9 copy-done.4
  8.9 2.5 %collective-permute-start.1 = (bf16[400,256]{1,0:T(8,128)(2,1)S(1)}, bf16[400,256]{1,0:T(8,128)(2,1)S(1)}, u32[]{:S(2)}, u32[]{:S(2)}) collective-permute-start(bf16[400,256]{1,0:T(8,128)(2,1)S(1)} %get-tuple-element.34), channel_id=1, source_target_pairs={{0,8},{1,9},{4,12},{5,13},{8,0},{9,1},{12,4},{13,5},{2,10},{3,11},... | collective-permute-start | bytes 614408 | tf_op jit(solution)/shard_map/ppermute | solution.py:379
  11.4 5.2 %collective-permute-done.2.refs_3_.refs_10_ = bf16[400,256]{1,0:T(8,128)(2,1)S(1)} collective-permute-done((bf16[400,256]{1,0:T(8,128)(2,1)S(1)}, bf16[400,256]{1,0:T(8,128)(2,1)S(1)}, u32[]{:S(2)}, u32[]{:S(2)}) %collective-permute-start.2) | collective-permute-done | bytes 204832 | tf_op jit(solution)/shard_map/ppermute | solution.py:379
  16.6 3.9 %collective-permute-start.4 = (bf16[400,256]{1,0:T(8,128)(2,1)S(1)}, bf16[400,256]{1,0:T(8,128)(2,1)S(1)}, u32[]{:S(2)}, u32[]{:S(2)}) collective-permute-start(bf16[400,256]{1,0:T(8,128)(2,1)S(1)} %get-tuple-element.39), channel_id=1, source_target_pairs={{0,5},{1,4},{4,1},{5,0},{8,13},{9,12},{12,9},{13,8},{2,7},{3,6},{6... | collective-permute-start | bytes 614408 | tf_op jit(solution)/shard_map/ppermute | solution.py:379
  20.6 3.5 %collective-permute-start.3 = (bf16[400,256]{1,0:T(8,128)(2,1)S(1)}, bf16[400,256]{1,0:T(8,128)(2,1)S(1)}, u32[]{:S(2)}, u32[]{:S(2)}) collective-permute-start(bf16[400,256]{1,0:T(8,128)(2,1)S(1)} %get-tuple-element.37), channel_id=1, source_target_pairs={{0,9},{1,8},{4,13},{5,12},{8,1},{9,0},{12,5},{13,4},{2,11},{3,10},... | collective-permute-start | bytes 614408 | tf_op jit(solution)/shard_map/ppermute | solution.py:379
  24.1 1.2 collective-permute-start.10
  25.6 2.5 %collective-permute-done.4.refs_5_.refs_14_ = bf16[400,256]{1,0:T(8,128)(2,1)S(1)} collective-permute-done((bf16[400,256]{1,0:T(8,128)(2,1)S(1)}, bf16[400,256]{1,0:T(8,128)(2,1)S(1)}, u32[]{:S(2)}, u32[]{:S(2)}) %collective-permute-start.4) | collective-permute-done | bytes 204832 | tf_op jit(solution)/shard_map/ppermute | solution.py:379
  28.1 11.3 %collective-permute-done.3.refs_4_.refs_12_ = bf16[400,256]{1,0:T(8,128)(2,1)S(1)} collective-permute-done((bf16[400,256]{1,0:T(8,128)(2,1)S(1)}, bf16[400,256]{1,0:T(8,128)(2,1)S(1)}, u32[]{:S(2)}, u32[]{:S(2)}) %collective-permute-start.3) | collective-permute-done | bytes 204832 | tf_op jit(solution)/shard_map/ppermute | solution.py:379
  39.4 1.4 collective-permute-start.12
  40.9 3.0 %collective-permute-done.6.refs_7_.refs_10_ = bf16[400,256]{1,0:T(8,128)(2,1)S(1)} collective-permute-done((bf16[400,256]{1,0:T(8,128)(2,1)}, bf16[400,256]{1,0:T(8,128)(2,1)S(1)}, u32[]{:S(2)}, u32[]{:S(2)}) %collective-permute-start.6) | collective-permute-done | bytes 204832 | tf_op jit(solution)/shard_map/ppermute | solution.py:379
  43.9 1.3 collective-permute-start.8
  45.2 4.7 %collective-permute-done.5.refs_6_.refs_8_ = bf16[400,256]{1,0:T(8,128)(2,1)S(1)} collective-permute-done((bf16[400,256]{1,0:T(8,128)(2,1)}, bf16[400,256]{1,0:T(8,128)(2,1)S(1)}, u32[]{:S(2)}, u32[]{:S(2)}) %collective-permute-start.5) | collective-permute-done | bytes 204832 | tf_op jit(solution)/shard_map/ppermute | solution.py:379
  49.9 1.2 collective-permute-start.7
  51.1 0.8 constant_dynamic-slice_fusion.1
  52.2 6.2 %place.1.refs_12_ = bf16[4096,512]{1,0:T(8,128)(2,1)S(1)} custom-call(bf16[400,512]{1,0:T(8,128)(2,1)S(1)} %get-tuple-element.32.refs_0_.refs_6_, bf16[400,512]{1,0:T(8,128)(2,1)S(1)} %collective-permute-done.refs_1_.refs_7_, bf16[400,256]{1,0:T(8,128)(2,1)S(1)} %collective-permute-done.1.refs_2_.refs_8_, ...), custom_call_target="tpu_custom_call" | custom-call | tf_op jit(solution)/shard_map/place/pallas_call | solution.py:397
  58.5 0.9 copy-done.9
  59.4 0.9 copy-done.12
  60.4 0.9 copy-done.14
  61.3 18.8 %attend.1 = (bf16[4096,256]{1,0:T(8,128)(2,1)S(1)}, s32[3072,128]{1,0:T(8,128)S(1)}) custom-call(bf16[400,512]{1,0:T(8,128)(2,1)S(1)} %get-tuple-element.32.refs_0_.refs_6_, bf16[400,512]{1,0:T(8,128)(2,1)S(1)} %collective-permute-done.refs_1_.refs_7_, bf16[400,256]{1,0:T(8,128)(2,1)S(1)} %collective-permute-done.1.refs_2_.refs_8_, ...), custom_call_target="tpu_custom_call" | custom-call | tf_op jit(solution)/shard_map/attend/pallas_call | solution.py:409
  80.1 2.5 %fetch.3 = (bf16[384,256]{1,0:T(8,128)(2,1)S(1)}, bf16[384,256]{1,0:T(8,128)(2,1)}) custom-call(bf16[4096,256]{1,0:T(8,128)(2,1)S(1)} %get-tuple-element.44.att_ref, s32[3072,128]{1,0:T(8,128)S(1)} %get-tuple-element.45.pos_ref), custom_call_target="tpu_custom_call" | custom-call | tf_op jit(solution)/shard_map/fetch/pallas_call | solution.py:428
  82.6 0.7 copy-done.21
  83.3 0.7 dynamic_slice.10
  84.0 1.2 collective-permute-start.29
  85.5 1.4 copy-done.1
  87.0 5.0 %fetch.2 = (bf16[384,256]{1,0:T(8,128)(2,1)S(1)}, bf16[384,256]{1,0:T(8,128)(2,1)S(1)}, bf16[384,256]{1,0:T(8,128)(2,1)S(1)}, bf16[384,256]{1,0:T(8,128)(2,1)S(1...) custom-call(bf16[4096,256]{1,0:T(8,128)(2,1)S(1)} %get-tuple-element.44.att_ref, s32[3072,128]{1,0:T(8,128)S(1)} %copy-done.1), custom_call_target="tpu_custom_call" | custom-call | tf_op jit(solution)/shard_map/fetch/pallas_call | solution.py:428
  92.0 5.4 %collective-permute-start.22 = (bf16[384,256]{1,0:T(8,128)(2,1)S(1)}, bf16[384,256]{1,0:T(8,128)(2,1)S(1)}, u32[]{:S(2)}, u32[]{:S(2)}) collective-permute-start(bf16[384,256]{1,0:T(8,128)(2,1)S(1)} %get-tuple-element.57), channel_id=1, source_target_pairs={{0,1},{1,0},{4,5},{5,4},{8,9},{9,8},{12,13},{13,12},{2,3},{3,2},{6... | collective-permute-start | bytes 589832 | tf_op jit(solution)/shard_map/ppermute | solution.py:443
  98.0 1.0 collective-permute-start.18
  99.0 2.0 %collective-permute-start.14 = (bf16[384,256]{1,0:T(8,128)(2,1)S(1)}, bf16[384,256]{1,0:T(8,128)(2,1)S(1)}, u32[]{:S(2)}, u32[]{:S(2)}) collective-permute-start(bf16[384,256]{1,0:T(8,128)(2,1)S(1)} %get-tuple-element.49), channel_id=1, source_target_pairs={{0,9},{1,8},{4,13},{5,12},{8,1},{9,0},{12,5},{13,4},{2,11},{3,10},... | collective-permute-start | bytes 589832 | tf_op jit(solution)/shard_map/ppermute | solution.py:443
  101.0 0.8 collective-permute-start.24
  102.4 1.3 collective-permute-done.21.refs_1_
  104.4 2.6 %collective-permute-done.18.refs_10_ = bf16[384,256]{1,0:T(8,128)(2,1)S(1)} collective-permute-done((bf16[384,256]{1,0:T(8,128)(2,1)S(1)}, bf16[384,256]{1,0:T(8,128)(2,1)S(1)}, u32[]{:S(2)}, u32[]{:S(2)}) %collective-permute-start.18) | collective-permute-done | bytes 196640 | tf_op jit(solution)/shard_map/ppermute | solution.py:443
  107.0 3.1 %collective-permute-done.14.refs_8_ = bf16[384,256]{1,0:T(8,128)(2,1)S(1)} collective-permute-done((bf16[384,256]{1,0:T(8,128)(2,1)S(1)}, bf16[384,256]{1,0:T(8,128)(2,1)S(1)}, u32[]{:S(2)}, u32[]{:S(2)}) %collective-permute-start.14) | collective-permute-done | bytes 196640 | tf_op jit(solution)/shard_map/ppermute | solution.py:443
  110.1 0.8 collective-permute-start.27
  110.9 0.8 collective-permute-start.19
  112.2 1.2 collective-permute-start.15
  113.3 3.0 %collective-permute-done.23.refs_3_ = bf16[384,256]{1,0:T(8,128)(2,1)S(1)} collective-permute-done((bf16[384,256]{1,0:T(8,128)(2,1)S(1)}, bf16[384,256]{1,0:T(8,128)(2,1)S(1)}, u32[]{:S(2)}, u32[]{:S(2)}) %collective-permute-start.23) | collective-permute-done | bytes 196640 | tf_op jit(solution)/shard_map/ppermute | solution.py:355
  116.4 0.8 collective-permute-start.26
  117.1 3.4 %collective-permute-done.27.refs_11_ = bf16[384,256]{1,0:T(8,128)(2,1)S(1)} collective-permute-done((bf16[384,256]{1,0:T(8,128)(2,1)S(1)}, bf16[384,256]{1,0:T(8,128)(2,1)S(1)}, u32[]{:S(2)}, u32[]{:S(2)}) %collective-permute-start.27) | collective-permute-done | bytes 196640 | tf_op jit(solution)/shard_map/ppermute | solution.py:355
  120.6 1.5 collective-permute-start.32
  122.1 4.5 %collective-permute-done.19.refs_2_ = bf16[384,256]{1,0:T(8,128)(2,1)S(1)} collective-permute-done((bf16[384,256]{1,0:T(8,128)(2,1)S(1)}, bf16[384,256]{1,0:T(8,128)(2,1)S(1)}, u32[]{:S(2)}, u32[]{:S(2)}) %collective-permute-start.19) | collective-permute-done | bytes 196640 | tf_op jit(solution)/shard_map/ppermute | solution.py:443
  127.2 3.5 %collective-permute-done.15.refs_0_ = bf16[384,256]{1,0:T(8,128)(2,1)S(1)} collective-permute-done((bf16[384,256]{1,0:T(8,128)(2,1)S(1)}, bf16[384,256]{1,0:T(8,128)(2,1)S(1)}, u32[]{:S(2)}, u32[]{:S(2)}) %collective-permute-start.15) | collective-permute-done | bytes 196640 | tf_op jit(solution)/shard_map/ppermute | solution.py:443
  131.4 0.9 collective-permute-start.33
  132.2 6.3 %unpack.1.refs_4_ = bf16[1536,512]{1,0:T(8,128)(2,1)S(1)} custom-call(bf16[384,256]{1,0:T(8,128)(2,1)S(1)} %get-tuple-element.56.refs_0_, bf16[384,256]{1,0:T(8,128)(2,1)S(1)} %collective-permute-done.21.refs_1_, bf16[384,256]{1,0:T(8,128)(2,1)S(1)} %collective-permute-done.22.refs_2_, bf16[384,256]{1,0:T(8,128)(2,1)S(1)} %collective-permute-done.23.refs_3_, ...), custom_call_target="tpu_custom_call" | custom-call | tf_op jit(solution)/shard_map/unpack/pallas_call | solution.py:448
  138.6 12.2 %final.1 = bf16[1536,256]{1,0:T(8,128)(2,1)} custom-call(bf16[384,256]{1,0:T(8,128)(2,1)S(1)} %collective-permute-done.15.refs_0_, bf16[384,256]{1,0:T(8,128)(2,1)S(1)} %collective-permute-done.16.refs_1_, bf16[384,256]{1,0:T(8,128)(2,1)S(1)} %collective-permute-done.19.refs_2_, bf16[384,256]{1,0:T(8,128)(2,1)S(1)} %collective-permute-done.20.refs_3_, ...), custom_call_target="tpu_custom_call" | custom-call | tf_op jit(solution)/shard_map/final/pallas_call | solution.py:460
  (75 shorter events, 4.8 us)
Async XLA Ops:
  2.8 48.3 %copy-start.6 = (bf16[512,1024]{1,0:T(8,128)(2,1)S(1)}, bf16[512,1024]{1,0:T(8,128)(2,1)}, u32[]{:S(2)}) copy-start(bf16[512,1024]{1,0:T(8,128)(2,1)} %refs_9_.1) | copy-start | bytes 3145732
  8.9 7.7 %collective-permute-start.2 = (bf16[400,256]{1,0:T(8,128)(2,1)S(1)}, bf16[400,256]{1,0:T(8,128)(2,1)S(1)}, u32[]{:S(2)}, u32[]{:S(2)}) collective-permute-start(bf16[400,256]{1,0:T(8,128)(2,1)S(1)} %get-tuple-element.35), channel_id=1, source_target_pairs={{0,4},{1,5},{4,0},{5,1},{8,12},{9,13},{12,8},{13,9},{2,6},{3,7},{6... | collective-permute-start | bytes 614408 | tf_op jit(solution)/shard_map/ppermute | solution.py:379
  8.9 11.7 %collective-permute-start.1 = (bf16[400,256]{1,0:T(8,128)(2,1)S(1)}, bf16[400,256]{1,0:T(8,128)(2,1)S(1)}, u32[]{:S(2)}, u32[]{:S(2)}) collective-permute-start(bf16[400,256]{1,0:T(8,128)(2,1)S(1)} %get-tuple-element.34), channel_id=1, source_target_pairs={{0,8},{1,9},{4,12},{5,13},{8,0},{9,1},{12,4},{13,5},{2,10},{3,11},... | collective-permute-start | bytes 614408 | tf_op jit(solution)/shard_map/ppermute | solution.py:379
  16.6 11.5 %collective-permute-start.4 = (bf16[400,256]{1,0:T(8,128)(2,1)S(1)}, bf16[400,256]{1,0:T(8,128)(2,1)S(1)}, u32[]{:S(2)}, u32[]{:S(2)}) collective-permute-start(bf16[400,256]{1,0:T(8,128)(2,1)S(1)} %get-tuple-element.39), channel_id=1, source_target_pairs={{0,5},{1,4},{4,1},{5,0},{8,13},{9,12},{12,9},{13,8},{2,7},{3,6},{6... | collective-permute-start | bytes 614408 | tf_op jit(solution)/shard_map/ppermute | solution.py:379
  20.6 18.8 %collective-permute-start.3 = (bf16[400,256]{1,0:T(8,128)(2,1)S(1)}, bf16[400,256]{1,0:T(8,128)(2,1)S(1)}, u32[]{:S(2)}, u32[]{:S(2)}) collective-permute-start(bf16[400,256]{1,0:T(8,128)(2,1)S(1)} %get-tuple-element.37), channel_id=1, source_target_pairs={{0,9},{1,8},{4,13},{5,12},{8,1},{9,0},{12,5},{13,4},{2,11},{3,10},... | collective-permute-start | bytes 614408 | tf_op jit(solution)/shard_map/ppermute | solution.py:379
  24.1 27.8 %collective-permute-start = (bf16[400,512]{1,0:T(8,128)(2,1)}, bf16[400,512]{1,0:T(8,128)(2,1)S(1)}, u32[]{:S(2)}, u32[]{:S(2)}) collective-permute-start(bf16[400,512]{1,0:T(8,128)(2,1)} %get-tuple-element.33), channel_id=1, source_target_pairs={{0,1},{1,0},{4,5},{5,4},{8,9},{9,8},{12,13},{13,12},{2,3},{3,2},{6... | collective-permute-start | bytes 1228808 | tf_op jit(solution)/shard_map/ppermute | solution.py:374
  24.1 15.3 %collective-permute-start.10 = (bf16[400,256]{1,0:T(8,128)(2,1)S(1)}, bf16[400,256]{1,0:T(8,128)(2,1)S(1)}, u32[]{:S(2)}, u32[]{:S(2)}) collective-permute-start(bf16[400,256]{1,0:T(8,128)(2,1)S(1)} %collective-permute-done.2.refs_3_.refs_10_), channel_id=1, source_target_pairs={{0,2},{2,0},{1,3},{3,1},{4,6},{6,4},{5,7},{7,5},{8,10},{10,8},{9,1... | collective-permute-start | bytes 614408 | tf_op jit(solution)/shard_map/ppermute | solution.py:355
  25.3 15.4 %collective-permute-start.9 = (bf16[400,256]{1,0:T(8,128)(2,1)S(1)}, bf16[400,256]{1,0:T(8,128)(2,1)S(1)}, u32[]{:S(2)}, u32[]{:S(2)}) collective-permute-start(bf16[400,256]{1,0:T(8,128)(2,1)S(1)} %collective-permute-done.1.refs_2_.refs_8_), channel_id=1, source_target_pairs={{0,2},{2,0},{1,3},{3,1},{4,6},{6,4},{5,7},{7,5},{8,10},{10,8},{9,1... | collective-permute-start | bytes 614408 | tf_op jit(solution)/shard_map/ppermute | solution.py:355
  28.1 15.8 %collective-permute-start.6 = (bf16[400,256]{1,0:T(8,128)(2,1)}, bf16[400,256]{1,0:T(8,128)(2,1)S(1)}, u32[]{:S(2)}, u32[]{:S(2)}) collective-permute-start(bf16[400,256]{1,0:T(8,128)(2,1)} %get-tuple-element.43), channel_id=1, source_target_pairs={{0,13},{1,12},{4,9},{5,8},{8,5},{9,4},{12,1},{13,0},{2,15},{3,14},... | collective-permute-start | bytes 614408 | tf_op jit(solution)/shard_map/ppermute | solution.py:379
  39.4 19.1 %copy-start.8 = (bf16[400,256]{1,0:T(8,128)(2,1)}, bf16[400,256]{1,0:T(8,128)(2,1)S(1)}, u32[]{:S(2)}) copy-start(bf16[400,256]{1,0:T(8,128)(2,1)S(1)} %collective-permute-done.3.refs_4_.refs_12_) | copy-start | bytes 614404
  39.4 10.5 %collective-permute-start.5 = (bf16[400,256]{1,0:T(8,128)(2,1)}, bf16[400,256]{1,0:T(8,128)(2,1)S(1)}, u32[]{:S(2)}, u32[]{:S(2)}) collective-permute-start(bf16[400,256]{1,0:T(8,128)(2,1)} %get-tuple-element.41), channel_id=1, source_target_pairs={{0,12},{1,13},{4,8},{5,9},{8,4},{9,5},{12,0},{13,1},{2,14},{3,15},... | collective-permute-start | bytes 614408 | tf_op jit(solution)/shard_map/ppermute | solution.py:379
  39.4 12.8 %collective-permute-start.12 = (bf16[400,256]{1,0:T(8,128)(2,1)S(1)}, bf16[400,256]{1,0:T(8,128)(2,1)S(1)}, u32[]{:S(2)}, u32[]{:S(2)}) collective-permute-start(bf16[400,256]{1,0:T(8,128)(2,1)S(1)} %collective-permute-done.4.refs_5_.refs_14_), channel_id=1, source_target_pairs={{0,2},{2,0},{1,3},{3,1},{4,6},{6,4},{5,7},{7,5},{8,10},{10,8},{9,1... | collective-permute-start | bytes 614408 | tf_op jit(solution)/shard_map/ppermute | solution.py:355
  40.7 11.4 %collective-permute-start.11 = (bf16[400,256]{1,0:T(8,128)(2,1)S(1)}, bf16[400,256]{1,0:T(8,128)(2,1)S(1)}, u32[]{:S(2)}, u32[]{:S(2)}) collective-permute-start(bf16[400,256]{1,0:T(8,128)(2,1)S(1)} %collective-permute-done.3.refs_4_.refs_12_), channel_id=1, source_target_pairs={{0,2},{2,0},{1,3},{3,1},{4,6},{6,4},{5,7},{7,5},{8,10},{10,8},{9,1... | collective-permute-start | bytes 614408 | tf_op jit(solution)/shard_map/ppermute | solution.py:355
  43.9 14.6 %copy-start.11 = (bf16[400,256]{1,0:T(8,128)(2,1)}, bf16[400,256]{1,0:T(8,128)(2,1)S(1)}, u32[]{:S(2)}) copy-start(bf16[400,256]{1,0:T(8,128)(2,1)S(1)} %collective-permute-done.6.refs_7_.refs_10_) | copy-start | bytes 614404
  43.9 14.6 %collective-permute-start.8 = (bf16[400,256]{1,0:T(8,128)(2,1)S(1)}, bf16[400,256]{1,0:T(8,128)(2,1)S(1)}, u32[]{:S(2)}, u32[]{:S(2)}) collective-permute-start(bf16[400,256]{1,0:T(8,128)(2,1)S(1)} %collective-permute-done.6.refs_7_.refs_10_), channel_id=1, source_target_pairs={{0,2},{2,0},{1,3},{3,1},{4,6},{6,4},{5,7},{7,5},{8,10},{10,8},{9,1... | collective-permute-start | bytes 614408 | tf_op jit(solution)/shard_map/ppermute | solution.py:355
  49.9 8.6 %copy-start.13 = (bf16[400,256]{1,0:T(8,128)(2,1)}, bf16[400,256]{1,0:T(8,128)(2,1)S(1)}, u32[]{:S(2)}) copy-start(bf16[400,256]{1,0:T(8,128)(2,1)S(1)} %collective-permute-done.5.refs_6_.refs_8_) | copy-start | bytes 614404
  49.9 8.6 %collective-permute-start.7 = (bf16[400,256]{1,0:T(8,128)(2,1)S(1)}, bf16[400,256]{1,0:T(8,128)(2,1)S(1)}, u32[]{:S(2)}, u32[]{:S(2)}) collective-permute-start(bf16[400,256]{1,0:T(8,128)(2,1)S(1)} %collective-permute-done.5.refs_6_.refs_8_), channel_id=1, source_target_pairs={{0,2},{2,0},{1,3},{3,1},{4,6},{6,4},{5,7},{7,5},{8,10},{10,8},{9,1... | collective-permute-start | bytes 614408 | tf_op jit(solution)/shard_map/ppermute | solution.py:355
  51.9 49.0 %collective-permute-start.28 = (bf16[512,512]{1,0:T(8,128)(2,1)}, bf16[512,512]{1,0:T(8,128)(2,1)}, u32[]{:S(2)}, u32[]{:S(2)}) collective-permute-start(bf16[512,512]{1,0:T(8,128)(2,1)} %constant_dynamic-slice_fusion.1), channel_id=1, source_target_pairs={{0,2},{2,0},{1,3},{3,1},{4,6},{6,4},{5,7},{7,5},{8,10},{10,8},{9,1... | collective-permute-start | bytes 1572872 | tf_op jit(solution)/shard_map/ppermute | solution.py:355
  52.2 6.3 %copy-start.16 = (bf16[2,512,256]{2,1,0:T(8,128)(2,1)S(1)}, bf16[2,512,256]{2,1,0:T(8,128)(2,1)}, u32[]{:S(2)}) copy-start(bf16[2,512,256]{2,1,0:T(8,128)(2,1)} %refs_13_.1) | copy-start | bytes 1572868
  52.2 6.3 %copy-start.17 = (bf16[512,256]{1,0:T(8,128)(2,1)S(1)}, bf16[512,256]{1,0:T(8,128)(2,1)}, u32[]{:S(2)}) copy-start(bf16[512,256]{1,0:T(8,128)(2,1)} %refs_14_.1) | copy-start | bytes 786436
  52.2 6.3 %copy-start.20 = (s32[128]{0:T(128)S(1)}, s32[128]{0:T(128)}, u32[]{:S(2)}) copy-start(s32[128]{0:T(128)} %refs_15_.1) | copy-start | bytes 1540
  80.1 2.5 %copy-start = (s32[3072,128]{1,0:T(8,128)}, s32[3072,128]{1,0:T(8,128)S(1)}, u32[]{:S(2)}) copy-start(s32[3072,128]{1,0:T(8,128)S(1)} %get-tuple-element.45.pos_ref) | copy-start | bytes 4718596
  80.1 3.2 %copy-start.10 = (bf16[1024,512]{1,0:T(8,128)(2,1)S(1)}, bf16[1024,512]{1,0:T(8,128)(2,1)}, u32[]{:S(2)}) copy-start(bf16[1024,512]{1,0:T(8,128)(2,1)} %refs_10_.1) | copy-start | bytes 3145732
  80.1 5.1 %copy-start.15 = (bf16[256,512]{1,0:T(8,128)(2,1)S(1)}, bf16[256,512]{1,0:T(8,128)(2,1)}, u32[]{:S(2)}) copy-start(bf16[256,512]{1,0:T(8,128)(2,1)} %refs_8_.1) | copy-start | bytes 786436
  83.3 8.7 %collective-permute-start.17 = (bf16[384,256]{1,0:T(8,128)(2,1)}, bf16[384,256]{1,0:T(8,128)(2,1)}, u32[]{:S(2)}, u32[]{:S(2)}) collective-permute-start(bf16[384,256]{1,0:T(8,128)(2,1)} %get-tuple-element.53), channel_id=1, source_target_pairs={{0,4},{1,5},{4,0},{5,1},{8,12},{9,13},{12,8},{13,9},{2,6},{3,7},{6... | collective-permute-start | bytes 589832 | tf_op jit(solution)/shard_map/ppermute | solution.py:443
  84.0 15.0 %collective-permute-start.29 = (bf16[512,256]{1,0:T(8,128)(2,1)}, bf16[512,256]{1,0:T(8,128)(2,1)}, u32[]{:S(2)}, u32[]{:S(2)}) collective-permute-start(bf16[512,256]{1,0:T(8,128)(2,1)} %dynamic_slice.10), channel_id=1, source_target_pairs={{0,2},{2,0},{1,3},{3,1},{4,6},{6,4},{5,7},{7,5},{8,10},{10,8},{9,1... | collective-permute-start | bytes 786440 | tf_op jit(solution)/shard_map/ppermute | solution.py:355
  85.2 12.8 %collective-permute-start.13 = (bf16[384,256]{1,0:T(8,128)(2,1)}, bf16[384,256]{1,0:T(8,128)(2,1)S(1)}, u32[]{:S(2)}, u32[]{:S(2)}) collective-permute-start(bf16[384,256]{1,0:T(8,128)(2,1)} %copy-done.21), channel_id=1, source_target_pairs={{0,8},{1,9},{4,12},{5,13},{8,0},{9,1},{12,4},{13,5},{2,10},{3,11},... | collective-permute-start | bytes 589832 | tf_op jit(solution)/shard_map/ppermute | solution.py:443
  85.2 12.1 %collective-permute-start.30 = (bf16[128,512]{1,0:T(8,128)(2,1)S(1)}, bf16[128,512]{1,0:T(8,128)(2,1)S(1)}, u32[]{:S(2)}, u32[]{:S(2)}) collective-permute-start(bf16[128,512]{1,0:T(8,128)(2,1)S(1)} %constant_dynamic-slice_fusion), channel_id=1, source_target_pairs={{0,2},{2,0},{1,3},{3,1},{4,6},{6,4},{5,7},{7,5},{8,10},{10,8},{9,1... | collective-permute-start | bytes 393224 | tf_op jit(solution)/shard_map/ppermute | solution.py:355
  86.9 45.3 %copy-start.5 = (s32[1536,128]{1,0:T(8,128)S(1)}, s32[1536,128]{1,0:T(8,128)}, u32[]{:S(2)}) copy-start(s32[1536,128]{1,0:T(8,128)} %copy-done.4) | copy-start | bytes 2359300
  92.0 9.8 %collective-permute-start.22 = (bf16[384,256]{1,0:T(8,128)(2,1)S(1)}, bf16[384,256]{1,0:T(8,128)(2,1)S(1)}, u32[]{:S(2)}, u32[]{:S(2)}) collective-permute-start(bf16[384,256]{1,0:T(8,128)(2,1)S(1)} %get-tuple-element.57), channel_id=1, source_target_pairs={{0,1},{1,0},{4,5},{5,4},{8,9},{9,8},{12,13},{13,12},{2,3},{3,2},{6... | collective-permute-start | bytes 589832 | tf_op jit(solution)/shard_map/ppermute | solution.py:443
  97.4 6.4 %collective-permute-start.21 = (bf16[384,256]{1,0:T(8,128)(2,1)S(1)}, bf16[384,256]{1,0:T(8,128)(2,1)S(1)}, u32[]{:S(2)}, u32[]{:S(2)}) collective-permute-start(bf16[384,256]{1,0:T(8,128)(2,1)S(1)} %get-tuple-element.56.refs_0_), channel_id=1, source_target_pairs={{0,2},{2,0},{1,3},{3,1},{4,6},{6,4},{5,7},{7,5},{8,10},{10,8},{9,1... | collective-permute-start | bytes 589832 | tf_op jit(solution)/shard_map/ppermute | solution.py:355
  98.0 9.0 %collective-permute-start.18 = (bf16[384,256]{1,0:T(8,128)(2,1)S(1)}, bf16[384,256]{1,0:T(8,128)(2,1)S(1)}, u32[]{:S(2)}, u32[]{:S(2)}) collective-permute-start(bf16[384,256]{1,0:T(8,128)(2,1)S(1)} %get-tuple-element.54), channel_id=1, source_target_pairs={{0,5},{1,4},{4,1},{5,0},{8,13},{9,12},{12,9},{13,8},{2,7},{3,6},{6... | collective-permute-start | bytes 589832 | tf_op jit(solution)/shard_map/ppermute | solution.py:443
  99.0 11.1 %collective-permute-start.14 = (bf16[384,256]{1,0:T(8,128)(2,1)S(1)}, bf16[384,256]{1,0:T(8,128)(2,1)S(1)}, u32[]{:S(2)}, u32[]{:S(2)}) collective-permute-start(bf16[384,256]{1,0:T(8,128)(2,1)S(1)} %get-tuple-element.49), channel_id=1, source_target_pairs={{0,9},{1,8},{4,13},{5,12},{8,1},{9,0},{12,5},{13,4},{2,11},{3,10},... | collective-permute-start | bytes 589832 | tf_op jit(solution)/shard_map/ppermute | solution.py:443
  101.0 10.0 %collective-permute-start.24 = (bf16[384,256]{1,0:T(8,128)(2,1)S(1)}, bf16[384,256]{1,0:T(8,128)(2,1)S(1)}, u32[]{:S(2)}, u32[]{:S(2)}) collective-permute-start(bf16[384,256]{1,0:T(8,128)(2,1)S(1)} %collective-permute-done.13.refs_4_), channel_id=1, source_target_pairs={{0,2},{2,0},{1,3},{3,1},{4,6},{6,4},{5,7},{7,5},{8,10},{10,8},{9,1... | collective-permute-start | bytes 589832 | tf_op jit(solution)/shard_map/ppermute | solution.py:355
  101.8 10.4 %collective-permute-start.25 = (bf16[384,256]{1,0:T(8,128)(2,1)}, bf16[384,256]{1,0:T(8,128)(2,1)S(1)}, u32[]{:S(2)}, u32[]{:S(2)}) collective-permute-start(bf16[384,256]{1,0:T(8,128)(2,1)} %collective-permute-done.17.refs_6_), channel_id=1, source_target_pairs={{0,2},{2,0},{1,3},{3,1},{4,6},{6,4},{5,7},{7,5},{8,10},{10,8},{9,1... | collective-permute-start | bytes 589832 | tf_op jit(solution)/shard_map/ppermute | solution.py:355
  103.7 12.6 %collective-permute-start.23 = (bf16[384,256]{1,0:T(8,128)(2,1)S(1)}, bf16[384,256]{1,0:T(8,128)(2,1)S(1)}, u32[]{:S(2)}, u32[]{:S(2)}) collective-permute-start(bf16[384,256]{1,0:T(8,128)(2,1)S(1)} %collective-permute-done.22.refs_2_), channel_id=1, source_target_pairs={{0,2},{2,0},{1,3},{3,1},{4,6},{6,4},{5,7},{7,5},{8,10},{10,8},{9,1... | collective-permute-start | bytes 589832 | tf_op jit(solution)/shard_map/ppermute | solution.py:355
  107.0 31.5 %collective-permute-start.31 = (bf16[512,512]{1,0:T(8,128)(2,1)}, bf16[512,512]{1,0:T(8,128)(2,1)S(1)}, u32[]{:S(2)}, u32[]{:S(2)}) collective-permute-start(bf16[512,512]{1,0:T(8,128)(2,1)} %collective-permute-done.28.refs_11_), channel_id=1, source_target_pairs={{1,0},{0,1},{3,2},{2,3},{5,4},{4,5},{7,6},{6,7},{9,8},{8,9},{11,10... | collective-permute-start | bytes 1572872 | tf_op jit(solution)/shard_map/ppermute | solution.py:393
  110.1 10.5 %collective-permute-start.27 = (bf16[384,256]{1,0:T(8,128)(2,1)S(1)}, bf16[384,256]{1,0:T(8,128)(2,1)S(1)}, u32[]{:S(2)}, u32[]{:S(2)}) collective-permute-start(bf16[384,256]{1,0:T(8,128)(2,1)S(1)} %collective-permute-done.18.refs_10_), channel_id=1, source_target_pairs={{0,2},{2,0},{1,3},{3,1},{4,6},{6,4},{5,7},{7,5},{8,10},{10,8},{9,1... | collective-permute-start | bytes 589832 | tf_op jit(solution)/shard_map/ppermute | solution.py:355
  110.9 15.6 %collective-permute-start.19 = (bf16[384,256]{1,0:T(8,128)(2,1)S(1)}, bf16[384,256]{1,0:T(8,128)(2,1)S(1)}, u32[]{:S(2)}, u32[]{:S(2)}) collective-permute-start(bf16[384,256]{1,0:T(8,128)(2,1)S(1)} %get-tuple-element.55), channel_id=1, source_target_pairs={{0,13},{1,12},{4,9},{5,8},{8,5},{9,4},{12,1},{13,0},{2,15},{3,14},... | collective-permute-start | bytes 589832 | tf_op jit(solution)/shard_map/ppermute | solution.py:443
  112.2 18.6 %collective-permute-start.15 = (bf16[384,256]{1,0:T(8,128)(2,1)S(1)}, bf16[384,256]{1,0:T(8,128)(2,1)S(1)}, u32[]{:S(2)}, u32[]{:S(2)}) collective-permute-start(bf16[384,256]{1,0:T(8,128)(2,1)S(1)} %get-tuple-element.50), channel_id=1, source_target_pairs={{0,12},{1,13},{4,8},{5,9},{8,4},{9,5},{12,0},{13,1},{2,14},{3,15},... | collective-permute-start | bytes 589832 | tf_op jit(solution)/shard_map/ppermute | solution.py:443
  116.4 15.0 %collective-permute-start.26 = (bf16[384,256]{1,0:T(8,128)(2,1)S(1)}, bf16[384,256]{1,0:T(8,128)(2,1)S(1)}, u32[]{:S(2)}, u32[]{:S(2)}) collective-permute-start(bf16[384,256]{1,0:T(8,128)(2,1)S(1)} %collective-permute-done.14.refs_8_), channel_id=1, source_target_pairs={{0,2},{2,0},{1,3},{3,1},{4,6},{6,4},{5,7},{7,5},{8,10},{10,8},{9,1... | collective-permute-start | bytes 589832 | tf_op jit(solution)/shard_map/ppermute | solution.py:355
  120.6 18.0 %collective-permute-start.32 = (bf16[512,256]{1,0:T(8,128)(2,1)}, bf16[512,256]{1,0:T(8,128)(2,1)S(1)}, u32[]{:S(2)}, u32[]{:S(2)}) collective-permute-start(bf16[512,256]{1,0:T(8,128)(2,1)} %collective-permute-done.29.refs_12_), channel_id=1, source_target_pairs={{1,0},{0,1},{3,2},{2,3},{5,4},{4,5},{7,6},{6,7},{9,8},{8,9},{11,10... | collective-permute-start | bytes 786440 | tf_op jit(solution)/shard_map/ppermute | solution.py:393
  126.6 12.0 %collective-permute-start.20 = (bf16[384,256]{1,0:T(8,128)(2,1)S(1)}, bf16[384,256]{1,0:T(8,128)(2,1)S(1)}, u32[]{:S(2)}, u32[]{:S(2)}) collective-permute-start(bf16[384,256]{1,0:T(8,128)(2,1)S(1)} %collective-permute-done.19.refs_2_), channel_id=1, source_target_pairs={{0,2},{2,0},{1,3},{3,1},{4,6},{6,4},{5,7},{7,5},{8,10},{10,8},{9,1... | collective-permute-start | bytes 589832 | tf_op jit(solution)/shard_map/ppermute | solution.py:355
  130.7 7.9 %collective-permute-start.16 = (bf16[384,256]{1,0:T(8,128)(2,1)S(1)}, bf16[384,256]{1,0:T(8,128)(2,1)S(1)}, u32[]{:S(2)}, u32[]{:S(2)}) collective-permute-start(bf16[384,256]{1,0:T(8,128)(2,1)S(1)} %collective-permute-done.15.refs_0_), channel_id=1, source_target_pairs={{0,2},{2,0},{1,3},{3,1},{4,6},{6,4},{5,7},{7,5},{8,10},{10,8},{9,1... | collective-permute-start | bytes 589832 | tf_op jit(solution)/shard_map/ppermute | solution.py:355
  131.4 7.2 %collective-permute-start.33 = (bf16[128,512]{1,0:T(8,128)(2,1)S(1)}, bf16[128,512]{1,0:T(8,128)(2,1)S(1)}, u32[]{:S(2)}, u32[]{:S(2)}) collective-permute-start(bf16[128,512]{1,0:T(8,128)(2,1)S(1)} %collective-permute-done.30.refs_13_), channel_id=1, source_target_pairs={{1,0},{0,1},{3,2},{2,3},{5,4},{4,5},{7,6},{6,7},{9,8},{8,9},{11,10... | collective-permute-start | bytes 393224 | tf_op jit(solution)/shard_map/ppermute | solution.py:393
  132.2 6.4 %copy-start.3 = (bf16[1536,512]{1,0:T(8,128)(2,1)S(1)}, bf16[1536,512]{1,0:T(8,128)(2,1)}, u32[]{:S(2)}) copy-start(bf16[1536,512]{1,0:T(8,128)(2,1)} %refs_6_.1) | copy-start | bytes 4718596
  132.2 6.4 %copy-start.7 = (bf16[512,1024]{1,0:T(8,128)(2,1)S(1)}, bf16[512,1024]{1,0:T(8,128)(2,1)}, u32[]{:S(2)}) copy-start(bf16[512,1024]{1,0:T(8,128)(2,1)} %refs_9_.1) | copy-start | bytes 3145732
  132.2 6.4 %copy-start.19 = (f32[512]{0:T(512)S(1)}, f32[512]{0:T(512)}, u32[]{:S(2)}) copy-start(f32[512]{0:T(512)} %param.18) | copy-start | bytes 6148
  (8 other events, 7.8 us)
where the time goes:
time: 151 us
  Pallas kernels  56.1 us (37%)
  waiting for transfers between devices  48.6 us (32%)
  starting transfers between devices  35.6 us (24%)
  local copies, waits for them, and re-layouts  10.2 us (7%)
    ppermute x6, waiting for transfers between devices, shards(): got = lax.ppermute(sent, OWN, steps.perm(k))  26.7 us
    pallas_call x1, Pallas kernels, shards(): pl.pallas_call(functools.partial(attend_kernel, names=[order.index(k) for...  18.8 us
    ppermute x7, waiting for transfers between devices, shards(): home = lax.ppermute(home, OWN, steps.perm(k, True))  13.7 us
    ppermute x17, starting transfers between devices, over_mp(): return lax.ppermute(x, 'mp', mp_steps.perm(t))  12.9 us
    pallas_call x1, Pallas kernels, shards(): pl.pallas_call(functools.partial(final_kernel, names=late, cap=cap, mp_st...  12.2 us
    ppermute x7, starting transfers between devices, shards(): home = lax.ppermute(home, OWN, steps.perm(k, True))  10.3 us
    ppermute x6, starting transfers between devices, shards(): got = lax.ppermute(sent, OWN, steps.perm(k))  9.98 us
    ppermute x17, waiting for transfers between devices, over_mp(): return lax.ppermute(x, 'mp', mp_steps.perm(t))  8.21 us
  transfers between devices with their start and end apart: 34, of which 13 were waited for; matrix products, arithmetic and copies ran while one was open for 1% of the time, Pallas kernels for 26%

commit v1 on v0

--- a/solution.py
+++ b/solution.py
@@ -19,6 +19,8 @@
 F32 = jnp.float32
 BF16 = jnp.bfloat16
 VM = pl.BlockSpec(memory_space=pltpu.VMEM)
+HB = pl.BlockSpec(memory_space=pltpu.MemorySpace.HBM)
+SM = pl.BlockSpec(memory_space=pltpu.SMEM)
 PARAMS = pltpu.CompilerParams(vmem_limit_bytes=20 * 1024 * 1024)
 
 
@@ -56,13 +58,17 @@
     return lax.axis_index("space") * sub_size + lax.axis_index("sub")
 
 
-def pack_kernel(ids_ref, vox_ref, gain_ref, *refs, steps, sub_size, near, cap, wins):
+def pack_kernel(ids_ref, vox_hbm, gain_hbm, *refs, steps, sub_size, near, cap, wins):
     n = steps.n
-    col_ref, outs, normed_ref, cnt_ref = refs[0], refs[1 : 1 + n], refs[1 + n], refs[2 + n]
+    col_ref, outs = refs[0], refs[1 : 1 + n]
+    normed_ref, cnt_ref, vox_ref, gain_ref, sem, sem_gain = refs[1 + n :]
     rows, _ = vox_ref.shape
     me = own_index(sub_size)
     mp = lax.axis_index("mp")
-    normed_ref[...] = layer_norm(vox_ref[...].astype(F32), gain_ref[...]).astype(BF16)
+    load = pltpu.make_async_copy(vox_hbm, vox_ref, sem)
+    load.start()
+    load_gain = pltpu.make_async_copy(gain_hbm, gain_ref, sem_gain)
+    load_gain.start()
     ids = ids_ref[...]
     step = 256
     win_iota = lax.broadcasted_iota(jnp.int32, (wins, step), 0)
@@ -90,6 +96,9 @@
     dest = steps.step(me, ids // WIN_DEV) * cap + rank
     col_ref[...] = jnp.transpose(jnp.broadcast_to(dest.astype(F32), (LANES, rows))).astype(jnp.int32)
     row_iota = lax.broadcasted_iota(jnp.int32, (cap, rows), 0)
+    load_gain.wait()
+    load.wait()
+    normed_ref[...] = layer_norm(vox_ref[...].astype(F32), gain_ref[...]).astype(BF16)
     for k in range(n):
         out = outs[k]
         piece = out.shape[1]
@@ -150,19 +159,24 @@
         dest[:, cols] = dest[:, cols] + term.astype(BF16)
 
 
-def place_kernel(*refs, names, parts, cap, mp_steps, tails_count, piece):
-    table = refs[-1]
-    part_refs, _ = split_refs(refs, tails_count, parts)
+def place_kernel(*refs, names, parts, cap, mp_steps, tails_count, piece, has_prev, with_pos):
+    table, pos_ref = refs[-2:] if with_pos else (refs[-1], None)
+    part_refs, at = split_refs(refs, tails_count, parts)
     mp = lax.axis_index("mp")
     tails = [r[cap : cap + META, 0:LANES] for r in refs[:tails_count]]
     where_all = places(tails, cap)
     bits = [window_bits(tails[i]) for i in names]
     slot = lax.broadcasted_iota(jnp.int32, (WLEN, cap), 0)
+    for i, p in enumerate(where_all if with_pos else []):
+        pos_ref[i * cap : (i + 1) * cap, :] = jnp.transpose(
+            jnp.broadcast_to(p.astype(F32), (LANES, cap))
+        ).astype(jnp.int32)
 
     @pl.loop(0, table.shape[0] // WLEN)
     def _(w):
-        rows = table.at[pl.ds(pl.multiple_of(w * WLEN, WLEN), WLEN), :]
-        rows[...] = jnp.zeros(rows.shape, BF16)
+        at_rows = pl.ds(pl.multiple_of(w * WLEN, WLEN), WLEN)
+        rows = table.at[at_rows, :]
+        rows[...] = refs[at][at_rows, :] if has_prev else jnp.zeros(rows.shape, BF16)
         for i, name in enumerate(names):
 
             @pl.when((bits[i] >> w) & 1 == 1)
@@ -171,8 +185,8 @@
                 add_rows(rows, hot, part_refs[i], mp, mp_steps, piece, cap)
 
 
-def attend_kernel(*refs, names, parts, cap, mp_steps, tails_count, piece, local, sub_size):
-    att, pos_ref, weight_ref, member_ref = refs[-4:]
+def project_kernel(*refs, names, parts, cap, mp_steps, tails_count, piece, local, sub_size, group):
+    qkv_ref, weight_ref, member_ref = refs[-3:]
     part_refs, at = split_refs(refs, tails_count, parts)
     table_ref, wqk_ref, wv_ref, counts_ref = refs[at : at + 4]
     mp = lax.axis_index("mp")
@@ -180,61 +194,88 @@
     tails = [r[cap : cap + META, 0:LANES] for r in refs[:tails_count]]
     where_all = places(tails, cap)
     bits = [window_bits(tails[i]) for i in names]
-    for i, p in enumerate(where_all):
-        pos_ref[i * cap : (i + 1) * cap, :] = jnp.transpose(
-            jnp.broadcast_to(p.astype(F32), (LANES, cap))
-        ).astype(jnp.int32)
     for t in range(mp_steps.n):
         block = pl.ds(pl.multiple_of(mp_steps.frm(mp, t) * piece, piece), piece)
         to = slice(t * piece, (t + 1) * piece)
         weight_ref[to, 0:local] = wqk_ref[0, block, :]
         weight_ref[to, local : 2 * local] = wqk_ref[1, block, :]
         weight_ref[to, 2 * local : 3 * local] = wv_ref[block, :]
-    windows = att.shape[0] // WLEN
     slot = lax.broadcasted_iota(jnp.int32, (WLEN, cap), 0)
-    low = lax.broadcasted_iota(jnp.int32, (WLEN, LANES), 1) < HDIM
-    key = lax.broadcasted_iota(jnp.int32, (WLEN, WLEN), 1)
-    factor = HDIM ** (-0.5) * 1.4426950408889634
-
-    @pl.loop(0, windows)
-    def _(w):
-        rows = pl.ds(pl.multiple_of(w * WLEN, WLEN), WLEN)
-        live = counts_ref[me * windows + w]
-
-        @pl.when(live == 0)
-        def _():
-            att[rows, :] = jnp.zeros((WLEN, local), BF16)
+    windows = table_ref.shape[0] // WLEN
+
+    @pl.loop(0, windows // group)
+    def _(g):
+        rows = pl.ds(pl.multiple_of(g * group * WLEN, WLEN), group * WLEN)
+        live = counts_ref[me * windows + g * group]
+        for j in range(1, group):
+            live = live + counts_ref[me * windows + g * group + j]
 
         @pl.when(live > 0)
         def _():
             member_ref[...] = table_ref[rows, :]
-            for i, name in enumerate(names):
-
-                @pl.when((bits[i] >> w) & 1 == 1)
-                def _():
-                    hot = (slot + w * WLEN == where_all[name]).astype(F32).astype(BF16)
-                    add_rows(member_ref, hot, part_refs[i], mp, mp_steps, piece, cap)
-
-            qkv = dot(member_ref[...], weight_ref[...]).astype(BF16)
-            zero = jnp.zeros((WLEN, LANES), BF16)
-            for pair in range(local // LANES):
-                q = qkv[:, pair * LANES : (pair + 1) * LANES]
-                k = qkv[:, local + pair * LANES : local + (pair + 1) * LANES]
-                v = qkv[:, 2 * local + pair * LANES : 2 * local + (pair + 1) * LANES]
-                total, mixed = [], None
-                for half in (low, ~low):
-                    scores = lax.dot_general(
-                        q, jnp.where(half, k, zero), (((1,), (1,)), ((), ())),
-                        preferred_element_type=F32,
-                    )
-                    scores = jnp.where(key < live, scores, -1e30)
-                    top = jnp.max(scores, axis=1, keepdims=True)
-                    grown = jnp.exp2((scores - top) * factor)
-                    total.append(jnp.sum(grown, axis=1, keepdims=True))
-                    term = dot(grown.astype(BF16), jnp.where(half, v, zero))
-                    mixed = term if mixed is None else mixed + term
-                mixed = mixed / jnp.where(low, total[0], total[1])
-                att[rows, pair * LANES : (pair + 1) * LANES] = mixed.astype(BF16)
+            for j in range(group):
+                w = g * group + j
+                part_rows = member_ref.at[j * WLEN : (j + 1) * WLEN, :]
+                for i, name in enumerate(names):
+
+                    @pl.when((bits[i] >> w) & 1 == 1)
+                    def _():
+                        hot = (slot + w * WLEN == where_all[name]).astype(F32).astype(BF16)
+                        add_rows(part_rows, hot, part_refs[i], mp, mp_steps, piece, cap)
+
+            qkv_ref[rows, :] = dot(member_ref[...], weight_ref[...]).astype(BF16)
+
+
+def attend_kernel(qkv_ref, counts_ref, att, *, pairs, local, sub_size, group):
+    me = own_index(sub_size)
+    windows = att.shape[0] // WLEN
+    low = lax.broadcasted_iota(jnp.int32, (WLEN, LANES), 1) < HDIM
+    key = lax.broadcasted_iota(jnp.int32, (1, WLEN), 1)
+    factor = HDIM ** (-0.5) * 1.4426950408889634
+    zero = jnp.zeros((WLEN, LANES), BF16)
+    one = jnp.ones((WLEN, LANES), BF16)
+    ones = [jnp.where(low, one, zero), jnp.where(low, zero, one)]
+
+    def mix(rows, live):
+        bias = jnp.where(key < live, 0.0, -1e30).astype(F32)
+        for at, pair in enumerate(pairs):
+            q = qkv_ref[rows, pair * LANES : (pair + 1) * LANES]
+            k = qkv_ref[rows, local + pair * LANES : local + (pair + 1) * LANES]
+            v = qkv_ref[rows, 2 * local + pair * LANES : 2 * local + (pair + 1) * LANES]
+            both = jnp.concatenate([jnp.where(low, q, zero), jnp.where(low, zero, q)], axis=0)
+            scores = lax.dot_general(both, k, (((1,), (1,)), ((), ())), preferred_element_type=F32)
+            scores = scores + bias
+            top = jnp.max(scores, axis=1, keepdims=True)
+            grown = jnp.exp2((scores - top) * factor).astype(BF16)
+            wide = jnp.concatenate([grown[:WLEN], grown[WLEN:]], axis=1)
+            mixer = jnp.concatenate(
+                [
+                    jnp.concatenate([jnp.where(low, v, zero), ones[0]], axis=1),
+                    jnp.concatenate([jnp.where(low, zero, v), ones[1]], axis=1),
+                ],
+                axis=0,
+            )
+            mixed = dot(wide, mixer)
+            att[rows, at * LANES : (at + 1) * LANES] = (
+                mixed[:, :LANES] / mixed[:, LANES:]
+            ).astype(BF16)
+
+    @pl.loop(0, windows // group)
+    def _(g):
+        lives = [counts_ref[me * windows + g * group + j] for j in range(group)]
+        spans = [
+            pl.ds(pl.multiple_of((g * group + j) * WLEN, WLEN), WLEN) for j in range(group)
+        ]
+
+        @pl.when(sum(lives) == 0)
+        def _():
+            for rows in spans:
+                att[rows, :] = jnp.zeros((WLEN, att.shape[1]), BF16)
+
+        @pl.when(sum(lives) > 0)
+        def _():
+            for rows, live in zip(spans, lives):
+                mix(rows, live)
 
 
 def fetch_kernel(att_ref, pos_ref, *outs, names, cap):
@@ -361,67 +402,96 @@
         ),
         out_shape=[jax.ShapeDtypeStruct((rows, LANES), jnp.int32)]
         + [jax.ShapeDtypeStruct((bucket, width if k < near else piece), BF16) for k in range(n)],
-        in_specs=[VM] * 3,
+        in_specs=[VM, HB, HB],
         out_specs=[VM] * (n + 1),
-        scratch_shapes=[pltpu.VMEM((rows, width), BF16), pltpu.VMEM((n * WIN_DEV, LANES), F32)],
+        scratch_shapes=[
+            pltpu.VMEM((rows, width), BF16), pltpu.VMEM((n * WIN_DEV, LANES), F32),
+            pltpu.VMEM((rows, width), BF16), pltpu.VMEM((1, width), F32),
+            pltpu.SemaphoreType.DMA, pltpu.SemaphoreType.DMA,
+        ],
         compiler_params=PARAMS,
         name="pack",
     )(window_ids.reshape(1, rows), voxels, norm_gain.reshape(1, width))
     dest_col, packed = packed[0], packed[1:]
+
+    part = w_up.shape[1] // sub_size
+    out_part = w_out.shape[0] // sub_size
+    pieces = []
+    for t in range(1, mp_size):
+        to = mp_steps.to(mp, t)
+        pieces.append((
+            lax.dynamic_slice_in_dim(w_up, sub * part, part, 1),
+            lax.dynamic_slice(w_down, (sub * part, to * piece), (part, piece)),
+            lax.dynamic_slice_in_dim(w_out, sub * out_part, out_part, 0),
+        ))
 
     arrived = {0: [packed[0]]}
     for k in range(1, near):
         arrived[k] = [lax.ppermute(packed[k], OWN, steps.perm(k))]
     for i, k in enumerate(far):
         sent = packed[k]
-        if i >= 2:
-            sent, _ = lax.optimization_barrier((sent, arrived[far[i - 2]][0]))
+        if i == 2:
+            sent, pieces = lax.optimization_barrier((sent, pieces))
         got = lax.ppermute(sent, OWN, steps.perm(k))
         arrived[k] = [got] + [over_mp(got, t) for t in range(1, mp_size)]
 
-    part = w_up.shape[1] // sub_size
-    out_part = w_out.shape[0] // sub_size
     extra = []
     for t in range(1, mp_size):
-        to = mp_steps.to(mp, t)
-        up = over_mp(lax.dynamic_slice_in_dim(w_up, sub * part, part, 1), t)
-        down = over_mp(lax.dynamic_slice(w_down, (sub * part, to * piece), (part, piece)), t)
-        proj = over_mp(lax.dynamic_slice_in_dim(w_out, sub * out_part, out_part, 0), t)
-        extra += [up, down, proj]
+        sent = [over_mp(x, t) for x in pieces[t - 1]]
+        extra += sent
         for j in range(1, sub_size):
             share = [((i + j) % sub_size, i) for i in range(sub_size)]
-            extra += [lax.ppermute(x, "sub", share) for x in (up, down, proj)]
+            extra += [lax.ppermute(x, "sub", share) for x in sent]
 
     slots = WIN_DEV * WLEN
-    flat = [x for k in early for x in arrived[k]]
-    table = pl.pallas_call(
+    tails = [arrived[k][0] for k in order]
+    cuts = [0, min(near + 2, len(early)), len(early)]
+    prev = []
+    for number in range(2):
+        group = list(range(cuts[number], cuts[number + 1]))
+        parts = [arrived[order[i]] for i in group]
+        with_pos = number == 1
+        seen = tails if with_pos else tails[: cuts[1]]
+        got = pl.pallas_call(
+            functools.partial(
+                place_kernel, names=group, parts=[len(p) for p in parts], cap=cap,
+                mp_steps=mp_steps, tails_count=len(seen), piece=piece, has_prev=bool(prev),
+                with_pos=with_pos,
+            ),
+            out_shape=[jax.ShapeDtypeStruct((slots, width), BF16)]
+            + [jax.ShapeDtypeStruct((n * cap, LANES), jnp.int32)] * with_pos,
+            in_specs=[VM] * (len(seen) + sum(len(p) for p in parts) + len(prev)),
+            out_specs=[VM] * (1 + with_pos),
+            compiler_params=PARAMS,
+            name="place",
+        )(*seen, *[x for p in parts for x in p], *prev)
+        prev = [got[0]]
+    table, pos = got
+    flat = [x for k in late for x in arrived[k]]
+    qkv = pl.pallas_call(
         functools.partial(
-            place_kernel, names=list(range(len(early))), parts=[len(arrived[k]) for k in early],
-            cap=cap, mp_steps=mp_steps, tails_count=len(early), piece=piece,
+            project_kernel, names=[order.index(k) for k in late],
+            parts=[len(arrived[k]) for k in late], cap=cap, mp_steps=mp_steps, tails_count=n,
+            piece=piece, local=local, sub_size=sub_size, group=2,
         ),
-        out_shape=jax.ShapeDtypeStruct((slots, width), BF16),
-        in_specs=[VM] * (len(early) + len(flat)),
+        out_shape=jax.ShapeDtypeStruct((slots, 3 * local), BF16),
+        in_specs=[VM] * (n + len(flat) + 3) + [SM],
+        out_specs=VM,
+        scratch_shapes=[pltpu.VMEM((width, 3 * local), BF16), pltpu.VMEM((2 * WLEN, width), BF16)],
+        compiler_params=PARAMS,
+        name="project",
+    )(*tails, *flat, table, w_query_key, w_value, window_counts)
+    att = pl.pallas_call(
+        functools.partial(
+            attend_kernel, pairs=list(range(local // LANES)), local=local, sub_size=sub_size,
+            group=2,
+        ),
+        out_shape=jax.ShapeDtypeStruct((slots, local), BF16),
+        in_specs=[VM, SM],
         out_specs=VM,
         compiler_params=PARAMS,
-        name="place",
-    )(*[arrived[k][0] for k in early], *flat)
-    flat = [x for k in late for x in arrived[k]]
-    att, pos = pl.pallas_call(
-        functools.partial(
-            attend_kernel, names=[order.index(k) for k in late],
-            parts=[len(arrived[k]) for k in late], cap=cap, mp_steps=mp_steps, tails_count=n,
-            piece=piece, local=local, sub_size=sub_size,
-        ),
-        out_shape=[
-            jax.ShapeDtypeStruct((slots, local), BF16),
-            jax.ShapeDtypeStruct((n * cap, LANES), jnp.int32),
-        ],
-        in_specs=[VM] * (n + len(flat) + 3) + [pl.BlockSpec(memory_space=pltpu.SMEM)],
-        out_specs=[VM, VM],
-        scratch_shapes=[pltpu.VMEM((width, 3 * local), BF16), pltpu.VMEM((WLEN, width), BF16)],
-        compiler_params=PARAMS,
         name="attend",
-    )(*[arrived[k][0] for k in order], *flat, table, w_query_key, w_value, window_counts)
+    )(qkv, window_counts)
 
     answers = {}
     for group in (far[:2], list(range(near)) + far[2:]):
@@ -435,10 +505,8 @@
         )(att, pos)
         answers.update(zip(group, got))
     returned = {}
-    for i, k in enumerate(order):
+    for k in order:
         home = answers[k]
-        if i >= near + 2:
-            home, _ = lax.optimization_barrier((home, returned[order[i - 2]][0]))
         if k > 0:
             home = lax.ppermute(home, OWN, steps.perm(k, True))
         returned[k] = [home] + [over_mp(home, t) for t in range(1, mp_size)]

time: 151 us -> 160 us (1.060)
  the two profiles are of different devices: /device:TPU:9 before, /device:TPU:30 now
where the time goes in v1:
time: 160 us
  waiting for transfers between devices  66.6 us (42%)
  Pallas kernels  49.5 us (31%)
  starting transfers between devices  37.3 us (23%)
  local copies, waits for them, and re-layouts  6.52 us (4%)
    ppermute x17, waiting for transfers between devices, over_mp(): return lax.ppermute(x, 'mp', mp_steps.perm(t))  40.2 us
    ppermute x6, waiting for transfers between devices, shards(): got = lax.ppermute(sent, OWN, steps.perm(k))  15.9 us
    ppermute x17, starting transfers between devices, over_mp(): return lax.ppermute(x, 'mp', mp_steps.perm(t))  13.3 us
    pallas_call x1, Pallas kernels, shards(): pl.pallas_call(functools.partial(final_kernel, names=late, cap=cap, mp_st...  11.1 us
    ppermute x7, waiting for transfers between devices, shards(): home = lax.ppermute(home, OWN, steps.perm(k, True))  10.4 us
    ppermute x3, starting transfers between devices, shards(): extra += [lax.ppermute(x, 'sub', share) for x in sent]  8.53 us
    ppermute x7, starting transfers between devices, shards(): home = lax.ppermute(home, OWN, steps.perm(k, True))  8.14 us
    pallas_call x1, Pallas kernels, shards(): pl.pallas_call(functools.partial(attend_kernel, pairs=list(range(local //...  7.33 us
  transfers between devices with their start and end apart: 34, of which 17 were waited for; matrix products, arithmetic and copies ran while one was open for 2% of the time, Pallas kernels for 21%

profile of v1, /device:TPU:30, one launch (start us, length us, event | category | flops | bytes accessed | tf_op | source)
XLA Modules:
  0.0 160.1 jit_solution(7463915836957095247)
XLA Ops:
  0.0 0.7 reshape.9.ids_ref
  0.7 1.4 copy-done
  2.1 0.7 copy-done.8
  2.8 5.5 %pack.1 = (s32[1536,128]{1,0:T(8,128)S(1)}, bf16[400,512]{1,0:T(8,128)(2,1)S(1)}, bf16[400,512]{1,0:T(8,128)(2,1)S(1)}, bf16[400,256]{1,0:T(8,128)(2,1)}, bf16[4...) custom-call(s32[1,1536]{1,0:T(1,128)S(1)} %reshape.9.ids_ref, ...), custom_call_target="tpu_custom_call" | custom-call | tf_op jit(solution)/shard_map/pack/pallas_call | solution.py:399
  8.3 0.7 copy-done.10
  10.2 1.9 %constant_dynamic-slice_fusion.1 = bf16[512,512]{1,0:T(8,128)(2,1)} fusion(bf16[512,1024]{1,0:T(8,128)(2,1)} %refs_9_.1, s32[]{:T(128)S(6)} %select_n.10), kind=kLoop, calls=%fused_computation.1 | loop fusion | bytes 1048580 | tf_op jit(solution)/shard_map/dynamic_slice | solution.py:423
  12.1 0.7 dynamic_slice.10
  12.8 1.1 collective-permute-start.3
  13.9 2.4 %collective-permute-start.4 = (bf16[400,256]{1,0:T(8,128)(2,1)}, bf16[400,256]{1,0:T(8,128)(2,1)S(1)}, u32[]{:S(2)}, u32[]{:S(2)}) collective-permute-start(bf16[400,256]{1,0:T(8,128)(2,1)} %copy-done.11), channel_id=1, source_target_pairs={{0,5},{1,4},{4,1},{5,0},{8,13},{9,12},{12,9},{13,8},{2,7},{3,6},{6... | collective-permute-start | bytes 614408 | tf_op jit(solution)/shard_map/ppermute | solution.py:435
  16.3 6.1 %collective-permute-done.1.refs_2_.refs_6_ = bf16[400,256]{1,0:T(8,128)(2,1)S(1)} collective-permute-done((bf16[400,256]{1,0:T(8,128)(2,1)}, bf16[400,256]{1,0:T(8,128)(2,1)S(1)}, u32[]{:S(2)}, u32[]{:S(2)}) %collective-permute-start.1) | collective-permute-done | bytes 204832 | tf_op jit(solution)/shard_map/ppermute | solution.py:435
  22.5 1.3 collective-permute-start.5
  23.8 1.7 %collective-permute-start.6 = (bf16[400,256]{1,0:T(8,128)(2,1)S(1)}, bf16[400,256]{1,0:T(8,128)(2,1)S(1)}, u32[]{:S(2)}, u32[]{:S(2)}) collective-permute-start(bf16[400,256]{1,0:T(8,128)(2,1)S(1)} %get-tuple-element.36), channel_id=1, source_target_pairs={{0,13},{1,12},{4,9},{5,8},{8,5},{9,4},{12,1},{13,0},{2,15},{3,14},... | collective-permute-start | bytes 614408 | tf_op jit(solution)/shard_map/ppermute | solution.py:435
  25.4 5.5 %collective-permute-done.3.refs_4_.refs_8_ = bf16[400,256]{1,0:T(8,128)(2,1)S(1)} collective-permute-done((bf16[400,256]{1,0:T(8,128)(2,1)}, bf16[400,256]{1,0:T(8,128)(2,1)S(1)}, u32[]{:S(2)}, u32[]{:S(2)}) %collective-permute-start.3) | collective-permute-done | bytes 204832 | tf_op jit(solution)/shard_map/ppermute | solution.py:435
  30.9 0.5 collective-permute-start.11
  31.4 1.5 collective-permute-start.12
  32.9 2.7 %collective-permute-done.5.refs_6_.refs_8_ = bf16[400,256]{1,0:T(8,128)(2,1)S(1)} collective-permute-done((bf16[400,256]{1,0:T(8,128)(2,1)}, bf16[400,256]{1,0:T(8,128)(2,1)S(1)}, u32[]{:S(2)}, u32[]{:S(2)}) %collective-permute-start.5) | collective-permute-done | bytes 204832 | tf_op jit(solution)/shard_map/ppermute | solution.py:435
  35.7 0.5 collective-permute-start.28
  36.2 1.6 collective-permute-done.6.refs_7_.refs_10_
  38.9 1.0 collective-permute-start.10
  39.8 3.4 %collective-permute-done.12.refs_9_ = bf16[400,256]{1,0:T(8,128)(2,1)S(1)} collective-permute-done((bf16[400,256]{1,0:T(8,128)(2,1)S(1)}, bf16[400,256]{1,0:T(8,128)(2,1)S(1)}, u32[]{:S(2)}, u32[]{:S(2)}) %collective-permute-start.12) | collective-permute-done | bytes 204832 | tf_op jit(solution)/shard_map/ppermute | solution.py:396
  43.2 0.5 collective-permute-start.7
  43.8 1.5 collective-permute-start.8
  45.3 13.6 %collective-permute-done.9.refs_9_ = bf16[400,256]{1,0:T(8,128)(2,1)S(1)} collective-permute-done((bf16[400,256]{1,0:T(8,128)(2,1)S(1)}, bf16[400,256]{1,0:T(8,128)(2,1)S(1)}, u32[]{:S(2)}, u32[]{:S(2)}) %collective-permute-start.9) | collective-permute-done | bytes 204832 | tf_op jit(solution)/shard_map/ppermute | solution.py:396
  58.9 0.5 collective-permute-start.29
  59.4 3.9 %collective-permute-done.10.refs_11_ = bf16[400,256]{1,0:T(8,128)(2,1)S(1)} collective-permute-done((bf16[400,256]{1,0:T(8,128)(2,1)S(1)}, bf16[400,256]{1,0:T(8,128)(2,1)S(1)}, u32[]{:S(2)}, u32[]{:S(2)}) %collective-permute-start.10) | collective-permute-done | bytes 204832 | tf_op jit(solution)/shard_map/ppermute | solution.py:396
  63.3 0.5 collective-permute-start.30
  63.8 4.2 %place.2.refs_12_ = bf16[4096,512]{1,0:T(8,128)(2,1)S(1)} custom-call(bf16[400,512]{1,0:T(8,128)(2,1)S(1)} %get-tuple-element.28.refs_0_.refs_4_, bf16[400,512]{1,0:T(8,128)(2,1)S(1)} %collective-permute-done.refs_1_.refs_5_, bf16[400,256]{1,0:T(8,128)(2,1)S(1)} %collective-permute-done.1.refs_2_.refs_6_, ...), custom_call_target="tpu_custom_call" | custom-call | tf_op jit(solution)/shard_map/place/pallas_call | solution.py:455
  68.0 2.7 %place.3 = (bf16[4096,512]{1,0:T(8,128)(2,1)S(1)}, s32[3072,128]{1,0:T(8,128)S(1)}) custom-call(bf16[400,512]{1,0:T(8,128)(2,1)S(1)} %get-tuple-element.28.refs_0_.refs_4_, bf16[400,512]{1,0:T(8,128)(2,1)S(1)} %collective-permute-done.refs_1_.refs_5_, bf16[400,256]{1,0:T(8,128)(2,1)S(1)} %collective-permute-done.1.refs_2_.refs_6_, ...), custom_call_target="tpu_custom_call" | custom-call | tf_op jit(solution)/shard_map/place/pallas_call | solution.py:455
  70.7 1.3 collective-permute-done.8.refs_11_
  72.0 6.8 %project.1.qkv_ref = bf16[4096,768]{1,0:T(8,128)(2,1)S(1)} custom-call(bf16[400,512]{1,0:T(8,128)(2,1)S(1)} %get-tuple-element.28.refs_0_.refs_4_, bf16[400,512]{1,0:T(8,128)(2,1)S(1)} %collective-permute-done.refs_1_.refs_5_, bf16[400,256]{1,0:T(8,128)(2,1)S(1)} %collective-permute-done.1.refs_2_.refs_6_, ...), custom_call_target="tpu_custom_call" | custom-call | tf_op jit(solution)/shard_map/project/pallas_call | solution.py:471
  78.8 7.3 %attend.1.att_ref = bf16[4096,256]{1,0:T(8,128)(2,1)S(1)} custom-call(bf16[4096,768]{1,0:T(8,128)(2,1)S(1)} %project.1.qkv_ref, s32[128]{0:T(128)S(1)} %copy-done.7), custom_call_target="tpu_custom_call" | custom-call | tf_op jit(solution)/shard_map/attend/pallas_call | solution.py:484
  86.2 1.8 %fetch.3 = (bf16[384,256]{1,0:T(8,128)(2,1)S(1)}, bf16[384,256]{1,0:T(8,128)(2,1)S(1)}) custom-call(bf16[4096,256]{1,0:T(8,128)(2,1)S(1)} %attend.1.att_ref, s32[3072,128]{1,0:T(8,128)S(1)} %get-tuple-element.38.pos_ref), custom_call_target="tpu_custom_call" | custom-call | tf_op jit(solution)/shard_map/fetch/pallas_call | solution.py:498
  87.9 5.9 %collective-permute-start.20 = (bf16[384,256]{1,0:T(8,128)(2,1)S(1)}, bf16[384,256]{1,0:T(8,128)(2,1)S(1)}, u32[]{:S(2)}, u32[]{:S(2)}) collective-permute-start(bf16[384,256]{1,0:T(8,128)(2,1)S(1)} %get-tuple-element.43), channel_id=1, source_target_pairs={{0,8},{1,9},{4,12},{5,13},{8,0},{9,1},{12,4},{13,5},{2,10},{3,11},... | collective-permute-start | bytes 589832 | tf_op jit(solution)/shard_map/ppermute | solution.py:511
  93.8 5.0 %fetch.2 = (bf16[384,256]{1,0:T(8,128)(2,1)S(1)}, bf16[384,256]{1,0:T(8,128)(2,1)S(1)}, bf16[384,256]{1,0:T(8,128)(2,1)S(1)}, bf16[384,256]{1,0:T(8,128)(2,1)S(1...) custom-call(bf16[4096,256]{1,0:T(8,128)(2,1)S(1)} %attend.1.att_ref, s32[3072,128]{1,0:T(8,128)S(1)} %get-tuple-element.38.pos_ref), custom_call_target="tpu_custom_call" | custom-call | tf_op jit(solution)/shard_map/fetch/pallas_call | solution.py:498
  99.2 2.0 %collective-permute-start.26 = (bf16[384,256]{1,0:T(8,128)(2,1)S(1)}, bf16[384,256]{1,0:T(8,128)(2,1)S(1)}, u32[]{:S(2)}, u32[]{:S(2)}) collective-permute-start(bf16[384,256]{1,0:T(8,128)(2,1)S(1)} %get-tuple-element.46), channel_id=1, source_target_pairs={{0,5},{1,4},{4,1},{5,0},{8,13},{9,12},{12,9},{13,8},{2,7},{3,6},{6... | collective-permute-start | bytes 589832 | tf_op jit(solution)/shard_map/ppermute | solution.py:511
  101.7 6.3 %collective-permute-done.22.refs_6_ = bf16[384,256]{1,0:T(8,128)(2,1)S(1)} collective-permute-done((bf16[384,256]{1,0:T(8,128)(2,1)S(1)}, bf16[384,256]{1,0:T(8,128)(2,1)S(1)}, u32[]{:S(2)}, u32[]{:S(2)}) %collective-permute-start.22) | collective-permute-done | bytes 196640 | tf_op jit(solution)/shard_map/ppermute | solution.py:511
  108.0 2.9 %collective-permute-done.24.refs_8_ = bf16[384,256]{1,0:T(8,128)(2,1)S(1)} collective-permute-done((bf16[384,256]{1,0:T(8,128)(2,1)S(1)}, bf16[384,256]{1,0:T(8,128)(2,1)S(1)}, u32[]{:S(2)}, u32[]{:S(2)}) %collective-permute-start.24) | collective-permute-done | bytes 196640 | tf_op jit(solution)/shard_map/ppermute | solution.py:511
  111.5 1.2 collective-permute-done.26.refs_10_
  112.7 8.5 %collective-permute-start.31 = (bf16[512,512]{1,0:T(8,128)(2,1)S(1)}, bf16[512,512]{1,0:T(8,128)(2,1)S(1)}, u32[]{:S(2)}, u32[]{:S(2)}) collective-permute-start(bf16[512,512]{1,0:T(8,128)(2,1)S(1)} %collective-permute-done.28.refs_11_), channel_id=1, source_target_pairs={{1,0},{0,1},{3,2},{2,3},{5,4},{4,5},{7,6},{6,7},{9,8},{8,9},{11,10... | collective-permute-start | bytes 1572872 | tf_op jit(solution)/shard_map/ppermute | solution.py:444
  121.7 1.5 collective-permute-start.19
  123.7 1.5 collective-permute-start.27
  125.2 3.7 %collective-permute-done.23.refs_7_ = bf16[384,256]{1,0:T(8,128)(2,1)S(1)} collective-permute-done((bf16[384,256]{1,0:T(8,128)(2,1)S(1)}, bf16[384,256]{1,0:T(8,128)(2,1)S(1)}, u32[]{:S(2)}, u32[]{:S(2)}) %collective-permute-start.23) | collective-permute-done | bytes 196640 | tf_op jit(solution)/shard_map/ppermute | solution.py:396
  129.0 4.2 %collective-permute-done.19.refs_3_ = bf16[384,256]{1,0:T(8,128)(2,1)S(1)} collective-permute-done((bf16[384,256]{1,0:T(8,128)(2,1)S(1)}, bf16[384,256]{1,0:T(8,128)(2,1)S(1)}, u32[]{:S(2)}, u32[]{:S(2)}) %collective-permute-start.19) | collective-permute-done | bytes 196640 | tf_op jit(solution)/shard_map/ppermute | solution.py:396
  133.7 3.7 %collective-permute-done.25.refs_9_ = bf16[384,256]{1,0:T(8,128)(2,1)S(1)} collective-permute-done((bf16[384,256]{1,0:T(8,128)(2,1)S(1)}, bf16[384,256]{1,0:T(8,128)(2,1)S(1)}, u32[]{:S(2)}, u32[]{:S(2)}) %collective-permute-start.25) | collective-permute-done | bytes 196640 | tf_op jit(solution)/shard_map/ppermute | solution.py:396
  137.9 3.7 %collective-permute-done.27.refs_11_ = bf16[384,256]{1,0:T(8,128)(2,1)S(1)} collective-permute-done((bf16[384,256]{1,0:T(8,128)(2,1)S(1)}, bf16[384,256]{1,0:T(8,128)(2,1)S(1)}, u32[]{:S(2)}, u32[]{:S(2)}) %collective-permute-start.27) | collective-permute-done | bytes 196640 | tf_op jit(solution)/shard_map/ppermute | solution.py:396
  141.6 5.2 %unpack.1.refs_4_ = bf16[1536,512]{1,0:T(8,128)(2,1)S(1)} custom-call(bf16[384,256]{1,0:T(8,128)(2,1)S(1)} %get-tuple-element.41.refs_0_, bf16[384,256]{1,0:T(8,128)(2,1)S(1)} %collective-permute-done.17.refs_1_, bf16[384,256]{1,0:T(8,128)(2,1)S(1)} %collective-permute-done.18.refs_2_, bf16[384,256]{1,0:T(8,128)(2,1)S(1)} %collective-permute-done.19.refs_3_, ...), custom_call_target="tpu_custom_call" | custom-call | tf_op jit(solution)/shard_map/unpack/pallas_call | solution.py:516
  146.8 2.2 %collective-permute-done.16.refs_3_ = bf16[384,256]{1,0:T(8,128)(2,1)S(1)} collective-permute-done((bf16[384,256]{1,0:T(8,128)(2,1)S(1)}, bf16[384,256]{1,0:T(8,128)(2,1)S(1)}, u32[]{:S(2)}, u32[]{:S(2)}) %collective-permute-start.16) | collective-permute-done | bytes 196640 | tf_op jit(solution)/shard_map/ppermute | solution.py:396
  149.1 11.1 %final.1 = bf16[1536,256]{1,0:T(8,128)(2,1)} custom-call(bf16[384,256]{1,0:T(8,128)(2,1)S(1)} %collective-permute-done.13.refs_0_, bf16[384,256]{1,0:T(8,128)(2,1)S(1)} %collective-permute-done.14.refs_1_, bf16[384,256]{1,0:T(8,128)(2,1)S(1)} %collective-permute-done.15.refs_2_, bf16[384,256]{1,0:T(8,128)(2,1)S(1)} %collective-permute-done.16.refs_3_, ...), custom_call_target="tpu_custom_call" | custom-call | tf_op jit(solution)/shard_map/final/pallas_call | solution.py:528
  (59 shorter events, 5.8 us)
Async XLA Ops:
  0.7 1.4 copy-start
  2.1 0.7 copy-start.8
  2.8 9.3 %copy-start.3 = (bf16[1024,512]{1,0:T(8,128)(2,1)S(1)}, bf16[1024,512]{1,0:T(8,128)(2,1)}, u32[]{:S(2)}) copy-start(bf16[1024,512]{1,0:T(8,128)(2,1)} %refs_10_.1) | copy-start | bytes 3145732
  2.8 10.0 %copy-start.4 = (bf16[256,512]{1,0:T(8,128)(2,1)S(1)}, bf16[256,512]{1,0:T(8,128)(2,1)}, u32[]{:S(2)}) copy-start(bf16[256,512]{1,0:T(8,128)(2,1)} %refs_8_.1) | copy-start | bytes 786436
  8.3 0.7 copy-start.10
  9.0 0.7 copy-start.11
  9.0 0.7 copy-start.12
  9.0 13.5 %collective-permute-start.1 = (bf16[400,256]{1,0:T(8,128)(2,1)}, bf16[400,256]{1,0:T(8,128)(2,1)S(1)}, u32[]{:S(2)}, u32[]{:S(2)}) collective-permute-start(bf16[400,256]{1,0:T(8,128)(2,1)} %get-tuple-element.30), channel_id=1, source_target_pairs={{0,8},{1,9},{4,12},{5,13},{8,0},{9,1},{12,4},{13,5},{2,10},{3,11},... | collective-permute-start | bytes 614408 | tf_op jit(solution)/shard_map/ppermute | solution.py:435
  9.7 14.0 %collective-permute-start.2 = (bf16[400,256]{1,0:T(8,128)(2,1)}, bf16[400,256]{1,0:T(8,128)(2,1)S(1)}, u32[]{:S(2)}, u32[]{:S(2)}) collective-permute-start(bf16[400,256]{1,0:T(8,128)(2,1)} %get-tuple-element.31), channel_id=1, source_target_pairs={{0,4},{1,5},{4,0},{5,1},{8,12},{9,13},{12,8},{13,9},{2,6},{3,7},{6... | collective-permute-start | bytes 614408 | tf_op jit(solution)/shard_map/ppermute | solution.py:435
  12.8 18.1 %collective-permute-start.3 = (bf16[400,256]{1,0:T(8,128)(2,1)}, bf16[400,256]{1,0:T(8,128)(2,1)S(1)}, u32[]{:S(2)}, u32[]{:S(2)}) collective-permute-start(bf16[400,256]{1,0:T(8,128)(2,1)} %copy-done.12), channel_id=1, source_target_pairs={{0,9},{1,8},{4,13},{5,12},{8,1},{9,0},{12,5},{13,4},{2,11},{3,10},... | collective-permute-start | bytes 614408 | tf_op jit(solution)/shard_map/ppermute | solution.py:435
  13.9 17.5 %collective-permute-start.4 = (bf16[400,256]{1,0:T(8,128)(2,1)}, bf16[400,256]{1,0:T(8,128)(2,1)S(1)}, u32[]{:S(2)}, u32[]{:S(2)}) collective-permute-start(bf16[400,256]{1,0:T(8,128)(2,1)} %copy-done.11), channel_id=1, source_target_pairs={{0,5},{1,4},{4,1},{5,0},{8,13},{9,12},{12,9},{13,8},{2,7},{3,6},{6... | collective-permute-start | bytes 614408 | tf_op jit(solution)/shard_map/ppermute | solution.py:435
  16.3 27.4 %collective-permute-start = (bf16[400,512]{1,0:T(8,128)(2,1)S(1)}, bf16[400,512]{1,0:T(8,128)(2,1)S(1)}, u32[]{:S(2)}, u32[]{:S(2)}) collective-permute-start(bf16[400,512]{1,0:T(8,128)(2,1)S(1)} %get-tuple-element.29), channel_id=1, source_target_pairs={{0,1},{1,0},{4,5},{5,4},{8,9},{9,8},{12,13},{13,12},{2,3},{3,2},{6... | collective-permute-start | bytes 1228808 | tf_op jit(solution)/shard_map/ppermute | solution.py:430
  22.5 13.2 %collective-permute-start.5 = (bf16[400,256]{1,0:T(8,128)(2,1)}, bf16[400,256]{1,0:T(8,128)(2,1)S(1)}, u32[]{:S(2)}, u32[]{:S(2)}) collective-permute-start(bf16[400,256]{1,0:T(8,128)(2,1)} %copy-done.10), channel_id=1, source_target_pairs={{0,12},{1,13},{4,8},{5,9},{8,4},{9,5},{12,0},{13,1},{2,14},{3,15},... | collective-permute-start | bytes 614408 | tf_op jit(solution)/shard_map/ppermute | solution.py:435
  23.8 14.0 %collective-permute-start.6 = (bf16[400,256]{1,0:T(8,128)(2,1)S(1)}, bf16[400,256]{1,0:T(8,128)(2,1)S(1)}, u32[]{:S(2)}, u32[]{:S(2)}) collective-permute-start(bf16[400,256]{1,0:T(8,128)(2,1)S(1)} %get-tuple-element.36), channel_id=1, source_target_pairs={{0,13},{1,12},{4,9},{5,8},{8,5},{9,4},{12,1},{13,0},{2,15},{3,14},... | collective-permute-start | bytes 614408 | tf_op jit(solution)/shard_map/ppermute | solution.py:435
  30.9 7.9 %collective-permute-start.11 = (bf16[400,256]{1,0:T(8,128)(2,1)S(1)}, bf16[400,256]{1,0:T(8,128)(2,1)S(1)}, u32[]{:S(2)}, u32[]{:S(2)}) collective-permute-start(bf16[400,256]{1,0:T(8,128)(2,1)S(1)} %collective-permute-done.1.refs_2_.refs_6_), channel_id=1, source_target_pairs={{0,2},{2,0},{1,3},{3,1},{4,6},{6,4},{5,7},{7,5},{8,10},{10,8},{9,1... | collective-permute-start | bytes 614408 | tf_op jit(solution)/shard_map/ppermute | solution.py:396
  31.4 11.8 %collective-permute-start.12 = (bf16[400,256]{1,0:T(8,128)(2,1)S(1)}, bf16[400,256]{1,0:T(8,128)(2,1)S(1)}, u32[]{:S(2)}, u32[]{:S(2)}) collective-permute-start(bf16[400,256]{1,0:T(8,128)(2,1)S(1)} %collective-permute-done.2.refs_3_.refs_8_), channel_id=1, source_target_pairs={{0,2},{2,0},{1,3},{3,1},{4,6},{6,4},{5,7},{7,5},{8,10},{10,8},{9,1... | collective-permute-start | bytes 614408 | tf_op jit(solution)/shard_map/ppermute | solution.py:396
  35.7 63.5 %collective-permute-start.28 = (bf16[512,512]{1,0:T(8,128)(2,1)}, bf16[512,512]{1,0:T(8,128)(2,1)S(1)}, u32[]{:S(2)}, u32[]{:S(2)}) collective-permute-start(bf16[512,512]{1,0:T(8,128)(2,1)} %constant_dynamic-slice_fusion.1), channel_id=1, source_target_pairs={{0,2},{2,0},{1,3},{3,1},{4,6},{6,4},{5,7},{7,5},{8,10},{10,8},{9,1... | collective-permute-start | bytes 1572872 | tf_op jit(solution)/shard_map/ppermute | solution.py:396
  37.8 21.1 %collective-permute-start.9 = (bf16[400,256]{1,0:T(8,128)(2,1)S(1)}, bf16[400,256]{1,0:T(8,128)(2,1)S(1)}, u32[]{:S(2)}, u32[]{:S(2)}) collective-permute-start(bf16[400,256]{1,0:T(8,128)(2,1)S(1)} %collective-permute-done.3.refs_4_.refs_8_), channel_id=1, source_target_pairs={{0,2},{2,0},{1,3},{3,1},{4,6},{6,4},{5,7},{7,5},{8,10},{10,8},{9,1... | collective-permute-start | bytes 614408 | tf_op jit(solution)/shard_map/ppermute | solution.py:396
  38.9 24.4 %collective-permute-start.10 = (bf16[400,256]{1,0:T(8,128)(2,1)S(1)}, bf16[400,256]{1,0:T(8,128)(2,1)S(1)}, u32[]{:S(2)}, u32[]{:S(2)}) collective-permute-start(bf16[400,256]{1,0:T(8,128)(2,1)S(1)} %collective-permute-done.4.refs_5_.refs_10_), channel_id=1, source_target_pairs={{0,2},{2,0},{1,3},{3,1},{4,6},{6,4},{5,7},{7,5},{8,10},{10,8},{9,1... | collective-permute-start | bytes 614408 | tf_op jit(solution)/shard_map/ppermute | solution.py:396
  43.2 27.5 %collective-permute-start.7 = (bf16[400,256]{1,0:T(8,128)(2,1)S(1)}, bf16[400,256]{1,0:T(8,128)(2,1)S(1)}, u32[]{:S(2)}, u32[]{:S(2)}) collective-permute-start(bf16[400,256]{1,0:T(8,128)(2,1)S(1)} %collective-permute-done.5.refs_6_.refs_8_), channel_id=1, source_target_pairs={{0,2},{2,0},{1,3},{3,1},{4,6},{6,4},{5,7},{7,5},{8,10},{10,8},{9,1... | collective-permute-start | bytes 614408 | tf_op jit(solution)/shard_map/ppermute | solution.py:396
  43.8 28.3 %collective-permute-start.8 = (bf16[400,256]{1,0:T(8,128)(2,1)S(1)}, bf16[400,256]{1,0:T(8,128)(2,1)S(1)}, u32[]{:S(2)}, u32[]{:S(2)}) collective-permute-start(bf16[400,256]{1,0:T(8,128)(2,1)S(1)} %collective-permute-done.6.refs_7_.refs_10_), channel_id=1, source_target_pairs={{0,2},{2,0},{1,3},{3,1},{4,6},{6,4},{5,7},{7,5},{8,10},{10,8},{9,1... | collective-permute-start | bytes 614408 | tf_op jit(solution)/shard_map/ppermute | solution.py:396
  58.9 40.2 %collective-permute-start.29 = (bf16[512,256]{1,0:T(8,128)(2,1)}, bf16[512,256]{1,0:T(8,128)(2,1)S(1)}, u32[]{:S(2)}, u32[]{:S(2)}) collective-permute-start(bf16[512,256]{1,0:T(8,128)(2,1)} %dynamic_slice.10), channel_id=1, source_target_pairs={{0,2},{2,0},{1,3},{3,1},{4,6},{6,4},{5,7},{7,5},{8,10},{10,8},{9,1... | collective-permute-start | bytes 786440 | tf_op jit(solution)/shard_map/ppermute | solution.py:396
  63.3 35.7 %collective-permute-start.30 = (bf16[128,512]{1,0:T(8,128)(2,1)S(1)}, bf16[128,512]{1,0:T(8,128)(2,1)S(1)}, u32[]{:S(2)}, u32[]{:S(2)}) collective-permute-start(bf16[128,512]{1,0:T(8,128)(2,1)S(1)} %constant_dynamic-slice_fusion), channel_id=1, source_target_pairs={{0,2},{2,0},{1,3},{3,1},{4,6},{6,4},{5,7},{7,5},{8,10},{10,8},{9,1... | collective-permute-start | bytes 393224 | tf_op jit(solution)/shard_map/ppermute | solution.py:396
  68.0 4.1 %copy-start.5 = (bf16[2,512,256]{2,1,0:T(8,128)(2,1)S(1)}, bf16[2,512,256]{2,1,0:T(8,128)(2,1)}, u32[]{:S(2)}) copy-start(bf16[2,512,256]{2,1,0:T(8,128)(2,1)} %refs_13_.1) | copy-start | bytes 1572868
  68.0 4.1 %copy-start.6 = (bf16[512,256]{1,0:T(8,128)(2,1)S(1)}, bf16[512,256]{1,0:T(8,128)(2,1)}, u32[]{:S(2)}) copy-start(bf16[512,256]{1,0:T(8,128)(2,1)} %refs_14_.1) | copy-start | bytes 786436
  68.0 4.1 %copy-start.7 = (s32[128]{0:T(128)S(1)}, s32[128]{0:T(128)}, u32[]{:S(2)}) copy-start(s32[128]{0:T(128)} %counts_ref.1) | copy-start | bytes 1540
  87.9 13.2 %collective-permute-start.20 = (bf16[384,256]{1,0:T(8,128)(2,1)S(1)}, bf16[384,256]{1,0:T(8,128)(2,1)S(1)}, u32[]{:S(2)}, u32[]{:S(2)}) collective-permute-start(bf16[384,256]{1,0:T(8,128)(2,1)S(1)} %get-tuple-element.43), channel_id=1, source_target_pairs={{0,8},{1,9},{4,12},{5,13},{8,0},{9,1},{12,4},{13,5},{2,10},{3,11},... | collective-permute-start | bytes 589832 | tf_op jit(solution)/shard_map/ppermute | solution.py:511
  98.9 9.2 %collective-permute-start.22 = (bf16[384,256]{1,0:T(8,128)(2,1)S(1)}, bf16[384,256]{1,0:T(8,128)(2,1)S(1)}, u32[]{:S(2)}, u32[]{:S(2)}) collective-permute-start(bf16[384,256]{1,0:T(8,128)(2,1)S(1)} %get-tuple-element.44), channel_id=1, source_target_pairs={{0,4},{1,5},{4,0},{5,1},{8,12},{9,13},{12,8},{13,9},{2,6},{3,7},{6... | collective-permute-start | bytes 589832 | tf_op jit(solution)/shard_map/ppermute | solution.py:511
  99.0 9.1 %collective-permute-start.18 = (bf16[384,256]{1,0:T(8,128)(2,1)S(1)}, bf16[384,256]{1,0:T(8,128)(2,1)S(1)}, u32[]{:S(2)}, u32[]{:S(2)}) collective-permute-start(bf16[384,256]{1,0:T(8,128)(2,1)S(1)} %get-tuple-element.42), channel_id=1, source_target_pairs={{0,1},{1,0},{4,5},{5,4},{8,9},{9,8},{12,13},{13,12},{2,3},{3,2},{6... | collective-permute-start | bytes 589832 | tf_op jit(solution)/shard_map/ppermute | solution.py:511
  99.0 11.9 %collective-permute-start.24 = (bf16[384,256]{1,0:T(8,128)(2,1)S(1)}, bf16[384,256]{1,0:T(8,128)(2,1)S(1)}, u32[]{:S(2)}, u32[]{:S(2)}) collective-permute-start(bf16[384,256]{1,0:T(8,128)(2,1)S(1)} %get-tuple-element.45), channel_id=1, source_target_pairs={{0,9},{1,8},{4,13},{5,12},{8,1},{9,0},{12,5},{13,4},{2,11},{3,10},... | collective-permute-start | bytes 589832 | tf_op jit(solution)/shard_map/ppermute | solution.py:511
  99.2 13.5 %collective-permute-start.26 = (bf16[384,256]{1,0:T(8,128)(2,1)S(1)}, bf16[384,256]{1,0:T(8,128)(2,1)S(1)}, u32[]{:S(2)}, u32[]{:S(2)}) collective-permute-start(bf16[384,256]{1,0:T(8,128)(2,1)S(1)} %get-tuple-element.46), channel_id=1, source_target_pairs={{0,5},{1,4},{4,1},{5,0},{8,13},{9,12},{12,9},{13,8},{2,7},{3,6},{6... | collective-permute-start | bytes 589832 | tf_op jit(solution)/shard_map/ppermute | solution.py:511
  101.2 20.0 %collective-permute-start.17 = (bf16[384,256]{1,0:T(8,128)(2,1)S(1)}, bf16[384,256]{1,0:T(8,128)(2,1)S(1)}, u32[]{:S(2)}, u32[]{:S(2)}) collective-permute-start(bf16[384,256]{1,0:T(8,128)(2,1)S(1)} %get-tuple-element.41.refs_0_), channel_id=1, source_target_pairs={{0,2},{2,0},{1,3},{3,1},{4,6},{6,4},{5,7},{7,5},{8,10},{10,8},{9,1... | collective-permute-start | bytes 589832 | tf_op jit(solution)/shard_map/ppermute | solution.py:396
  108.0 13.7 %collective-permute-start.13 = (bf16[384,256]{1,0:T(8,128)(2,1)S(1)}, bf16[384,256]{1,0:T(8,128)(2,1)S(1)}, u32[]{:S(2)}, u32[]{:S(2)}) collective-permute-start(bf16[384,256]{1,0:T(8,128)(2,1)S(1)} %get-tuple-element.39), channel_id=1, source_target_pairs={{0,12},{1,13},{4,8},{5,9},{8,4},{9,5},{12,0},{13,1},{2,14},{3,15},... | collective-permute-start | bytes 589832 | tf_op jit(solution)/shard_map/ppermute | solution.py:511
  108.0 15.2 %collective-permute-start.15 = (bf16[384,256]{1,0:T(8,128)(2,1)S(1)}, bf16[384,256]{1,0:T(8,128)(2,1)S(1)}, u32[]{:S(2)}, u32[]{:S(2)}) collective-permute-start(bf16[384,256]{1,0:T(8,128)(2,1)S(1)} %get-tuple-element.40), channel_id=1, source_target_pairs={{0,13},{1,12},{4,9},{5,8},{8,5},{9,4},{12,1},{13,0},{2,15},{3,14},... | collective-permute-start | bytes 589832 | tf_op jit(solution)/shard_map/ppermute | solution.py:511
  111.0 12.8 %collective-permute-start.21 = (bf16[384,256]{1,0:T(8,128)(2,1)S(1)}, bf16[384,256]{1,0:T(8,128)(2,1)S(1)}, u32[]{:S(2)}, u32[]{:S(2)}) collective-permute-start(bf16[384,256]{1,0:T(8,128)(2,1)S(1)} %collective-permute-done.20.refs_4_), channel_id=1, source_target_pairs={{0,2},{2,0},{1,3},{3,1},{4,6},{6,4},{5,7},{7,5},{8,10},{10,8},{9,1... | collective-permute-start | bytes 589832 | tf_op jit(solution)/shard_map/ppermute | solution.py:396
  112.7 36.4 %collective-permute-start.31 = (bf16[512,512]{1,0:T(8,128)(2,1)S(1)}, bf16[512,512]{1,0:T(8,128)(2,1)S(1)}, u32[]{:S(2)}, u32[]{:S(2)}) collective-permute-start(bf16[512,512]{1,0:T(8,128)(2,1)S(1)} %collective-permute-done.28.refs_11_), channel_id=1, source_target_pairs={{1,0},{0,1},{3,2},{2,3},{5,4},{4,5},{7,6},{6,7},{9,8},{8,9},{11,10... | collective-permute-start | bytes 1572872 | tf_op jit(solution)/shard_map/ppermute | solution.py:444
  121.2 7.8 %collective-permute-start.23 = (bf16[384,256]{1,0:T(8,128)(2,1)S(1)}, bf16[384,256]{1,0:T(8,128)(2,1)S(1)}, u32[]{:S(2)}, u32[]{:S(2)}) collective-permute-start(bf16[384,256]{1,0:T(8,128)(2,1)S(1)} %collective-permute-done.22.refs_6_), channel_id=1, source_target_pairs={{0,2},{2,0},{1,3},{3,1},{4,6},{6,4},{5,7},{7,5},{8,10},{10,8},{9,1... | collective-permute-start | bytes 589832 | tf_op jit(solution)/shard_map/ppermute | solution.py:396
  121.7 11.5 %collective-permute-start.19 = (bf16[384,256]{1,0:T(8,128)(2,1)S(1)}, bf16[384,256]{1,0:T(8,128)(2,1)S(1)}, u32[]{:S(2)}, u32[]{:S(2)}) collective-permute-start(bf16[384,256]{1,0:T(8,128)(2,1)S(1)} %collective-permute-done.18.refs_2_), channel_id=1, source_target_pairs={{0,2},{2,0},{1,3},{3,1},{4,6},{6,4},{5,7},{7,5},{8,10},{10,8},{9,1... | collective-permute-start | bytes 589832 | tf_op jit(solution)/shard_map/ppermute | solution.py:396
  123.2 14.2 %collective-permute-start.25 = (bf16[384,256]{1,0:T(8,128)(2,1)S(1)}, bf16[384,256]{1,0:T(8,128)(2,1)S(1)}, u32[]{:S(2)}, u32[]{:S(2)}) collective-permute-start(bf16[384,256]{1,0:T(8,128)(2,1)S(1)} %collective-permute-done.24.refs_8_), channel_id=1, source_target_pairs={{0,2},{2,0},{1,3},{3,1},{4,6},{6,4},{5,7},{7,5},{8,10},{10,8},{9,1... | collective-permute-start | bytes 589832 | tf_op jit(solution)/shard_map/ppermute | solution.py:396
  123.7 17.8 %collective-permute-start.27 = (bf16[384,256]{1,0:T(8,128)(2,1)S(1)}, bf16[384,256]{1,0:T(8,128)(2,1)S(1)}, u32[]{:S(2)}, u32[]{:S(2)}) collective-permute-start(bf16[384,256]{1,0:T(8,128)(2,1)S(1)} %collective-permute-done.26.refs_10_), channel_id=1, source_target_pairs={{0,2},{2,0},{1,3},{3,1},{4,6},{6,4},{5,7},{7,5},{8,10},{10,8},{9,1... | collective-permute-start | bytes 589832 | tf_op jit(solution)/shard_map/ppermute | solution.py:396
  129.0 17.9 %collective-permute-start.32 = (bf16[512,256]{1,0:T(8,128)(2,1)S(1)}, bf16[512,256]{1,0:T(8,128)(2,1)S(1)}, u32[]{:S(2)}, u32[]{:S(2)}) collective-permute-start(bf16[512,256]{1,0:T(8,128)(2,1)S(1)} %collective-permute-done.29.refs_12_), channel_id=1, source_target_pairs={{1,0},{0,1},{3,2},{2,3},{5,4},{4,5},{7,6},{6,7},{9,8},{8,9},{11,10... | collective-permute-start | bytes 786440 | tf_op jit(solution)/shard_map/ppermute | solution.py:444
  133.2 13.7 %collective-permute-start.14 = (bf16[384,256]{1,0:T(8,128)(2,1)S(1)}, bf16[384,256]{1,0:T(8,128)(2,1)S(1)}, u32[]{:S(2)}, u32[]{:S(2)}) collective-permute-start(bf16[384,256]{1,0:T(8,128)(2,1)S(1)} %collective-permute-done.13.refs_0_), channel_id=1, source_target_pairs={{0,2},{2,0},{1,3},{3,1},{4,6},{6,4},{5,7},{7,5},{8,10},{10,8},{9,1... | collective-permute-start | bytes 589832 | tf_op jit(solution)/shard_map/ppermute | solution.py:396
  137.4 11.7 %collective-permute-start.16 = (bf16[384,256]{1,0:T(8,128)(2,1)S(1)}, bf16[384,256]{1,0:T(8,128)(2,1)S(1)}, u32[]{:S(2)}, u32[]{:S(2)}) collective-permute-start(bf16[384,256]{1,0:T(8,128)(2,1)S(1)} %collective-permute-done.15.refs_2_), channel_id=1, source_target_pairs={{0,2},{2,0},{1,3},{3,1},{4,6},{6,4},{5,7},{7,5},{8,10},{10,8},{9,1... | collective-permute-start | bytes 589832 | tf_op jit(solution)/shard_map/ppermute | solution.py:396
  141.6 5.2 %collective-permute-start.33 = (bf16[128,512]{1,0:T(8,128)(2,1)S(1)}, bf16[128,512]{1,0:T(8,128)(2,1)S(1)}, u32[]{:S(2)}, u32[]{:S(2)}) collective-permute-start(bf16[128,512]{1,0:T(8,128)(2,1)S(1)} %collective-permute-done.30.refs_13_), channel_id=1, source_target_pairs={{1,0},{0,1},{3,2},{2,3},{5,4},{4,5},{7,6},{6,7},{9,8},{8,9},{11,10... | collective-permute-start | bytes 393224 | tf_op jit(solution)/shard_map/ppermute | solution.py:444
  141.6 7.5 %copy-start.1 = (bf16[1536,512]{1,0:T(8,128)(2,1)S(1)}, bf16[1536,512]{1,0:T(8,128)(2,1)}, u32[]{:S(2)}) copy-start(bf16[1536,512]{1,0:T(8,128)(2,1)} %refs_6_.1) | copy-start | bytes 4718596
  141.6 7.5 %copy-start.2 = (bf16[512,1024]{1,0:T(8,128)(2,1)S(1)}, bf16[512,1024]{1,0:T(8,128)(2,1)}, u32[]{:S(2)}) copy-start(bf16[512,1024]{1,0:T(8,128)(2,1)} %refs_9_.1) | copy-start | bytes 3145732
  141.6 7.5 %copy-start.9 = (f32[512]{0:T(512)S(1)}, f32[512]{0:T(512)}, u32[]{:S(2)}) copy-start(f32[512]{0:T(512)} %param.18) | copy-start | bytes 6148

commit v2 on v1

--- a/solution.py
+++ b/solution.py
@@ -14,12 +14,14 @@
 META = 16
 LANES = 128
 OWN = ("space", "sub")
+FIRST = 1
+SLICES_AT = 4
+FINAL_BLOCKS = 2
 
 
 F32 = jnp.float32
 BF16 = jnp.bfloat16
 VM = pl.BlockSpec(memory_space=pltpu.VMEM)
-HB = pl.BlockSpec(memory_space=pltpu.MemorySpace.HBM)
 SM = pl.BlockSpec(memory_space=pltpu.SMEM)
 PARAMS = pltpu.CompilerParams(vmem_limit_bytes=20 * 1024 * 1024)
 
@@ -58,29 +60,36 @@
     return lax.axis_index("space") * sub_size + lax.axis_index("sub")
 
 
-def pack_kernel(ids_ref, vox_hbm, gain_hbm, *refs, steps, sub_size, near, cap, wins):
-    n = steps.n
-    col_ref, outs = refs[0], refs[1 : 1 + n]
-    normed_ref, cnt_ref, vox_ref, gain_ref, sem, sem_gain = refs[1 + n :]
-    rows, _ = vox_ref.shape
-    me = own_index(sub_size)
-    mp = lax.axis_index("mp")
-    load = pltpu.make_async_copy(vox_hbm, vox_ref, sem)
-    load.start()
-    load_gain = pltpu.make_async_copy(gain_hbm, gain_ref, sem_gain)
-    load_gain.start()
+def pack_bucket(out, k, dest, row_iota, normed_ref, cnt_ref, me, mp, steps, near, cap):
+    piece = out.shape[1]
+    pick = (dest == row_iota + k * cap).astype(F32).astype(BF16)
+    if k < near:
+        source = normed_ref[...]
+    else:
+        source = normed_ref[:, pl.ds(pl.multiple_of(mp * piece, LANES), piece)]
+    out[0:cap, :] = dot(pick, source).astype(BF16)
+    at = pl.ds(pl.multiple_of(steps.to(me, k) * WIN_DEV, WIN_DEV), WIN_DEV)
+    tail = cnt_ref[at, :]
+    out[cap : cap + META, :] = jnp.concatenate([tail] * (piece // LANES), axis=1).astype(BF16)
+
+
+def rank_kernel(ids_ref, dest_ref, cnt_ref, *, steps, sub_size, cap):
+    wins = cnt_ref.shape[0]
     ids = ids_ref[...]
+    rows = ids.shape[1]
     step = 256
     win_iota = lax.broadcasted_iota(jnp.int32, (wins, step), 0)
     upper = (
         lax.broadcasted_iota(jnp.int32, (step, step), 0)
         < lax.broadcasted_iota(jnp.int32, (step, step), 1)
     ).astype(F32).astype(BF16)
-    hots, counts = [], jnp.zeros((wins, 1), F32)
+    hots, sums = [], []
+    counts = jnp.zeros((wins, 1), F32)
     for b in range(rows // step):
         hot = (ids[:, b * step : (b + 1) * step] == win_iota).astype(F32)
         hots.append(hot)
-        counts = counts + jnp.sum(hot, axis=1, keepdims=True)
+        sums.append(jnp.sum(hot, axis=1, keepdims=True))
+        counts = counts + sums[-1]
     wide = jnp.broadcast_to(counts, (wins, LANES))
     cnt_ref[...] = wide
     r_io = lax.broadcasted_iota(jnp.int32, (wins, wins), 0)
@@ -88,29 +97,37 @@
     same = (r_io // WIN_DEV == c_io // WIN_DEV) & (c_io < r_io)
     carry = dot(same.astype(F32).astype(BF16), wide.astype(BF16))[:, :1]
     ranks = []
-    for hot in hots:
+    for hot, total in zip(hots, sums):
         cum = dot(hot.astype(BF16), upper) + carry
         ranks.append(jnp.sum(hot * cum, axis=0, keepdims=True))
-        carry = carry + jnp.sum(hot, axis=1, keepdims=True)
+        carry = carry + total
     rank = jnp.concatenate(ranks, axis=1).astype(jnp.int32)
-    dest = steps.step(me, ids // WIN_DEV) * cap + rank
+    dest_ref[...] = steps.step(own_index(sub_size), ids // WIN_DEV) * cap + rank
+
+
+def pack_kernel(
+    dest_ref, cnt_ref, vox_ref, gain_ref, normed_ref, *outs, steps, sub_size, near, cap, names
+):
+    rows = vox_ref.shape[0]
+    me = own_index(sub_size)
+    mp = lax.axis_index("mp")
+    row_iota = lax.broadcasted_iota(jnp.int32, (cap, rows), 0)
+    normed_ref[...] = layer_norm(vox_ref[...].astype(F32), gain_ref[...]).astype(BF16)
+    for out, k in zip(outs, names):
+        pack_bucket(
+            out, k, dest_ref[...], row_iota, normed_ref, cnt_ref, me, mp, steps, near, cap
+        )
+
+
+def pack_rest_kernel(dest_ref, normed_ref, cnt_ref, col_ref, *outs, steps, sub_size, near, cap, names):
+    rows = normed_ref.shape[0]
+    me = own_index(sub_size)
+    mp = lax.axis_index("mp")
+    dest = dest_ref[...]
+    row_iota = lax.broadcasted_iota(jnp.int32, (cap, rows), 0)
+    for out, k in zip(outs, names):
+        pack_bucket(out, k, dest, row_iota, normed_ref, cnt_ref, me, mp, steps, near, cap)
     col_ref[...] = jnp.transpose(jnp.broadcast_to(dest.astype(F32), (LANES, rows))).astype(jnp.int32)
-    row_iota = lax.broadcasted_iota(jnp.int32, (cap, rows), 0)
-    load_gain.wait()
-    load.wait()
-    normed_ref[...] = layer_norm(vox_ref[...].astype(F32), gain_ref[...]).astype(BF16)
-    for k in range(n):
-        out = outs[k]
-        piece = out.shape[1]
-        pick = (dest == row_iota + k * cap).astype(F32).astype(BF16)
-        if k < near:
-            source = normed_ref[...]
-        else:
-            source = normed_ref[:, pl.ds(pl.multiple_of(mp * piece, LANES), piece)]
-        out[0:cap, :] = dot(pick, source).astype(BF16)
-        owner = steps.to(me, k)
-        tail = cnt_ref[pl.ds(pl.multiple_of(owner * WIN_DEV, WIN_DEV), WIN_DEV), :]
-        out[cap : cap + META, :] = jnp.concatenate([tail] * (piece // LANES), axis=1).astype(BF16)
 
 
 def places(tails, cap):
@@ -132,12 +149,6 @@
     return out
 
 
-def read_piece(refs, t, piece, cap, block):
-    if len(refs) == 1:
-        return refs[0][0:cap, pl.ds(pl.multiple_of(block * piece, LANES), piece)]
-    return refs[t][0:cap, :]
-
-
 def window_bits(tail):
     power = jnp.left_shift(1, lax.broadcasted_iota(jnp.int32, (META, LANES), 0)).astype(F32)
     lane = lax.broadcasted_iota(jnp.int32, (META, LANES), 1)
@@ -152,23 +163,41 @@
     return out, at
 
 
-def add_rows(dest, hot, part, mp, mp_steps, piece, cap):
+def add_rows(dest, hot, part, which, mp, mp_steps, piece, cap):
+    for t, ref in zip(which, part if len(part) == len(which) else part * len(which)):
+        if ref.shape[1] > piece:
+            block = mp_steps.frm(mp, t)
+            rows = ref[0:cap, pl.ds(pl.multiple_of(block * piece, LANES), piece)]
+        else:
+            rows = ref[0:cap, :]
+        cols = slice(t * piece, (t + 1) * piece)
+        dest[:, cols] = dest[:, cols] + dot(hot, rows).astype(BF16)
+
+
+def weights_kernel(wqk_ref, wv_ref, out_ref, mp, mp_steps, piece):
+    local = wv_ref.shape[1]
     for t in range(mp_steps.n):
-        cols = slice(t * piece, (t + 1) * piece)
-        term = dot(hot, read_piece(part, t, piece, cap, mp_steps.frm(mp, t)))
-        dest[:, cols] = dest[:, cols] + term.astype(BF16)
-
-
-def place_kernel(*refs, names, parts, cap, mp_steps, tails_count, piece, has_prev, with_pos):
-    table, pos_ref = refs[-2:] if with_pos else (refs[-1], None)
+        block = pl.ds(pl.multiple_of(mp_steps.frm(mp, t) * piece, piece), piece)
+        to = slice(t * piece, (t + 1) * piece)
+        out_ref[to, 0:local] = wqk_ref[0, block, :]
+        out_ref[to, local : 2 * local] = wqk_ref[1, block, :]
+        out_ref[to, 2 * local : 3 * local] = wv_ref[block, :]
+
+
+def place_kernel(
+    *refs, names, parts, which, cap, mp_steps, tails_count, piece, has_prev, weights
+):
+    table, side_ref = refs[-2:]
     part_refs, at = split_refs(refs, tails_count, parts)
     mp = lax.axis_index("mp")
     tails = [r[cap : cap + META, 0:LANES] for r in refs[:tails_count]]
     where_all = places(tails, cap)
     bits = [window_bits(tails[i]) for i in names]
     slot = lax.broadcasted_iota(jnp.int32, (WLEN, cap), 0)
-    for i, p in enumerate(where_all if with_pos else []):
-        pos_ref[i * cap : (i + 1) * cap, :] = jnp.transpose(
+    if weights:
+        weights_kernel(*refs[at : at + 2], side_ref, mp, mp_steps, piece)
+    for i, p in enumerate([] if weights else where_all):
+        side_ref[i * cap : (i + 1) * cap, :] = jnp.transpose(
             jnp.broadcast_to(p.astype(F32), (LANES, cap))
         ).astype(jnp.int32)
 
@@ -182,24 +211,20 @@
             @pl.when((bits[i] >> w) & 1 == 1)
             def _():
                 hot = (slot + w * WLEN == where_all[name]).astype(F32).astype(BF16)
-                add_rows(rows, hot, part_refs[i], mp, mp_steps, piece, cap)
-
-
-def project_kernel(*refs, names, parts, cap, mp_steps, tails_count, piece, local, sub_size, group):
-    qkv_ref, weight_ref, member_ref = refs[-3:]
+                add_rows(rows, hot, part_refs[i], which[i], mp, mp_steps, piece, cap)
+
+
+def project_kernel(
+    *refs, names, parts, which, cap, mp_steps, tails_count, piece, sub_size, group
+):
+    qkv_ref, member_ref = refs[-2:]
     part_refs, at = split_refs(refs, tails_count, parts)
-    table_ref, wqk_ref, wv_ref, counts_ref = refs[at : at + 4]
+    table_ref, weight_ref, counts_ref = refs[at : at + 3]
     mp = lax.axis_index("mp")
     me = own_index(sub_size)
     tails = [r[cap : cap + META, 0:LANES] for r in refs[:tails_count]]
     where_all = places(tails, cap)
     bits = [window_bits(tails[i]) for i in names]
-    for t in range(mp_steps.n):
-        block = pl.ds(pl.multiple_of(mp_steps.frm(mp, t) * piece, piece), piece)
-        to = slice(t * piece, (t + 1) * piece)
-        weight_ref[to, 0:local] = wqk_ref[0, block, :]
-        weight_ref[to, local : 2 * local] = wqk_ref[1, block, :]
-        weight_ref[to, 2 * local : 3 * local] = wv_ref[block, :]
     slot = lax.broadcasted_iota(jnp.int32, (WLEN, cap), 0)
     windows = table_ref.shape[0] // WLEN
 
@@ -221,7 +246,7 @@
                     @pl.when((bits[i] >> w) & 1 == 1)
                     def _():
                         hot = (slot + w * WLEN == where_all[name]).astype(F32).astype(BF16)
-                        add_rows(part_rows, hot, part_refs[i], mp, mp_steps, piece, cap)
+                        add_rows(part_rows, hot, part_refs[i], which[i], mp, mp_steps, piece, cap)
 
             qkv_ref[rows, :] = dot(member_ref[...], weight_ref[...]).astype(BF16)
 
@@ -298,7 +323,7 @@
     return hot[:, 0:cap]
 
 
-def unpack_kernel(*refs, names, cap, parts, local, block_rows):
+def unpack_kernel(*refs, items, cap, parts, local, block_rows):
     col_ref, out_ref = refs[-2], refs[-1]
     lane = lax.broadcasted_iota(jnp.int32, (block_rows, LANES), 1)
 
@@ -307,22 +332,23 @@
         rows = pl.ds(pl.multiple_of(b * block_rows, block_rows), block_rows)
         dest = col_ref[rows, :]
         heads = [None] * parts
-        for i, k in enumerate(names):
-            hot = spots(dest, lane, k * cap, cap)
-            for t in range(parts):
-                term = dot(hot, refs[i * parts + t][...])
-                heads[t] = term if heads[t] is None else heads[t] + term
+        hots = {}
+        for (k, t), ref in zip(items, refs):
+            if k not in hots:
+                hots[k] = spots(dest, lane, k * cap, cap)
+            term = dot(hots[k], ref[...])
+            heads[t] = term if heads[t] is None else heads[t] + term
         for t in range(parts):
             out_ref[rows, t * local : (t + 1) * local] = heads[t].astype(BF16)
 
 
-def final_kernel(*refs, names, cap, mp_steps, sub_size, local, block_rows):
+def final_kernel(*refs, items, cap, mp_steps, sub_size, local, block_rows):
     parts = mp_steps.n
-    at = len(names) * parts
+    at = len(items)
     early_ref, col_ref, vox_ref, gain_ref, wout_ref, wup_ref, wdown_ref = refs[at : at + 7]
     at += 7
     extra = refs[at : at + 3 * sub_size * (parts - 1)]
-    out_ref, proj_ref = refs[-2], refs[-1]
+    out_ref, proj_ref = refs[-2:]
     mp = lax.axis_index("mp")
     sub = lax.axis_index("sub")
     width = vox_ref.shape[1]
@@ -345,10 +371,11 @@
         rows = pl.ds(pl.multiple_of(b * block_rows, block_rows), block_rows)
         dest = col_ref[rows, :]
         heads = [early_ref[rows, t * local : (t + 1) * local].astype(F32) for t in range(parts)]
-        for i, k in enumerate(names):
-            hot = spots(dest, lane, k * cap, cap)
-            for t in range(parts):
-                heads[t] = heads[t] + dot(hot, refs[i * parts + t][...])
+        hots = {}
+        for (k, t), ref in zip(items, refs):
+            if k not in hots:
+                hots[k] = spots(dest, lane, k * cap, cap)
+            heads[t] = heads[t] + dot(hots[k], ref[...])
         every = jnp.concatenate([h.astype(BF16) for h in heads], axis=1)
         after = vox_ref[rows, :].astype(F32) + dot(every, proj_ref[...])
         normed = layer_norm(after, gain_ref[...]).astype(BF16)
@@ -368,7 +395,7 @@
 
 def far_order(n, near):
     if n == 8 and near == 2:
-        return [4, 2, 5, 3, 6, 7]
+        return [4, 2, 6, 5, 3, 7]
     return list(range(near, n))
 
 
@@ -386,7 +413,6 @@
     near = near_count(n, sub_size)
     far = far_order(n, near)
     order = list(range(near)) + far
-    early, late = order[:-2], order[-2:]
     piece = width // mp_size
     local = w_value.shape[1]
     mp = lax.axis_index("mp")
@@ -396,23 +422,44 @@
         return lax.ppermute(x, "mp", mp_steps.perm(t))
 
     bucket = cap + META
-    packed = pl.pallas_call(
-        functools.partial(
-            pack_kernel, steps=steps, sub_size=sub_size, near=near, cap=cap, wins=n * WIN_DEV
-        ),
-        out_shape=[jax.ShapeDtypeStruct((rows, LANES), jnp.int32)]
-        + [jax.ShapeDtypeStruct((bucket, width if k < near else piece), BF16) for k in range(n)],
-        in_specs=[VM, HB, HB],
-        out_specs=[VM] * (n + 1),
-        scratch_shapes=[
-            pltpu.VMEM((rows, width), BF16), pltpu.VMEM((n * WIN_DEV, LANES), F32),
-            pltpu.VMEM((rows, width), BF16), pltpu.VMEM((1, width), F32),
-            pltpu.SemaphoreType.DMA, pltpu.SemaphoreType.DMA,
+
+    def bucket_shape(k):
+        return jax.ShapeDtypeStruct((bucket, width if k < near else piece), BF16)
+
+    first, rest = far[:FIRST], far[FIRST:] + list(range(near))
+    common = dict(steps=steps, sub_size=sub_size, near=near, cap=cap)
+    dest, counts = pl.pallas_call(
+        functools.partial(rank_kernel, steps=steps, sub_size=sub_size, cap=cap),
+        out_shape=[
+            jax.ShapeDtypeStruct((1, rows), jnp.int32),
+            jax.ShapeDtypeStruct((n * WIN_DEV, LANES), F32),
         ],
+        in_specs=[VM],
+        out_specs=[VM, VM],
+        compiler_params=PARAMS,
+        name="rank",
+    )(window_ids.reshape(1, rows))
+    got = pl.pallas_call(
+        functools.partial(pack_kernel, names=first, **common),
+        out_shape=[jax.ShapeDtypeStruct((rows, width), BF16)] + [bucket_shape(k) for k in first],
+        in_specs=[VM] * 4,
+        out_specs=[VM] * (1 + len(first)),
         compiler_params=PARAMS,
         name="pack",
-    )(window_ids.reshape(1, rows), voxels, norm_gain.reshape(1, width))
-    dest_col, packed = packed[0], packed[1:]
+    )(dest, counts, voxels, norm_gain.reshape(1, width))
+    normed = got[0]
+    packed = dict(zip(first, got[1:]))
+    got = pl.pallas_call(
+        functools.partial(pack_rest_kernel, names=rest, **common),
+        out_shape=[jax.ShapeDtypeStruct((rows, LANES), jnp.int32)]
+        + [bucket_shape(k) for k in rest],
+        in_specs=[VM] * 3,
+        out_specs=[VM] * (1 + len(rest)),
+        compiler_params=PARAMS,
+        name="pack",
+    )(dest, normed, counts)
+    dest_col = got[0]
+    packed.update(zip(rest, got[1:]))
 
     part = w_up.shape[1] // sub_size
     out_part = w_out.shape[0] // sub_size
@@ -430,7 +477,7 @@
         arrived[k] = [lax.ppermute(packed[k], OWN, steps.perm(k))]
     for i, k in enumerate(far):
         sent = packed[k]
-        if i == 2:
+        if i == min(SLICES_AT, len(far) - 1):
             sent, pieces = lax.optimization_barrier((sent, pieces))
         got = lax.ppermute(sent, OWN, steps.perm(k))
         arrived[k] = [got] + [over_mp(got, t) for t in range(1, mp_size)]
@@ -445,42 +492,57 @@
 
     slots = WIN_DEV * WLEN
     tails = [arrived[k][0] for k in order]
-    cuts = [0, min(near + 2, len(early)), len(early)]
+    every = tuple(range(mp_size))
+    cut = near + 2
+    work = [
+        [(i, every) for i in range(cut)],
+        [(i, every) for i in range(cut, n - 1)] + [(n - 1, every[:1])],
+        [(n - 1, every[1:])] * (mp_size > 1),
+    ]
+
+    def place_args(items):
+        names, which = [i for i, _ in items], [w for _, w in items]
+        parts = [
+            arrived[order[i]] if i < near else [arrived[order[i]][t] for t in w] for i, w in items
+        ]
+        keys = dict(names=names, which=which, parts=[len(p) for p in parts])
+        return keys, [x for p in parts for x in p]
+
     prev = []
     for number in range(2):
-        group = list(range(cuts[number], cuts[number + 1]))
-        parts = [arrived[order[i]] for i in group]
-        with_pos = number == 1
-        seen = tails if with_pos else tails[: cuts[1]]
+        keys, flat = place_args(work[number])
+        seen, tail_args, side = tails, prev, jax.ShapeDtypeStruct((n * cap, LANES), jnp.int32)
+        if number == 0:
+            seen, tail_args = tails[:cut], [w_query_key, w_value]
+            side = jax.ShapeDtypeStruct((width, 3 * local), BF16)
         got = pl.pallas_call(
             functools.partial(
-                place_kernel, names=group, parts=[len(p) for p in parts], cap=cap,
-                mp_steps=mp_steps, tails_count=len(seen), piece=piece, has_prev=bool(prev),
-                with_pos=with_pos,
+                place_kernel, cap=cap, mp_steps=mp_steps, tails_count=len(seen), piece=piece,
+                has_prev=number == 1, weights=number == 0, **keys,
             ),
-            out_shape=[jax.ShapeDtypeStruct((slots, width), BF16)]
-            + [jax.ShapeDtypeStruct((n * cap, LANES), jnp.int32)] * with_pos,
-            in_specs=[VM] * (len(seen) + sum(len(p) for p in parts) + len(prev)),
-            out_specs=[VM] * (1 + with_pos),
+            out_shape=[jax.ShapeDtypeStruct((slots, width), BF16), side],
+            in_specs=[VM] * (len(seen) + len(flat) + len(tail_args)),
+            out_specs=[VM, VM],
             compiler_params=PARAMS,
             name="place",
-        )(*seen, *[x for p in parts for x in p], *prev)
+        )(*seen, *flat, *tail_args)
+        if number == 0:
+            weight = got[1]
         prev = [got[0]]
     table, pos = got
-    flat = [x for k in late for x in arrived[k]]
+    keys, flat = place_args(work[2])
     qkv = pl.pallas_call(
         functools.partial(
-            project_kernel, names=[order.index(k) for k in late],
-            parts=[len(arrived[k]) for k in late], cap=cap, mp_steps=mp_steps, tails_count=n,
-            piece=piece, local=local, sub_size=sub_size, group=2,
+            project_kernel, cap=cap, mp_steps=mp_steps, tails_count=n, piece=piece,
+            sub_size=sub_size, group=2, **keys,
         ),
         out_shape=jax.ShapeDtypeStruct((slots, 3 * local), BF16),
-        in_specs=[VM] * (n + len(flat) + 3) + [SM],
+        in_specs=[VM] * (n + len(flat) + 2) + [SM],
         out_specs=VM,
-        scratch_shapes=[pltpu.VMEM((width, 3 * local), BF16), pltpu.VMEM((2 * WLEN, width), BF16)],
+        scratch_shapes=[pltpu.VMEM((2 * WLEN, width), BF16)],
         compiler_params=PARAMS,
         name="project",
-    )(*tails, *flat, table, w_query_key, w_value, window_counts)
+    )(*tails, *flat, table, weight, window_counts)
     att = pl.pallas_call(
         functools.partial(
             attend_kernel, pairs=list(range(local // LANES)), local=local, sub_size=sub_size,
@@ -494,7 +556,7 @@
     )(qkv, window_counts)
 
     answers = {}
-    for group in (far[:2], list(range(near)) + far[2:]):
+    for group in (far[:FIRST], list(range(near)) + far[FIRST:]):
         got = pl.pallas_call(
             functools.partial(fetch_kernel, names=[order.index(k) for k in group], cap=cap),
             out_shape=[jax.ShapeDtypeStruct((cap, local), BF16) for _ in group],
@@ -511,24 +573,25 @@
             home = lax.ppermute(home, OWN, steps.perm(k, True))
         returned[k] = [home] + [over_mp(home, t) for t in range(1, mp_size)]
 
-    block_rows = rows // 2
-    flat = [x for k in early for x in returned[k]]
+    pieces_back = [(k, t) for k in order for t in every]
+    soon = [x for x in pieces_back if x[0] not in order[-2:] or x[1] == 0]
+    last = [x for x in pieces_back if x not in soon]
     heads = pl.pallas_call(
         functools.partial(
-            unpack_kernel, names=early, cap=cap, parts=mp_size, local=local,
-            block_rows=block_rows,
+            unpack_kernel, items=soon, cap=cap, parts=mp_size, local=local,
+            block_rows=rows // 2,
         ),
         out_shape=jax.ShapeDtypeStruct((rows, mp_size * local), BF16),
-        in_specs=[VM] * (len(flat) + 1),
+        in_specs=[VM] * (len(soon) + 1),
         out_specs=VM,
         compiler_params=PARAMS,
         name="unpack",
-    )(*flat, dest_col)
-    flat = [x for k in late for x in returned[k]]
+    )(*[returned[k][t] for k, t in soon], dest_col)
+    flat = [returned[k][t] for k, t in last]
     return pl.pallas_call(
         functools.partial(
-            final_kernel, names=late, cap=cap, mp_steps=mp_steps, sub_size=sub_size, local=local,
-            block_rows=block_rows,
+            final_kernel, items=last, cap=cap, mp_steps=mp_steps, sub_size=sub_size, local=local,
+            block_rows=rows // FINAL_BLOCKS,
         ),
         out_shape=jax.ShapeDtypeStruct((rows, piece), BF16),
         in_specs=[VM] * (len(flat) + 7 + len(extra)),

time: 160 us -> 168 us (1.050)
  the two profiles are of different devices: /device:TPU:30 before, /device:TPU:4 now
where the time goes in v2:
time: 168 us
  waiting for transfers between devices  71.5 us (43%)
  starting transfers between devices  54.6 us (32%)
  Pallas kernels  33.7 us (20%)
  local copies, waits for them, and re-layouts  8.33 us (5%)
    ppermute x17, waiting for transfers between devices, over_mp(): return lax.ppermute(x, 'mp', mp_steps.perm(t))  37 us
    ppermute x7, starting transfers between devices, shards(): home = lax.ppermute(home, OWN, steps.perm(k, True))  23.4 us
    ppermute x6, waiting for transfers between devices, shards(): got = lax.ppermute(sent, OWN, steps.perm(k))  21.5 us
    ppermute x17, starting transfers between devices, over_mp(): return lax.ppermute(x, 'mp', mp_steps.perm(t))  17.7 us
    ppermute x7, waiting for transfers between devices, shards(): home = lax.ppermute(home, OWN, steps.perm(k, True))  12.9 us
    pallas_call x1, Pallas kernels, shards(): pl.pallas_call(functools.partial(final_kernel, items=last, cap=cap, mp_st...  10.3 us
    ppermute x6, starting transfers between devices, shards(): got = lax.ppermute(sent, OWN, steps.perm(k))  7.42 us
    pallas_call x2, Pallas kernels, shards(): pl.pallas_call(functools.partial(fetch_kernel, names=[order.index(k) for...  6.81 us
  transfers between devices with their start and end apart: 34, of which 16 were waited for; matrix products, arithmetic and copies ran while one was open for 1% of the time, Pallas kernels for 10%

profile of v2, /device:TPU:4, one launch (start us, length us, event | category | flops | bytes accessed | tf_op | source)
XLA Modules:
  0.0 168.2 jit_solution(80624805778173454)
XLA Ops:
  1.3 1.4 copy-done
  3.3 2.1 %pack.2 = (bf16[1536,512]{1,0:T(8,128)(2,1)S(1)}, bf16[400,256]{1,0:T(8,128)(2,1)}) custom-call(s32[1,1536]{1,0:T(1,128)S(1)} %get-tuple-element.32.dest_ref, f32[128,128]{1,0:T(8,128)S(1)} %get-tuple-element.33.cnt_ref, bf16[1536,512]{1,0:T(8,128)(2,1)S(1)} %copy-done, f32[1,512]{1,0:T(1,128)S(1)} %bitcast.2), custom_call_target="tpu_custom_call" | custom-call | tf_op jit(solution)/shard_map/pack/pallas_call | solution.py:442
  5.5 3.5 %pack.3 = (s32[1536,128]{1,0:T(8,128)S(1)}, bf16[400,256]{1,0:T(8,128)(2,1)}, bf16[400,256]{1,0:T(8,128)(2,1)S(1)}, bf16[400,256]{1,0:T(8,128)(2,1)S(1)}, bf16[4...) custom-call(s32[1,1536]{1,0:T(1,128)S(1)} %get-tuple-element.32.dest, ...), custom_call_target="tpu_custom_call" | custom-call | tf_op jit(solution)/shard_map/pack/pallas_call | solution.py:452
  11.0 1.6 collective-permute-start.2
  12.6 2.6 %collective-permute-start.1 = (bf16[400,256]{1,0:T(8,128)(2,1)}, bf16[400,256]{1,0:T(8,128)(2,1)S(1)}, u32[]{:S(2)}, u32[]{:S(2)}) collective-permute-start(bf16[400,256]{1,0:T(8,128)(2,1)} %get-tuple-element.37), channel_id=1, source_target_pairs={{0,8},{1,9},{4,12},{5,13},{8,0},{9,1},{12,4},{13,5},{2,10},{3,11},... | collective-permute-start | bytes 614408 | tf_op jit(solution)/shard_map/ppermute | solution.py:482
  15.2 0.8 constant_dynamic-slice_fusion.1
  16.0 1.7 %dynamic_slice.10 = bf16[512,256]{1,0:T(8,128)(2,1)} dynamic-slice(bf16[1024,512]{1,0:T(8,128)(2,1)} %refs_8_.1, s32[]{:T(128)S(6)} %select_n.10, s32[]{:T(128)S(6)} %select_n.11), dynamic_slice_sizes={512,256} | dynamic-slice | bytes 524292 | tf_op jit(solution)/shard_map/dynamic_slice | solution.py:471
  17.8 0.9 collective-permute-start
  18.7 1.0 collective-permute-start.3
  19.7 3.7 %collective-permute-done.2.refs_3_.refs_8_ = bf16[400,256]{1,0:T(8,128)(2,1)S(1)} collective-permute-done((bf16[400,256]{1,0:T(8,128)(2,1)}, bf16[400,256]{1,0:T(8,128)(2,1)S(1)}, u32[]{:S(2)}, u32[]{:S(2)}) %collective-permute-start.2) | collective-permute-done | bytes 204832 | tf_op jit(solution)/shard_map/ppermute | solution.py:482
  24.0 2.2 %collective-permute-start.6 = (bf16[400,256]{1,0:T(8,128)(2,1)}, bf16[400,256]{1,0:T(8,128)(2,1)S(1)}, u32[]{:S(2)}, u32[]{:S(2)}) collective-permute-start(bf16[400,256]{1,0:T(8,128)(2,1)} %copy-done.11), channel_id=1, source_target_pairs={{0,13},{1,12},{4,9},{5,8},{8,5},{9,4},{12,1},{13,0},{2,15},{3,14},... | collective-permute-start | bytes 614408 | tf_op jit(solution)/shard_map/ppermute | solution.py:482
  26.2 1.0 collective-permute-done.5.refs_6_.refs_12_
  27.2 1.5 collective-permute-start.12
  28.7 5.8 %collective-permute-done.3.refs_4_.refs_8_ = bf16[400,256]{1,0:T(8,128)(2,1)S(1)} collective-permute-done((bf16[400,256]{1,0:T(8,128)(2,1)}, bf16[400,256]{1,0:T(8,128)(2,1)S(1)}, u32[]{:S(2)}, u32[]{:S(2)}) %collective-permute-start.3) | collective-permute-done | bytes 204832 | tf_op jit(solution)/shard_map/ppermute | solution.py:482
  34.5 1.5 collective-permute-start.11
  36.0 10.5 %collective-permute-done.4.refs_5_.refs_10_ = bf16[400,256]{1,0:T(8,128)(2,1)S(1)} collective-permute-done((bf16[400,256]{1,0:T(8,128)(2,1)}, bf16[400,256]{1,0:T(8,128)(2,1)S(1)}, u32[]{:S(2)}, u32[]{:S(2)}) %collective-permute-start.4) | collective-permute-done | bytes 204832 | tf_op jit(solution)/shard_map/ppermute | solution.py:482
  46.5 1.5 collective-permute-start.28
  48.5 1.5 collective-permute-start.8
  50.6 1.5 collective-permute-start.7
  52.1 13.8 %collective-permute-done.10.refs_13_ = bf16[400,256]{1,0:T(8,128)(2,1)S(1)} collective-permute-done((bf16[400,256]{1,0:T(8,128)(2,1)S(1)}, bf16[400,256]{1,0:T(8,128)(2,1)S(1)}, u32[]{:S(2)}, u32[]{:S(2)}) %collective-permute-start.10) | collective-permute-done | bytes 204832 | tf_op jit(solution)/shard_map/ppermute | solution.py:422
  65.9 1.5 collective-permute-start.29
  67.4 2.9 %collective-permute-done.8.refs_9_ = bf16[400,256]{1,0:T(8,128)(2,1)S(1)} collective-permute-done((bf16[400,256]{1,0:T(8,128)(2,1)S(1)}, bf16[400,256]{1,0:T(8,128)(2,1)S(1)}, u32[]{:S(2)}, u32[]{:S(2)}) %collective-permute-start.8) | collective-permute-done | bytes 204832 | tf_op jit(solution)/shard_map/ppermute | solution.py:422
  70.3 1.5 collective-permute-start.30
  71.8 0.9 copy-done.6
  72.7 1.1 place.2
  74.7 1.4 place.3
  76.0 3.0 %collective-permute-done.7.refs_8_ = bf16[400,256]{1,0:T(8,128)(2,1)S(1)} collective-permute-done((bf16[400,256]{1,0:T(8,128)(2,1)S(1)}, bf16[400,256]{1,0:T(8,128)(2,1)S(1)}, u32[]{:S(2)}, u32[]{:S(2)}) %collective-permute-start.7) | collective-permute-done | bytes 204832 | tf_op jit(solution)/shard_map/ppermute | solution.py:422
  79.1 0.9 project.1.qkv_ref
  80.8 1.0 fetch.3
  81.8 3.3 %collective-permute-start.20 = (bf16[384,256]{1,0:T(8,128)(2,1)S(1)}, bf16[384,256]{1,0:T(8,128)(2,1)S(1)}, u32[]{:S(2)}, u32[]{:S(2)}) collective-permute-start(bf16[384,256]{1,0:T(8,128)(2,1)S(1)} %fetch.3), channel_id=1, source_target_pairs={{0,8},{1,9},{4,12},{5,13},{8,0},{9,1},{12,4},{13,5},{2,10},{3,11},... | collective-permute-start | bytes 589832 | tf_op jit(solution)/shard_map/ppermute | solution.py:573
  85.1 5.8 %fetch.2 = (bf16[384,256]{1,0:T(8,128)(2,1)S(1)}, bf16[384,256]{1,0:T(8,128)(2,1)S(1)}, bf16[384,256]{1,0:T(8,128)(2,1)S(1)}, bf16[384,256]{1,0:T(8,128)(2,1)S(1...) custom-call(bf16[4096,256]{1,0:T(8,128)(2,1)S(1)} %attend.1.att_ref, ...), custom_call_target="tpu_custom_call" | custom-call | tf_op jit(solution)/shard_map/fetch/pallas_call | solution.py:560
  90.9 8.3 %collective-permute-start.18 = (bf16[384,256]{1,0:T(8,128)(2,1)S(1)}, bf16[384,256]{1,0:T(8,128)(2,1)S(1)}, u32[]{:S(2)}, u32[]{:S(2)}) collective-permute-start(bf16[384,256]{1,0:T(8,128)(2,1)S(1)} %get-tuple-element.51), channel_id=1, source_target_pairs={{0,1},{1,0},{4,5},{5,4},{8,9},{9,8},{12,13},{13,12},{2,3},{3,2},{6... | collective-permute-start | bytes 589832 | tf_op jit(solution)/shard_map/ppermute | solution.py:573
  99.3 5.4 %collective-permute-start.22 = (bf16[384,256]{1,0:T(8,128)(2,1)S(1)}, bf16[384,256]{1,0:T(8,128)(2,1)S(1)}, u32[]{:S(2)}, u32[]{:S(2)}) collective-permute-start(bf16[384,256]{1,0:T(8,128)(2,1)S(1)} %get-tuple-element.52), channel_id=1, source_target_pairs={{0,4},{1,5},{4,0},{5,1},{8,12},{9,13},{12,8},{13,9},{2,6},{3,7},{6... | collective-permute-start | bytes 589832 | tf_op jit(solution)/shard_map/ppermute | solution.py:573
  104.7 2.4 %collective-permute-start.24 = (bf16[384,256]{1,0:T(8,128)(2,1)S(1)}, bf16[384,256]{1,0:T(8,128)(2,1)S(1)}, u32[]{:S(2)}, u32[]{:S(2)}) collective-permute-start(bf16[384,256]{1,0:T(8,128)(2,1)S(1)} %get-tuple-element.53), channel_id=1, source_target_pairs={{0,12},{1,13},{4,8},{5,9},{8,4},{9,5},{12,0},{13,1},{2,14},{3,15},... | collective-permute-start | bytes 589832 | tf_op jit(solution)/shard_map/ppermute | solution.py:573
  107.4 1.4 collective-permute-start.13
  108.8 2.2 %collective-permute-start.15 = (bf16[384,256]{1,0:T(8,128)(2,1)S(1)}, bf16[384,256]{1,0:T(8,128)(2,1)S(1)}, u32[]{:S(2)}, u32[]{:S(2)}) collective-permute-start(bf16[384,256]{1,0:T(8,128)(2,1)S(1)} %get-tuple-element.49), channel_id=1, source_target_pairs={{0,13},{1,12},{4,9},{5,8},{8,5},{9,4},{12,1},{13,0},{2,15},{3,14},... | collective-permute-start | bytes 589832 | tf_op jit(solution)/shard_map/ppermute | solution.py:573
  111.5 5.6 %collective-permute-done.24.refs_8_ = bf16[384,256]{1,0:T(8,128)(2,1)S(1)} collective-permute-done((bf16[384,256]{1,0:T(8,128)(2,1)S(1)}, bf16[384,256]{1,0:T(8,128)(2,1)S(1)}, u32[]{:S(2)}, u32[]{:S(2)}) %collective-permute-start.24) | collective-permute-done | bytes 196640 | tf_op jit(solution)/shard_map/ppermute | solution.py:573
  117.6 7.3 %collective-permute-done.26.refs_10_ = bf16[384,256]{1,0:T(8,128)(2,1)S(1)} collective-permute-done((bf16[384,256]{1,0:T(8,128)(2,1)S(1)}, bf16[384,256]{1,0:T(8,128)(2,1)S(1)}, u32[]{:S(2)}, u32[]{:S(2)}) %collective-permute-start.26) | collective-permute-done | bytes 196640 | tf_op jit(solution)/shard_map/ppermute | solution.py:573
  124.9 5.1 %collective-permute-start.31 = (bf16[512,512]{1,0:T(8,128)(2,1)S(1)}, bf16[512,512]{1,0:T(8,128)(2,1)S(1)}, u32[]{:S(2)}, u32[]{:S(2)}) collective-permute-start(bf16[512,512]{1,0:T(8,128)(2,1)S(1)} %collective-permute-done.28.refs_9_), channel_id=1, source_target_pairs={{1,0},{0,1},{3,2},{2,3},{5,4},{4,5},{7,6},{6,7},{9,8},{8,9},{11,10... | collective-permute-start | bytes 1572872 | tf_op jit(solution)/shard_map/ppermute | solution.py:491
  130.6 1.5 collective-permute-start.23
  132.6 1.5 collective-permute-start.27
  134.1 3.7 %collective-permute-done.19.refs_3_ = bf16[384,256]{1,0:T(8,128)(2,1)S(1)} collective-permute-done((bf16[384,256]{1,0:T(8,128)(2,1)S(1)}, bf16[384,256]{1,0:T(8,128)(2,1)S(1)}, u32[]{:S(2)}, u32[]{:S(2)}) %collective-permute-start.19) | collective-permute-done | bytes 196640 | tf_op jit(solution)/shard_map/ppermute | solution.py:422
  137.8 4.2 %collective-permute-done.23.refs_7_ = bf16[384,256]{1,0:T(8,128)(2,1)S(1)} collective-permute-done((bf16[384,256]{1,0:T(8,128)(2,1)S(1)}, bf16[384,256]{1,0:T(8,128)(2,1)S(1)}, u32[]{:S(2)}, u32[]{:S(2)}) %collective-permute-start.23) | collective-permute-done | bytes 196640 | tf_op jit(solution)/shard_map/ppermute | solution.py:422
  142.5 3.7 %collective-permute-done.25.refs_9_ = bf16[384,256]{1,0:T(8,128)(2,1)S(1)} collective-permute-done((bf16[384,256]{1,0:T(8,128)(2,1)S(1)}, bf16[384,256]{1,0:T(8,128)(2,1)S(1)}, u32[]{:S(2)}, u32[]{:S(2)}) %collective-permute-start.25) | collective-permute-done | bytes 196640 | tf_op jit(solution)/shard_map/ppermute | solution.py:422
  146.8 3.7 %collective-permute-done.27.refs_11_ = bf16[384,256]{1,0:T(8,128)(2,1)S(1)} collective-permute-done((bf16[384,256]{1,0:T(8,128)(2,1)S(1)}, bf16[384,256]{1,0:T(8,128)(2,1)S(1)}, u32[]{:S(2)}, u32[]{:S(2)}) %collective-permute-start.27) | collective-permute-done | bytes 196640 | tf_op jit(solution)/shard_map/ppermute | solution.py:422
  150.5 6.2 %unpack.1.refs_2_ = bf16[1536,512]{1,0:T(8,128)(2,1)S(1)} custom-call(bf16[384,256]{1,0:T(8,128)(2,1)S(1)} %get-tuple-element.50.refs_0_, bf16[384,256]{1,0:T(8,128)(2,1)S(1)} %collective-permute-done.17.refs_1_, bf16[384,256]{1,0:T(8,128)(2,1)S(1)} %collective-permute-done.18.refs_2_, bf16[384,256]{1,0:T(8,128)(2,1)S(1)} %collective-permute-done.19.refs_3_, ...), custom_call_target="tpu_custom_call" | custom-call | tf_op jit(solution)/shard_map/unpack/pallas_call | solution.py:579
  156.7 1.2 collective-permute-done.16.refs_1_
  157.9 10.3 %final.1 = bf16[1536,256]{1,0:T(8,128)(2,1)} custom-call(bf16[384,256]{1,0:T(8,128)(2,1)S(1)} %collective-permute-done.14.refs_0_, bf16[384,256]{1,0:T(8,128)(2,1)S(1)} %collective-permute-done.16.refs_1_, bf16[1536,512]{1,0:T(8,128)(2,1)S(1)} %unpack.1.refs_2_, s32[1536,128]{1,0:T(8,128)S(1)} %get-tuple-element.55.refs_14_.refs_3_, ...), custom_call_target="tpu_custom_call" | custom-call | tf_op jit(solution)/shard_map/final/pallas_call | solution.py:591
  (65 shorter events, 10.6 us)
Async XLA Ops:
  1.2 1.4 copy-start
  2.7 0.7 copy-start.7
  3.3 11.8 %copy-start.2 = (bf16[512,1024]{1,0:T(8,128)(2,1)S(1)}, bf16[512,1024]{1,0:T(8,128)(2,1)}, u32[]{:S(2)}) copy-start(bf16[512,1024]{1,0:T(8,128)(2,1)} %refs_7_.1) | copy-start | bytes 3145732
  3.3 14.4 %copy-start.4 = (bf16[256,512]{1,0:T(8,128)(2,1)S(1)}, bf16[256,512]{1,0:T(8,128)(2,1)}, u32[]{:S(2)}) copy-start(bf16[256,512]{1,0:T(8,128)(2,1)} %refs_6_.1) | copy-start | bytes 786436
  5.5 66.3 %copy-start.5 = (bf16[2,512,256]{2,1,0:T(8,128)(2,1)S(1)}, bf16[2,512,256]{2,1,0:T(8,128)(2,1)}, u32[]{:S(2)}) copy-start(bf16[2,512,256]{2,1,0:T(8,128)(2,1)} %refs_10_.1) | copy-start | bytes 1572868
  9.0 0.7 copy-start.11
  10.3 0.7 copy-start.14
  11.0 1.6 copy-start.10
  11.0 1.6 copy-start.12
  11.0 12.4 %collective-permute-start.2 = (bf16[400,256]{1,0:T(8,128)(2,1)}, bf16[400,256]{1,0:T(8,128)(2,1)S(1)}, u32[]{:S(2)}, u32[]{:S(2)}) collective-permute-start(bf16[400,256]{1,0:T(8,128)(2,1)} %get-tuple-element.38), channel_id=1, source_target_pairs={{0,4},{1,5},{4,0},{5,1},{8,12},{9,13},{12,8},{13,9},{2,6},{3,7},{6... | collective-permute-start | bytes 614408 | tf_op jit(solution)/shard_map/ppermute | solution.py:482
  12.6 11.4 %collective-permute-start.1 = (bf16[400,256]{1,0:T(8,128)(2,1)}, bf16[400,256]{1,0:T(8,128)(2,1)S(1)}, u32[]{:S(2)}, u32[]{:S(2)}) collective-permute-start(bf16[400,256]{1,0:T(8,128)(2,1)} %get-tuple-element.37), channel_id=1, source_target_pairs={{0,8},{1,9},{4,12},{5,13},{8,0},{9,1},{12,4},{13,5},{2,10},{3,11},... | collective-permute-start | bytes 614408 | tf_op jit(solution)/shard_map/ppermute | solution.py:482
  17.7 9.5 %collective-permute-start.5 = (bf16[400,256]{1,0:T(8,128)(2,1)}, bf16[400,256]{1,0:T(8,128)(2,1)S(1)}, u32[]{:S(2)}, u32[]{:S(2)}) collective-permute-start(bf16[400,256]{1,0:T(8,128)(2,1)} %copy-done.14), channel_id=1, source_target_pairs={{0,5},{1,4},{4,1},{5,0},{8,13},{9,12},{12,9},{13,8},{2,7},{3,6},{6... | collective-permute-start | bytes 614408 | tf_op jit(solution)/shard_map/ppermute | solution.py:482
  17.8 32.3 %collective-permute-start = (bf16[400,512]{1,0:T(8,128)(2,1)}, bf16[400,512]{1,0:T(8,128)(2,1)S(1)}, u32[]{:S(2)}, u32[]{:S(2)}) collective-permute-start(bf16[400,512]{1,0:T(8,128)(2,1)} %copy-done.10), channel_id=1, source_target_pairs={{0,1},{1,0},{4,5},{5,4},{8,9},{9,8},{12,13},{13,12},{2,3},{3,2},{6... | collective-permute-start | bytes 1228808 | tf_op jit(solution)/shard_map/ppermute | solution.py:477
  18.7 15.8 %collective-permute-start.3 = (bf16[400,256]{1,0:T(8,128)(2,1)}, bf16[400,256]{1,0:T(8,128)(2,1)S(1)}, u32[]{:S(2)}, u32[]{:S(2)}) collective-permute-start(bf16[400,256]{1,0:T(8,128)(2,1)} %copy-done.13), channel_id=1, source_target_pairs={{0,12},{1,13},{4,8},{5,9},{8,4},{9,5},{12,0},{13,1},{2,14},{3,15},... | collective-permute-start | bytes 614408 | tf_op jit(solution)/shard_map/ppermute | solution.py:482
  23.4 23.1 %collective-permute-start.4 = (bf16[400,256]{1,0:T(8,128)(2,1)}, bf16[400,256]{1,0:T(8,128)(2,1)S(1)}, u32[]{:S(2)}, u32[]{:S(2)}) collective-permute-start(bf16[400,256]{1,0:T(8,128)(2,1)} %copy-done.12), channel_id=1, source_target_pairs={{0,9},{1,8},{4,13},{5,12},{8,1},{9,0},{12,5},{13,4},{2,11},{3,10},... | collective-permute-start | bytes 614408 | tf_op jit(solution)/shard_map/ppermute | solution.py:482
  24.0 24.1 %collective-permute-start.6 = (bf16[400,256]{1,0:T(8,128)(2,1)}, bf16[400,256]{1,0:T(8,128)(2,1)S(1)}, u32[]{:S(2)}, u32[]{:S(2)}) collective-permute-start(bf16[400,256]{1,0:T(8,128)(2,1)} %copy-done.11), channel_id=1, source_target_pairs={{0,13},{1,12},{4,9},{5,8},{8,5},{9,4},{12,1},{13,0},{2,15},{3,14},... | collective-permute-start | bytes 614408 | tf_op jit(solution)/shard_map/ppermute | solution.py:482
  27.2 21.3 %collective-permute-start.12 = (bf16[400,256]{1,0:T(8,128)(2,1)S(1)}, bf16[400,256]{1,0:T(8,128)(2,1)S(1)}, u32[]{:S(2)}, u32[]{:S(2)}) collective-permute-start(bf16[400,256]{1,0:T(8,128)(2,1)S(1)} %collective-permute-done.2.refs_3_.refs_8_), channel_id=1, source_target_pairs={{0,2},{2,0},{1,3},{3,1},{4,6},{6,4},{5,7},{7,5},{8,10},{10,8},{9,1... | collective-permute-start | bytes 614408 | tf_op jit(solution)/shard_map/ppermute | solution.py:422
  34.5 16.1 %collective-permute-start.11 = (bf16[400,256]{1,0:T(8,128)(2,1)S(1)}, bf16[400,256]{1,0:T(8,128)(2,1)S(1)}, u32[]{:S(2)}, u32[]{:S(2)}) collective-permute-start(bf16[400,256]{1,0:T(8,128)(2,1)S(1)} %collective-permute-done.1.refs_2_.refs_6_), channel_id=1, source_target_pairs={{0,2},{2,0},{1,3},{3,1},{4,6},{6,4},{5,7},{7,5},{8,10},{10,8},{9,1... | collective-permute-start | bytes 614408 | tf_op jit(solution)/shard_map/ppermute | solution.py:422
  46.5 60.6 %collective-permute-start.28 = (bf16[512,512]{1,0:T(8,128)(2,1)}, bf16[512,512]{1,0:T(8,128)(2,1)S(1)}, u32[]{:S(2)}, u32[]{:S(2)}) collective-permute-start(bf16[512,512]{1,0:T(8,128)(2,1)} %constant_dynamic-slice_fusion.1), channel_id=1, source_target_pairs={{0,2},{2,0},{1,3},{3,1},{4,6},{6,4},{5,7},{7,5},{8,10},{10,8},{9,1... | collective-permute-start | bytes 1572872 | tf_op jit(solution)/shard_map/ppermute | solution.py:422
  48.0 17.9 %collective-permute-start.10 = (bf16[400,256]{1,0:T(8,128)(2,1)S(1)}, bf16[400,256]{1,0:T(8,128)(2,1)S(1)}, u32[]{:S(2)}, u32[]{:S(2)}) collective-permute-start(bf16[400,256]{1,0:T(8,128)(2,1)S(1)} %collective-permute-done.5.refs_6_.refs_12_), channel_id=1, source_target_pairs={{0,2},{2,0},{1,3},{3,1},{4,6},{6,4},{5,7},{7,5},{8,10},{10,8},{9,1... | collective-permute-start | bytes 614408 | tf_op jit(solution)/shard_map/ppermute | solution.py:422
  48.5 21.7 %collective-permute-start.8 = (bf16[400,256]{1,0:T(8,128)(2,1)S(1)}, bf16[400,256]{1,0:T(8,128)(2,1)S(1)}, u32[]{:S(2)}, u32[]{:S(2)}) collective-permute-start(bf16[400,256]{1,0:T(8,128)(2,1)S(1)} %collective-permute-done.3.refs_4_.refs_8_), channel_id=1, source_target_pairs={{0,2},{2,0},{1,3},{3,1},{4,6},{6,4},{5,7},{7,5},{8,10},{10,8},{9,1... | collective-permute-start | bytes 614408 | tf_op jit(solution)/shard_map/ppermute | solution.py:422
  50.0 24.6 %collective-permute-start.9 = (bf16[400,256]{1,0:T(8,128)(2,1)S(1)}, bf16[400,256]{1,0:T(8,128)(2,1)S(1)}, u32[]{:S(2)}, u32[]{:S(2)}) collective-permute-start(bf16[400,256]{1,0:T(8,128)(2,1)S(1)} %collective-permute-done.4.refs_5_.refs_10_), channel_id=1, source_target_pairs={{0,2},{2,0},{1,3},{3,1},{4,6},{6,4},{5,7},{7,5},{8,10},{10,8},{9,1... | collective-permute-start | bytes 614408 | tf_op jit(solution)/shard_map/ppermute | solution.py:422
  50.6 28.5 %collective-permute-start.7 = (bf16[400,256]{1,0:T(8,128)(2,1)S(1)}, bf16[400,256]{1,0:T(8,128)(2,1)S(1)}, u32[]{:S(2)}, u32[]{:S(2)}) collective-permute-start(bf16[400,256]{1,0:T(8,128)(2,1)S(1)} %collective-permute-done.6.refs_7_.refs_14_), channel_id=1, source_target_pairs={{0,2},{2,0},{1,3},{3,1},{4,6},{6,4},{5,7},{7,5},{8,10},{10,8},{9,1... | collective-permute-start | bytes 614408 | tf_op jit(solution)/shard_map/ppermute | solution.py:422
  65.9 38.8 %collective-permute-start.29 = (bf16[512,256]{1,0:T(8,128)(2,1)}, bf16[512,256]{1,0:T(8,128)(2,1)S(1)}, u32[]{:S(2)}, u32[]{:S(2)}) collective-permute-start(bf16[512,256]{1,0:T(8,128)(2,1)} %dynamic_slice.10), channel_id=1, source_target_pairs={{0,2},{2,0},{1,3},{3,1},{4,6},{6,4},{5,7},{7,5},{8,10},{10,8},{9,1... | collective-permute-start | bytes 786440 | tf_op jit(solution)/shard_map/ppermute | solution.py:422
  70.3 29.0 %collective-permute-start.30 = (bf16[128,512]{1,0:T(8,128)(2,1)S(1)}, bf16[128,512]{1,0:T(8,128)(2,1)S(1)}, u32[]{:S(2)}, u32[]{:S(2)}) collective-permute-start(bf16[128,512]{1,0:T(8,128)(2,1)S(1)} %constant_dynamic-slice_fusion), channel_id=1, source_target_pairs={{0,2},{2,0},{1,3},{3,1},{4,6},{6,4},{5,7},{7,5},{8,10},{10,8},{9,1... | collective-permute-start | bytes 393224 | tf_op jit(solution)/shard_map/ppermute | solution.py:422
  71.8 1.0 copy-start.6
  74.7 4.4 %copy-start.9 = (s32[128]{0:T(128)S(1)}, s32[128]{0:T(128)}, u32[]{:S(2)}) copy-start(s32[128]{0:T(128)} %counts_ref.1) | copy-start | bytes 1540
  81.8 25.7 %collective-permute-start.20 = (bf16[384,256]{1,0:T(8,128)(2,1)S(1)}, bf16[384,256]{1,0:T(8,128)(2,1)S(1)}, u32[]{:S(2)}, u32[]{:S(2)}) collective-permute-start(bf16[384,256]{1,0:T(8,128)(2,1)S(1)} %fetch.3), channel_id=1, source_target_pairs={{0,8},{1,9},{4,12},{5,13},{8,0},{9,1},{12,4},{13,5},{2,10},{3,11},... | collective-permute-start | bytes 589832 | tf_op jit(solution)/shard_map/ppermute | solution.py:573
  90.9 17.9 %collective-permute-start.18 = (bf16[384,256]{1,0:T(8,128)(2,1)S(1)}, bf16[384,256]{1,0:T(8,128)(2,1)S(1)}, u32[]{:S(2)}, u32[]{:S(2)}) collective-permute-start(bf16[384,256]{1,0:T(8,128)(2,1)S(1)} %get-tuple-element.51), channel_id=1, source_target_pairs={{0,1},{1,0},{4,5},{5,4},{8,9},{9,8},{12,13},{13,12},{2,3},{3,2},{6... | collective-permute-start | bytes 589832 | tf_op jit(solution)/shard_map/ppermute | solution.py:573
  99.3 11.7 %collective-permute-start.22 = (bf16[384,256]{1,0:T(8,128)(2,1)S(1)}, bf16[384,256]{1,0:T(8,128)(2,1)S(1)}, u32[]{:S(2)}, u32[]{:S(2)}) collective-permute-start(bf16[384,256]{1,0:T(8,128)(2,1)S(1)} %get-tuple-element.52), channel_id=1, source_target_pairs={{0,4},{1,5},{4,0},{5,1},{8,12},{9,13},{12,8},{13,9},{2,6},{3,7},{6... | collective-permute-start | bytes 589832 | tf_op jit(solution)/shard_map/ppermute | solution.py:573
  104.7 12.4 %collective-permute-start.24 = (bf16[384,256]{1,0:T(8,128)(2,1)S(1)}, bf16[384,256]{1,0:T(8,128)(2,1)S(1)}, u32[]{:S(2)}, u32[]{:S(2)}) collective-permute-start(bf16[384,256]{1,0:T(8,128)(2,1)S(1)} %get-tuple-element.53), channel_id=1, source_target_pairs={{0,12},{1,13},{4,8},{5,9},{8,4},{9,5},{12,0},{13,1},{2,14},{3,15},... | collective-permute-start | bytes 589832 | tf_op jit(solution)/shard_map/ppermute | solution.py:573
  107.1 17.8 %collective-permute-start.26 = (bf16[384,256]{1,0:T(8,128)(2,1)S(1)}, bf16[384,256]{1,0:T(8,128)(2,1)S(1)}, u32[]{:S(2)}, u32[]{:S(2)}) collective-permute-start(bf16[384,256]{1,0:T(8,128)(2,1)S(1)} %get-tuple-element.54), channel_id=1, source_target_pairs={{0,9},{1,8},{4,13},{5,12},{8,1},{9,0},{12,5},{13,4},{2,11},{3,10},... | collective-permute-start | bytes 589832 | tf_op jit(solution)/shard_map/ppermute | solution.py:573
  107.4 22.6 %collective-permute-start.13 = (bf16[384,256]{1,0:T(8,128)(2,1)S(1)}, bf16[384,256]{1,0:T(8,128)(2,1)S(1)}, u32[]{:S(2)}, u32[]{:S(2)}) collective-permute-start(bf16[384,256]{1,0:T(8,128)(2,1)S(1)} %get-tuple-element.48), channel_id=1, source_target_pairs={{0,5},{1,4},{4,1},{5,0},{8,13},{9,12},{12,9},{13,8},{2,7},{3,6},{6... | collective-permute-start | bytes 589832 | tf_op jit(solution)/shard_map/ppermute | solution.py:573
  108.8 21.7 %collective-permute-start.15 = (bf16[384,256]{1,0:T(8,128)(2,1)S(1)}, bf16[384,256]{1,0:T(8,128)(2,1)S(1)}, u32[]{:S(2)}, u32[]{:S(2)}) collective-permute-start(bf16[384,256]{1,0:T(8,128)(2,1)S(1)} %get-tuple-element.49), channel_id=1, source_target_pairs={{0,13},{1,12},{4,9},{5,8},{8,5},{9,4},{12,1},{13,0},{2,15},{3,14},... | collective-permute-start | bytes 589832 | tf_op jit(solution)/shard_map/ppermute | solution.py:573
  111.0 21.1 %collective-permute-start.17 = (bf16[384,256]{1,0:T(8,128)(2,1)S(1)}, bf16[384,256]{1,0:T(8,128)(2,1)S(1)}, u32[]{:S(2)}, u32[]{:S(2)}) collective-permute-start(bf16[384,256]{1,0:T(8,128)(2,1)S(1)} %get-tuple-element.50.refs_0_), channel_id=1, source_target_pairs={{0,2},{2,0},{1,3},{3,1},{4,6},{6,4},{5,7},{7,5},{8,10},{10,8},{9,1... | collective-permute-start | bytes 589832 | tf_op jit(solution)/shard_map/ppermute | solution.py:422
  117.1 15.5 %collective-permute-start.21 = (bf16[384,256]{1,0:T(8,128)(2,1)S(1)}, bf16[384,256]{1,0:T(8,128)(2,1)S(1)}, u32[]{:S(2)}, u32[]{:S(2)}) collective-permute-start(bf16[384,256]{1,0:T(8,128)(2,1)S(1)} %collective-permute-done.20.refs_4_), channel_id=1, source_target_pairs={{0,2},{2,0},{1,3},{3,1},{4,6},{6,4},{5,7},{7,5},{8,10},{10,8},{9,1... | collective-permute-start | bytes 589832 | tf_op jit(solution)/shard_map/ppermute | solution.py:422
  124.9 33.0 %collective-permute-start.31 = (bf16[512,512]{1,0:T(8,128)(2,1)S(1)}, bf16[512,512]{1,0:T(8,128)(2,1)S(1)}, u32[]{:S(2)}, u32[]{:S(2)}) collective-permute-start(bf16[512,512]{1,0:T(8,128)(2,1)S(1)} %collective-permute-done.28.refs_9_), channel_id=1, source_target_pairs={{1,0},{0,1},{3,2},{2,3},{5,4},{4,5},{7,6},{6,7},{9,8},{8,9},{11,10... | collective-permute-start | bytes 1572872 | tf_op jit(solution)/shard_map/ppermute | solution.py:491
  130.0 7.8 %collective-permute-start.19 = (bf16[384,256]{1,0:T(8,128)(2,1)S(1)}, bf16[384,256]{1,0:T(8,128)(2,1)S(1)}, u32[]{:S(2)}, u32[]{:S(2)}) collective-permute-start(bf16[384,256]{1,0:T(8,128)(2,1)S(1)} %collective-permute-done.18.refs_2_), channel_id=1, source_target_pairs={{0,2},{2,0},{1,3},{3,1},{4,6},{6,4},{5,7},{7,5},{8,10},{10,8},{9,1... | collective-permute-start | bytes 589832 | tf_op jit(solution)/shard_map/ppermute | solution.py:422
  130.6 11.5 %collective-permute-start.23 = (bf16[384,256]{1,0:T(8,128)(2,1)S(1)}, bf16[384,256]{1,0:T(8,128)(2,1)S(1)}, u32[]{:S(2)}, u32[]{:S(2)}) collective-permute-start(bf16[384,256]{1,0:T(8,128)(2,1)S(1)} %collective-permute-done.22.refs_6_), channel_id=1, source_target_pairs={{0,2},{2,0},{1,3},{3,1},{4,6},{6,4},{5,7},{7,5},{8,10},{10,8},{9,1... | collective-permute-start | bytes 589832 | tf_op jit(solution)/shard_map/ppermute | solution.py:422
  132.1 14.2 %collective-permute-start.25 = (bf16[384,256]{1,0:T(8,128)(2,1)S(1)}, bf16[384,256]{1,0:T(8,128)(2,1)S(1)}, u32[]{:S(2)}, u32[]{:S(2)}) collective-permute-start(bf16[384,256]{1,0:T(8,128)(2,1)S(1)} %collective-permute-done.24.refs_8_), channel_id=1, source_target_pairs={{0,2},{2,0},{1,3},{3,1},{4,6},{6,4},{5,7},{7,5},{8,10},{10,8},{9,1... | collective-permute-start | bytes 589832 | tf_op jit(solution)/shard_map/ppermute | solution.py:422
  132.6 17.9 %collective-permute-start.27 = (bf16[384,256]{1,0:T(8,128)(2,1)S(1)}, bf16[384,256]{1,0:T(8,128)(2,1)S(1)}, u32[]{:S(2)}, u32[]{:S(2)}) collective-permute-start(bf16[384,256]{1,0:T(8,128)(2,1)S(1)} %collective-permute-done.26.refs_10_), channel_id=1, source_target_pairs={{0,2},{2,0},{1,3},{3,1},{4,6},{6,4},{5,7},{7,5},{8,10},{10,8},{9,1... | collective-permute-start | bytes 589832 | tf_op jit(solution)/shard_map/ppermute | solution.py:422
  137.8 18.9 %collective-permute-start.32 = (bf16[512,256]{1,0:T(8,128)(2,1)S(1)}, bf16[512,256]{1,0:T(8,128)(2,1)S(1)}, u32[]{:S(2)}, u32[]{:S(2)}) collective-permute-start(bf16[512,256]{1,0:T(8,128)(2,1)S(1)} %collective-permute-done.29.refs_10_), channel_id=1, source_target_pairs={{1,0},{0,1},{3,2},{2,3},{5,4},{4,5},{7,6},{6,7},{9,8},{8,9},{11,10... | collective-permute-start | bytes 786440 | tf_op jit(solution)/shard_map/ppermute | solution.py:491
  142.0 14.7 %collective-permute-start.14 = (bf16[384,256]{1,0:T(8,128)(2,1)S(1)}, bf16[384,256]{1,0:T(8,128)(2,1)S(1)}, u32[]{:S(2)}, u32[]{:S(2)}) collective-permute-start(bf16[384,256]{1,0:T(8,128)(2,1)S(1)} %collective-permute-done.13.refs_12_), channel_id=1, source_target_pairs={{0,2},{2,0},{1,3},{3,1},{4,6},{6,4},{5,7},{7,5},{8,10},{10,8},{9,1... | collective-permute-start | bytes 589832 | tf_op jit(solution)/shard_map/ppermute | solution.py:422
  146.2 11.7 %collective-permute-start.16 = (bf16[384,256]{1,0:T(8,128)(2,1)S(1)}, bf16[384,256]{1,0:T(8,128)(2,1)S(1)}, u32[]{:S(2)}, u32[]{:S(2)}) collective-permute-start(bf16[384,256]{1,0:T(8,128)(2,1)S(1)} %collective-permute-done.15.refs_13_), channel_id=1, source_target_pairs={{0,2},{2,0},{1,3},{3,1},{4,6},{6,4},{5,7},{7,5},{8,10},{10,8},{9,1... | collective-permute-start | bytes 589832 | tf_op jit(solution)/shard_map/ppermute | solution.py:422
  150.5 6.2 %collective-permute-start.33 = (bf16[128,512]{1,0:T(8,128)(2,1)S(1)}, bf16[128,512]{1,0:T(8,128)(2,1)S(1)}, u32[]{:S(2)}, u32[]{:S(2)}) collective-permute-start(bf16[128,512]{1,0:T(8,128)(2,1)S(1)} %collective-permute-done.30.refs_11_), channel_id=1, source_target_pairs={{1,0},{0,1},{3,2},{2,3},{5,4},{4,5},{7,6},{6,7},{9,8},{8,9},{11,10... | collective-permute-start | bytes 393224 | tf_op jit(solution)/shard_map/ppermute | solution.py:491
  150.5 7.5 %copy-start.1 = (bf16[1536,512]{1,0:T(8,128)(2,1)S(1)}, bf16[1536,512]{1,0:T(8,128)(2,1)}, u32[]{:S(2)}) copy-start(bf16[1536,512]{1,0:T(8,128)(2,1)} %refs_4_.1) | copy-start | bytes 4718596
  150.5 7.5 %copy-start.3 = (bf16[1024,512]{1,0:T(8,128)(2,1)S(1)}, bf16[1024,512]{1,0:T(8,128)(2,1)}, u32[]{:S(2)}) copy-start(bf16[1024,512]{1,0:T(8,128)(2,1)} %refs_8_.1) | copy-start | bytes 3145732
  150.5 7.5 %copy-start.8 = (f32[512]{0:T(512)S(1)}, f32[512]{0:T(512)}, u32[]{:S(2)}) copy-start(f32[512]{0:T(512)} %param.18) | copy-start | bytes 6148
  (1 other events, 0.7 us)

commit v3 on v2

--- a/solution.py
+++ b/solution.py
@@ -24,6 +24,7 @@
 VM = pl.BlockSpec(memory_space=pltpu.VMEM)
 SM = pl.BlockSpec(memory_space=pltpu.SMEM)
 PARAMS = pltpu.CompilerParams(vmem_limit_bytes=20 * 1024 * 1024)
+PACKED = pltpu.CompilerParams(vmem_limit_bytes=20 * 1024 * 1024)
 
 
 class Steps:
@@ -551,7 +552,7 @@
         out_shape=jax.ShapeDtypeStruct((slots, local), BF16),
         in_specs=[VM, SM],
         out_specs=VM,
-        compiler_params=PARAMS,
+        compiler_params=PACKED,
         name="attend",
     )(qkv, window_counts)
 
@@ -597,7 +598,7 @@
         in_specs=[VM] * (len(flat) + 7 + len(extra)),
         out_specs=VM,
         scratch_shapes=[pltpu.VMEM((mp_size * local, width), BF16)],
-        compiler_params=PARAMS,
+        compiler_params=PACKED,
         name="final",
     )(*flat, heads, dest_col, voxels, ffn_gain.reshape(1, width), w_out, w_up, w_down, *extra)
 

time: 168 us -> 168 us (level)
  no operation moved by 1% of the time
where the time goes in v3:
time: 168 us
  waiting for transfers between devices  71.5 us (43%)
  starting transfers between devices  54.6 us (32%)
  Pallas kernels  33.7 us (20%)
  local copies, waits for them, and re-layouts  8.33 us (5%)
    ppermute x17, waiting for transfers between devices, over_mp(): return lax.ppermute(x, 'mp', mp_steps.perm(t))  37 us
    ppermute x7, starting transfers between devices, shards(): home = lax.ppermute(home, OWN, steps.perm(k, True))  23.4 us
    ppermute x6, waiting for transfers between devices, shards(): got = lax.ppermute(sent, OWN, steps.perm(k))  21.5 us
    ppermute x17, starting transfers between devices, over_mp(): return lax.ppermute(x, 'mp', mp_steps.perm(t))  17.7 us
    ppermute x7, waiting for transfers between devices, shards(): home = lax.ppermute(home, OWN, steps.perm(k, True))  12.9 us
    pallas_call x1, Pallas kernels, shards(): pl.pallas_call(functools.partial(final_kernel, items=last, cap=cap, mp_st...  10.3 us
    ppermute x6, starting transfers between devices, shards(): got = lax.ppermute(sent, OWN, steps.perm(k))  7.42 us
    pallas_call x2, Pallas kernels, shards(): pl.pallas_call(functools.partial(fetch_kernel, names=[order.index(k) for...  6.81 us
  transfers between devices with their start and end apart: 34, of which 16 were waited for; matrix products, arithmetic and copies ran while one was open for 1% of the time, Pallas kernels for 10%

profile of v3, /device:TPU:4, one launch (start us, length us, event | category | flops | bytes accessed | tf_op | source)
XLA Modules:
  0.0 168.2 jit_solution(80624805778173454)
XLA Ops:
  1.3 1.4 copy-done
  3.3 2.1 %pack.2 = (bf16[1536,512]{1,0:T(8,128)(2,1)S(1)}, bf16[400,256]{1,0:T(8,128)(2,1)}) custom-call(s32[1,1536]{1,0:T(1,128)S(1)} %get-tuple-element.32.dest_ref, f32[128,128]{1,0:T(8,128)S(1)} %get-tuple-element.33.cnt_ref, bf16[1536,512]{1,0:T(8,128)(2,1)S(1)} %copy-done, f32[1,512]{1,0:T(1,128)S(1)} %bitcast.2), custom_call_target="tpu_custom_call" | custom-call | tf_op jit(solution)/shard_map/pack/pallas_call | solution.py:443
  5.5 3.5 %pack.3 = (s32[1536,128]{1,0:T(8,128)S(1)}, bf16[400,256]{1,0:T(8,128)(2,1)}, bf16[400,256]{1,0:T(8,128)(2,1)S(1)}, bf16[400,256]{1,0:T(8,128)(2,1)S(1)}, bf16[4...) custom-call(s32[1,1536]{1,0:T(1,128)S(1)} %get-tuple-element.32.dest, ...), custom_call_target="tpu_custom_call" | custom-call | tf_op jit(solution)/shard_map/pack/pallas_call | solution.py:453
  11.0 1.6 collective-permute-start.2
  12.6 2.6 %collective-permute-start.1 = (bf16[400,256]{1,0:T(8,128)(2,1)}, bf16[400,256]{1,0:T(8,128)(2,1)S(1)}, u32[]{:S(2)}, u32[]{:S(2)}) collective-permute-start(bf16[400,256]{1,0:T(8,128)(2,1)} %get-tuple-element.37), channel_id=1, source_target_pairs={{0,8},{1,9},{4,12},{5,13},{8,0},{9,1},{12,4},{13,5},{2,10},{3,11},... | collective-permute-start | bytes 614408 | tf_op jit(solution)/shard_map/ppermute | solution.py:483
  15.2 0.8 constant_dynamic-slice_fusion.1
  16.0 1.7 %dynamic_slice.10 = bf16[512,256]{1,0:T(8,128)(2,1)} dynamic-slice(bf16[1024,512]{1,0:T(8,128)(2,1)} %refs_8_.1, s32[]{:T(128)S(6)} %select_n.10, s32[]{:T(128)S(6)} %select_n.11), dynamic_slice_sizes={512,256} | dynamic-slice | bytes 524292 | tf_op jit(solution)/shard_map/dynamic_slice | solution.py:472
  17.8 0.9 collective-permute-start
  18.7 1.0 collective-permute-start.3
  19.7 3.7 %collective-permute-done.2.refs_3_.refs_8_ = bf16[400,256]{1,0:T(8,128)(2,1)S(1)} collective-permute-done((bf16[400,256]{1,0:T(8,128)(2,1)}, bf16[400,256]{1,0:T(8,128)(2,1)S(1)}, u32[]{:S(2)}, u32[]{:S(2)}) %collective-permute-start.2) | collective-permute-done | bytes 204832 | tf_op jit(solution)/shard_map/ppermute | solution.py:483
  24.0 2.2 %collective-permute-start.6 = (bf16[400,256]{1,0:T(8,128)(2,1)}, bf16[400,256]{1,0:T(8,128)(2,1)S(1)}, u32[]{:S(2)}, u32[]{:S(2)}) collective-permute-start(bf16[400,256]{1,0:T(8,128)(2,1)} %copy-done.11), channel_id=1, source_target_pairs={{0,13},{1,12},{4,9},{5,8},{8,5},{9,4},{12,1},{13,0},{2,15},{3,14},... | collective-permute-start | bytes 614408 | tf_op jit(solution)/shard_map/ppermute | solution.py:483
  26.2 1.0 collective-permute-done.5.refs_6_.refs_12_
  27.2 1.5 collective-permute-start.12
  28.7 5.8 %collective-permute-done.3.refs_4_.refs_8_ = bf16[400,256]{1,0:T(8,128)(2,1)S(1)} collective-permute-done((bf16[400,256]{1,0:T(8,128)(2,1)}, bf16[400,256]{1,0:T(8,128)(2,1)S(1)}, u32[]{:S(2)}, u32[]{:S(2)}) %collective-permute-start.3) | collective-permute-done | bytes 204832 | tf_op jit(solution)/shard_map/ppermute | solution.py:483
  34.5 1.5 collective-permute-start.11
  36.0 10.5 %collective-permute-done.4.refs_5_.refs_10_ = bf16[400,256]{1,0:T(8,128)(2,1)S(1)} collective-permute-done((bf16[400,256]{1,0:T(8,128)(2,1)}, bf16[400,256]{1,0:T(8,128)(2,1)S(1)}, u32[]{:S(2)}, u32[]{:S(2)}) %collective-permute-start.4) | collective-permute-done | bytes 204832 | tf_op jit(solution)/shard_map/ppermute | solution.py:483
  46.5 1.5 collective-permute-start.28
  48.5 1.5 collective-permute-start.8
  50.6 1.5 collective-permute-start.7
  52.1 13.8 %collective-permute-done.10.refs_13_ = bf16[400,256]{1,0:T(8,128)(2,1)S(1)} collective-permute-done((bf16[400,256]{1,0:T(8,128)(2,1)S(1)}, bf16[400,256]{1,0:T(8,128)(2,1)S(1)}, u32[]{:S(2)}, u32[]{:S(2)}) %collective-permute-start.10) | collective-permute-done | bytes 204832 | tf_op jit(solution)/shard_map/ppermute | solution.py:423
  65.9 1.5 collective-permute-start.29
  67.4 2.9 %collective-permute-done.8.refs_9_ = bf16[400,256]{1,0:T(8,128)(2,1)S(1)} collective-permute-done((bf16[400,256]{1,0:T(8,128)(2,1)S(1)}, bf16[400,256]{1,0:T(8,128)(2,1)S(1)}, u32[]{:S(2)}, u32[]{:S(2)}) %collective-permute-start.8) | collective-permute-done | bytes 204832 | tf_op jit(solution)/shard_map/ppermute | solution.py:423
  70.3 1.5 collective-permute-start.30
  71.8 0.9 copy-done.6
  72.7 1.1 place.2
  74.7 1.4 place.3
  76.0 3.0 %collective-permute-done.7.refs_8_ = bf16[400,256]{1,0:T(8,128)(2,1)S(1)} collective-permute-done((bf16[400,256]{1,0:T(8,128)(2,1)S(1)}, bf16[400,256]{1,0:T(8,128)(2,1)S(1)}, u32[]{:S(2)}, u32[]{:S(2)}) %collective-permute-start.7) | collective-permute-done | bytes 204832 | tf_op jit(solution)/shard_map/ppermute | solution.py:423
  79.1 0.9 project.1.qkv_ref
  80.8 1.0 fetch.3
  81.8 3.3 %collective-permute-start.20 = (bf16[384,256]{1,0:T(8,128)(2,1)S(1)}, bf16[384,256]{1,0:T(8,128)(2,1)S(1)}, u32[]{:S(2)}, u32[]{:S(2)}) collective-permute-start(bf16[384,256]{1,0:T(8,128)(2,1)S(1)} %fetch.3), channel_id=1, source_target_pairs={{0,8},{1,9},{4,12},{5,13},{8,0},{9,1},{12,4},{13,5},{2,10},{3,11},... | collective-permute-start | bytes 589832 | tf_op jit(solution)/shard_map/ppermute | solution.py:574
  85.1 5.8 %fetch.2 = (bf16[384,256]{1,0:T(8,128)(2,1)S(1)}, bf16[384,256]{1,0:T(8,128)(2,1)S(1)}, bf16[384,256]{1,0:T(8,128)(2,1)S(1)}, bf16[384,256]{1,0:T(8,128)(2,1)S(1...) custom-call(bf16[4096,256]{1,0:T(8,128)(2,1)S(1)} %attend.1.att_ref, ...), custom_call_target="tpu_custom_call" | custom-call | tf_op jit(solution)/shard_map/fetch/pallas_call | solution.py:561
  90.9 8.3 %collective-permute-start.18 = (bf16[384,256]{1,0:T(8,128)(2,1)S(1)}, bf16[384,256]{1,0:T(8,128)(2,1)S(1)}, u32[]{:S(2)}, u32[]{:S(2)}) collective-permute-start(bf16[384,256]{1,0:T(8,128)(2,1)S(1)} %get-tuple-element.51), channel_id=1, source_target_pairs={{0,1},{1,0},{4,5},{5,4},{8,9},{9,8},{12,13},{13,12},{2,3},{3,2},{6... | collective-permute-start | bytes 589832 | tf_op jit(solution)/shard_map/ppermute | solution.py:574
  99.3 5.4 %collective-permute-start.22 = (bf16[384,256]{1,0:T(8,128)(2,1)S(1)}, bf16[384,256]{1,0:T(8,128)(2,1)S(1)}, u32[]{:S(2)}, u32[]{:S(2)}) collective-permute-start(bf16[384,256]{1,0:T(8,128)(2,1)S(1)} %get-tuple-element.52), channel_id=1, source_target_pairs={{0,4},{1,5},{4,0},{5,1},{8,12},{9,13},{12,8},{13,9},{2,6},{3,7},{6... | collective-permute-start | bytes 589832 | tf_op jit(solution)/shard_map/ppermute | solution.py:574
  104.7 2.4 %collective-permute-start.24 = (bf16[384,256]{1,0:T(8,128)(2,1)S(1)}, bf16[384,256]{1,0:T(8,128)(2,1)S(1)}, u32[]{:S(2)}, u32[]{:S(2)}) collective-permute-start(bf16[384,256]{1,0:T(8,128)(2,1)S(1)} %get-tuple-element.53), channel_id=1, source_target_pairs={{0,12},{1,13},{4,8},{5,9},{8,4},{9,5},{12,0},{13,1},{2,14},{3,15},... | collective-permute-start | bytes 589832 | tf_op jit(solution)/shard_map/ppermute | solution.py:574
  107.4 1.4 collective-permute-start.13
  108.8 2.2 %collective-permute-start.15 = (bf16[384,256]{1,0:T(8,128)(2,1)S(1)}, bf16[384,256]{1,0:T(8,128)(2,1)S(1)}, u32[]{:S(2)}, u32[]{:S(2)}) collective-permute-start(bf16[384,256]{1,0:T(8,128)(2,1)S(1)} %get-tuple-element.49), channel_id=1, source_target_pairs={{0,13},{1,12},{4,9},{5,8},{8,5},{9,4},{12,1},{13,0},{2,15},{3,14},... | collective-permute-start | bytes 589832 | tf_op jit(solution)/shard_map/ppermute | solution.py:574
  111.5 5.6 %collective-permute-done.24.refs_8_ = bf16[384,256]{1,0:T(8,128)(2,1)S(1)} collective-permute-done((bf16[384,256]{1,0:T(8,128)(2,1)S(1)}, bf16[384,256]{1,0:T(8,128)(2,1)S(1)}, u32[]{:S(2)}, u32[]{:S(2)}) %collective-permute-start.24) | collective-permute-done | bytes 196640 | tf_op jit(solution)/shard_map/ppermute | solution.py:574
  117.6 7.3 %collective-permute-done.26.refs_10_ = bf16[384,256]{1,0:T(8,128)(2,1)S(1)} collective-permute-done((bf16[384,256]{1,0:T(8,128)(2,1)S(1)}, bf16[384,256]{1,0:T(8,128)(2,1)S(1)}, u32[]{:S(2)}, u32[]{:S(2)}) %collective-permute-start.26) | collective-permute-done | bytes 196640 | tf_op jit(solution)/shard_map/ppermute | solution.py:574
  124.9 5.1 %collective-permute-start.31 = (bf16[512,512]{1,0:T(8,128)(2,1)S(1)}, bf16[512,512]{1,0:T(8,128)(2,1)S(1)}, u32[]{:S(2)}, u32[]{:S(2)}) collective-permute-start(bf16[512,512]{1,0:T(8,128)(2,1)S(1)} %collective-permute-done.28.refs_9_), channel_id=1, source_target_pairs={{1,0},{0,1},{3,2},{2,3},{5,4},{4,5},{7,6},{6,7},{9,8},{8,9},{11,10... | collective-permute-start | bytes 1572872 | tf_op jit(solution)/shard_map/ppermute | solution.py:492
  130.6 1.5 collective-permute-start.23
  132.6 1.5 collective-permute-start.27
  134.1 3.7 %collective-permute-done.19.refs_3_ = bf16[384,256]{1,0:T(8,128)(2,1)S(1)} collective-permute-done((bf16[384,256]{1,0:T(8,128)(2,1)S(1)}, bf16[384,256]{1,0:T(8,128)(2,1)S(1)}, u32[]{:S(2)}, u32[]{:S(2)}) %collective-permute-start.19) | collective-permute-done | bytes 196640 | tf_op jit(solution)/shard_map/ppermute | solution.py:423
  137.8 4.2 %collective-permute-done.23.refs_7_ = bf16[384,256]{1,0:T(8,128)(2,1)S(1)} collective-permute-done((bf16[384,256]{1,0:T(8,128)(2,1)S(1)}, bf16[384,256]{1,0:T(8,128)(2,1)S(1)}, u32[]{:S(2)}, u32[]{:S(2)}) %collective-permute-start.23) | collective-permute-done | bytes 196640 | tf_op jit(solution)/shard_map/ppermute | solution.py:423
  142.5 3.7 %collective-permute-done.25.refs_9_ = bf16[384,256]{1,0:T(8,128)(2,1)S(1)} collective-permute-done((bf16[384,256]{1,0:T(8,128)(2,1)S(1)}, bf16[384,256]{1,0:T(8,128)(2,1)S(1)}, u32[]{:S(2)}, u32[]{:S(2)}) %collective-permute-start.25) | collective-permute-done | bytes 196640 | tf_op jit(solution)/shard_map/ppermute | solution.py:423
  146.8 3.7 %collective-permute-done.27.refs_11_ = bf16[384,256]{1,0:T(8,128)(2,1)S(1)} collective-permute-done((bf16[384,256]{1,0:T(8,128)(2,1)S(1)}, bf16[384,256]{1,0:T(8,128)(2,1)S(1)}, u32[]{:S(2)}, u32[]{:S(2)}) %collective-permute-start.27) | collective-permute-done | bytes 196640 | tf_op jit(solution)/shard_map/ppermute | solution.py:423
  150.5 6.2 %unpack.1.refs_2_ = bf16[1536,512]{1,0:T(8,128)(2,1)S(1)} custom-call(bf16[384,256]{1,0:T(8,128)(2,1)S(1)} %get-tuple-element.50.refs_0_, bf16[384,256]{1,0:T(8,128)(2,1)S(1)} %collective-permute-done.17.refs_1_, bf16[384,256]{1,0:T(8,128)(2,1)S(1)} %collective-permute-done.18.refs_2_, bf16[384,256]{1,0:T(8,128)(2,1)S(1)} %collective-permute-done.19.refs_3_, ...), custom_call_target="tpu_custom_call" | custom-call | tf_op jit(solution)/shard_map/unpack/pallas_call | solution.py:580
  156.7 1.2 collective-permute-done.16.refs_1_
  157.9 10.3 %final.1 = bf16[1536,256]{1,0:T(8,128)(2,1)} custom-call(bf16[384,256]{1,0:T(8,128)(2,1)S(1)} %collective-permute-done.14.refs_0_, bf16[384,256]{1,0:T(8,128)(2,1)S(1)} %collective-permute-done.16.refs_1_, bf16[1536,512]{1,0:T(8,128)(2,1)S(1)} %unpack.1.refs_2_, s32[1536,128]{1,0:T(8,128)S(1)} %get-tuple-element.55.refs_14_.refs_3_, ...), custom_call_target="tpu_custom_call" | custom-call | tf_op jit(solution)/shard_map/final/pallas_call | solution.py:592
  (65 shorter events, 10.6 us)
Async XLA Ops:
  1.2 1.4 copy-start
  2.7 0.7 copy-start.7
  3.3 11.8 %copy-start.2 = (bf16[512,1024]{1,0:T(8,128)(2,1)S(1)}, bf16[512,1024]{1,0:T(8,128)(2,1)}, u32[]{:S(2)}) copy-start(bf16[512,1024]{1,0:T(8,128)(2,1)} %refs_7_.1) | copy-start | bytes 3145732
  3.3 14.4 %copy-start.4 = (bf16[256,512]{1,0:T(8,128)(2,1)S(1)}, bf16[256,512]{1,0:T(8,128)(2,1)}, u32[]{:S(2)}) copy-start(bf16[256,512]{1,0:T(8,128)(2,1)} %refs_6_.1) | copy-start | bytes 786436
  5.5 66.3 %copy-start.5 = (bf16[2,512,256]{2,1,0:T(8,128)(2,1)S(1)}, bf16[2,512,256]{2,1,0:T(8,128)(2,1)}, u32[]{:S(2)}) copy-start(bf16[2,512,256]{2,1,0:T(8,128)(2,1)} %refs_10_.1) | copy-start | bytes 1572868
  9.0 0.7 copy-start.11
  10.3 0.7 copy-start.14
  11.0 1.6 copy-start.10
  11.0 1.6 copy-start.12
  11.0 12.4 %collective-permute-start.2 = (bf16[400,256]{1,0:T(8,128)(2,1)}, bf16[400,256]{1,0:T(8,128)(2,1)S(1)}, u32[]{:S(2)}, u32[]{:S(2)}) collective-permute-start(bf16[400,256]{1,0:T(8,128)(2,1)} %get-tuple-element.38), channel_id=1, source_target_pairs={{0,4},{1,5},{4,0},{5,1},{8,12},{9,13},{12,8},{13,9},{2,6},{3,7},{6... | collective-permute-start | bytes 614408 | tf_op jit(solution)/shard_map/ppermute | solution.py:483
  12.6 11.4 %collective-permute-start.1 = (bf16[400,256]{1,0:T(8,128)(2,1)}, bf16[400,256]{1,0:T(8,128)(2,1)S(1)}, u32[]{:S(2)}, u32[]{:S(2)}) collective-permute-start(bf16[400,256]{1,0:T(8,128)(2,1)} %get-tuple-element.37), channel_id=1, source_target_pairs={{0,8},{1,9},{4,12},{5,13},{8,0},{9,1},{12,4},{13,5},{2,10},{3,11},... | collective-permute-start | bytes 614408 | tf_op jit(solution)/shard_map/ppermute | solution.py:483
  17.7 9.5 %collective-permute-start.5 = (bf16[400,256]{1,0:T(8,128)(2,1)}, bf16[400,256]{1,0:T(8,128)(2,1)S(1)}, u32[]{:S(2)}, u32[]{:S(2)}) collective-permute-start(bf16[400,256]{1,0:T(8,128)(2,1)} %copy-done.14), channel_id=1, source_target_pairs={{0,5},{1,4},{4,1},{5,0},{8,13},{9,12},{12,9},{13,8},{2,7},{3,6},{6... | collective-permute-start | bytes 614408 | tf_op jit(solution)/shard_map/ppermute | solution.py:483
  17.8 32.3 %collective-permute-start = (bf16[400,512]{1,0:T(8,128)(2,1)}, bf16[400,512]{1,0:T(8,128)(2,1)S(1)}, u32[]{:S(2)}, u32[]{:S(2)}) collective-permute-start(bf16[400,512]{1,0:T(8,128)(2,1)} %copy-done.10), channel_id=1, source_target_pairs={{0,1},{1,0},{4,5},{5,4},{8,9},{9,8},{12,13},{13,12},{2,3},{3,2},{6... | collective-permute-start | bytes 1228808 | tf_op jit(solution)/shard_map/ppermute | solution.py:478
  18.7 15.8 %collective-permute-start.3 = (bf16[400,256]{1,0:T(8,128)(2,1)}, bf16[400,256]{1,0:T(8,128)(2,1)S(1)}, u32[]{:S(2)}, u32[]{:S(2)}) collective-permute-start(bf16[400,256]{1,0:T(8,128)(2,1)} %copy-done.13), channel_id=1, source_target_pairs={{0,12},{1,13},{4,8},{5,9},{8,4},{9,5},{12,0},{13,1},{2,14},{3,15},... | collective-permute-start | bytes 614408 | tf_op jit(solution)/shard_map/ppermute | solution.py:483
  23.4 23.1 %collective-permute-start.4 = (bf16[400,256]{1,0:T(8,128)(2,1)}, bf16[400,256]{1,0:T(8,128)(2,1)S(1)}, u32[]{:S(2)}, u32[]{:S(2)}) collective-permute-start(bf16[400,256]{1,0:T(8,128)(2,1)} %copy-done.12), channel_id=1, source_target_pairs={{0,9},{1,8},{4,13},{5,12},{8,1},{9,0},{12,5},{13,4},{2,11},{3,10},... | collective-permute-start | bytes 614408 | tf_op jit(solution)/shard_map/ppermute | solution.py:483
  24.0 24.1 %collective-permute-start.6 = (bf16[400,256]{1,0:T(8,128)(2,1)}, bf16[400,256]{1,0:T(8,128)(2,1)S(1)}, u32[]{:S(2)}, u32[]{:S(2)}) collective-permute-start(bf16[400,256]{1,0:T(8,128)(2,1)} %copy-done.11), channel_id=1, source_target_pairs={{0,13},{1,12},{4,9},{5,8},{8,5},{9,4},{12,1},{13,0},{2,15},{3,14},... | collective-permute-start | bytes 614408 | tf_op jit(solution)/shard_map/ppermute | solution.py:483
  27.2 21.3 %collective-permute-start.12 = (bf16[400,256]{1,0:T(8,128)(2,1)S(1)}, bf16[400,256]{1,0:T(8,128)(2,1)S(1)}, u32[]{:S(2)}, u32[]{:S(2)}) collective-permute-start(bf16[400,256]{1,0:T(8,128)(2,1)S(1)} %collective-permute-done.2.refs_3_.refs_8_), channel_id=1, source_target_pairs={{0,2},{2,0},{1,3},{3,1},{4,6},{6,4},{5,7},{7,5},{8,10},{10,8},{9,1... | collective-permute-start | bytes 614408 | tf_op jit(solution)/shard_map/ppermute | solution.py:423
  34.5 16.1 %collective-permute-start.11 = (bf16[400,256]{1,0:T(8,128)(2,1)S(1)}, bf16[400,256]{1,0:T(8,128)(2,1)S(1)}, u32[]{:S(2)}, u32[]{:S(2)}) collective-permute-start(bf16[400,256]{1,0:T(8,128)(2,1)S(1)} %collective-permute-done.1.refs_2_.refs_6_), channel_id=1, source_target_pairs={{0,2},{2,0},{1,3},{3,1},{4,6},{6,4},{5,7},{7,5},{8,10},{10,8},{9,1... | collective-permute-start | bytes 614408 | tf_op jit(solution)/shard_map/ppermute | solution.py:423
  46.5 60.6 %collective-permute-start.28 = (bf16[512,512]{1,0:T(8,128)(2,1)}, bf16[512,512]{1,0:T(8,128)(2,1)S(1)}, u32[]{:S(2)}, u32[]{:S(2)}) collective-permute-start(bf16[512,512]{1,0:T(8,128)(2,1)} %constant_dynamic-slice_fusion.1), channel_id=1, source_target_pairs={{0,2},{2,0},{1,3},{3,1},{4,6},{6,4},{5,7},{7,5},{8,10},{10,8},{9,1... | collective-permute-start | bytes 1572872 | tf_op jit(solution)/shard_map/ppermute | solution.py:423
  48.0 17.9 %collective-permute-start.10 = (bf16[400,256]{1,0:T(8,128)(2,1)S(1)}, bf16[400,256]{1,0:T(8,128)(2,1)S(1)}, u32[]{:S(2)}, u32[]{:S(2)}) collective-permute-start(bf16[400,256]{1,0:T(8,128)(2,1)S(1)} %collective-permute-done.5.refs_6_.refs_12_), channel_id=1, source_target_pairs={{0,2},{2,0},{1,3},{3,1},{4,6},{6,4},{5,7},{7,5},{8,10},{10,8},{9,1... | collective-permute-start | bytes 614408 | tf_op jit(solution)/shard_map/ppermute | solution.py:423
  48.5 21.7 %collective-permute-start.8 = (bf16[400,256]{1,0:T(8,128)(2,1)S(1)}, bf16[400,256]{1,0:T(8,128)(2,1)S(1)}, u32[]{:S(2)}, u32[]{:S(2)}) collective-permute-start(bf16[400,256]{1,0:T(8,128)(2,1)S(1)} %collective-permute-done.3.refs_4_.refs_8_), channel_id=1, source_target_pairs={{0,2},{2,0},{1,3},{3,1},{4,6},{6,4},{5,7},{7,5},{8,10},{10,8},{9,1... | collective-permute-start | bytes 614408 | tf_op jit(solution)/shard_map/ppermute | solution.py:423
  50.0 24.6 %collective-permute-start.9 = (bf16[400,256]{1,0:T(8,128)(2,1)S(1)}, bf16[400,256]{1,0:T(8,128)(2,1)S(1)}, u32[]{:S(2)}, u32[]{:S(2)}) collective-permute-start(bf16[400,256]{1,0:T(8,128)(2,1)S(1)} %collective-permute-done.4.refs_5_.refs_10_), channel_id=1, source_target_pairs={{0,2},{2,0},{1,3},{3,1},{4,6},{6,4},{5,7},{7,5},{8,10},{10,8},{9,1... | collective-permute-start | bytes 614408 | tf_op jit(solution)/shard_map/ppermute | solution.py:423
  50.6 28.5 %collective-permute-start.7 = (bf16[400,256]{1,0:T(8,128)(2,1)S(1)}, bf16[400,256]{1,0:T(8,128)(2,1)S(1)}, u32[]{:S(2)}, u32[]{:S(2)}) collective-permute-start(bf16[400,256]{1,0:T(8,128)(2,1)S(1)} %collective-permute-done.6.refs_7_.refs_14_), channel_id=1, source_target_pairs={{0,2},{2,0},{1,3},{3,1},{4,6},{6,4},{5,7},{7,5},{8,10},{10,8},{9,1... | collective-permute-start | bytes 614408 | tf_op jit(solution)/shard_map/ppermute | solution.py:423
  65.9 38.8 %collective-permute-start.29 = (bf16[512,256]{1,0:T(8,128)(2,1)}, bf16[512,256]{1,0:T(8,128)(2,1)S(1)}, u32[]{:S(2)}, u32[]{:S(2)}) collective-permute-start(bf16[512,256]{1,0:T(8,128)(2,1)} %dynamic_slice.10), channel_id=1, source_target_pairs={{0,2},{2,0},{1,3},{3,1},{4,6},{6,4},{5,7},{7,5},{8,10},{10,8},{9,1... | collective-permute-start | bytes 786440 | tf_op jit(solution)/shard_map/ppermute | solution.py:423
  70.3 29.0 %collective-permute-start.30 = (bf16[128,512]{1,0:T(8,128)(2,1)S(1)}, bf16[128,512]{1,0:T(8,128)(2,1)S(1)}, u32[]{:S(2)}, u32[]{:S(2)}) collective-permute-start(bf16[128,512]{1,0:T(8,128)(2,1)S(1)} %constant_dynamic-slice_fusion), channel_id=1, source_target_pairs={{0,2},{2,0},{1,3},{3,1},{4,6},{6,4},{5,7},{7,5},{8,10},{10,8},{9,1... | collective-permute-start | bytes 393224 | tf_op jit(solution)/shard_map/ppermute | solution.py:423
  71.8 1.0 copy-start.6
  74.7 4.4 %copy-start.9 = (s32[128]{0:T(128)S(1)}, s32[128]{0:T(128)}, u32[]{:S(2)}) copy-start(s32[128]{0:T(128)} %counts_ref.1) | copy-start | bytes 1540
  81.8 25.7 %collective-permute-start.20 = (bf16[384,256]{1,0:T(8,128)(2,1)S(1)}, bf16[384,256]{1,0:T(8,128)(2,1)S(1)}, u32[]{:S(2)}, u32[]{:S(2)}) collective-permute-start(bf16[384,256]{1,0:T(8,128)(2,1)S(1)} %fetch.3), channel_id=1, source_target_pairs={{0,8},{1,9},{4,12},{5,13},{8,0},{9,1},{12,4},{13,5},{2,10},{3,11},... | collective-permute-start | bytes 589832 | tf_op jit(solution)/shard_map/ppermute | solution.py:574
  90.9 17.9 %collective-permute-start.18 = (bf16[384,256]{1,0:T(8,128)(2,1)S(1)}, bf16[384,256]{1,0:T(8,128)(2,1)S(1)}, u32[]{:S(2)}, u32[]{:S(2)}) collective-permute-start(bf16[384,256]{1,0:T(8,128)(2,1)S(1)} %get-tuple-element.51), channel_id=1, source_target_pairs={{0,1},{1,0},{4,5},{5,4},{8,9},{9,8},{12,13},{13,12},{2,3},{3,2},{6... | collective-permute-start | bytes 589832 | tf_op jit(solution)/shard_map/ppermute | solution.py:574
  99.3 11.7 %collective-permute-start.22 = (bf16[384,256]{1,0:T(8,128)(2,1)S(1)}, bf16[384,256]{1,0:T(8,128)(2,1)S(1)}, u32[]{:S(2)}, u32[]{:S(2)}) collective-permute-start(bf16[384,256]{1,0:T(8,128)(2,1)S(1)} %get-tuple-element.52), channel_id=1, source_target_pairs={{0,4},{1,5},{4,0},{5,1},{8,12},{9,13},{12,8},{13,9},{2,6},{3,7},{6... | collective-permute-start | bytes 589832 | tf_op jit(solution)/shard_map/ppermute | solution.py:574
  104.7 12.4 %collective-permute-start.24 = (bf16[384,256]{1,0:T(8,128)(2,1)S(1)}, bf16[384,256]{1,0:T(8,128)(2,1)S(1)}, u32[]{:S(2)}, u32[]{:S(2)}) collective-permute-start(bf16[384,256]{1,0:T(8,128)(2,1)S(1)} %get-tuple-element.53), channel_id=1, source_target_pairs={{0,12},{1,13},{4,8},{5,9},{8,4},{9,5},{12,0},{13,1},{2,14},{3,15},... | collective-permute-start | bytes 589832 | tf_op jit(solution)/shard_map/ppermute | solution.py:574
  107.1 17.8 %collective-permute-start.26 = (bf16[384,256]{1,0:T(8,128)(2,1)S(1)}, bf16[384,256]{1,0:T(8,128)(2,1)S(1)}, u32[]{:S(2)}, u32[]{:S(2)}) collective-permute-start(bf16[384,256]{1,0:T(8,128)(2,1)S(1)} %get-tuple-element.54), channel_id=1, source_target_pairs={{0,9},{1,8},{4,13},{5,12},{8,1},{9,0},{12,5},{13,4},{2,11},{3,10},... | collective-permute-start | bytes 589832 | tf_op jit(solution)/shard_map/ppermute | solution.py:574
  107.4 22.6 %collective-permute-start.13 = (bf16[384,256]{1,0:T(8,128)(2,1)S(1)}, bf16[384,256]{1,0:T(8,128)(2,1)S(1)}, u32[]{:S(2)}, u32[]{:S(2)}) collective-permute-start(bf16[384,256]{1,0:T(8,128)(2,1)S(1)} %get-tuple-element.48), channel_id=1, source_target_pairs={{0,5},{1,4},{4,1},{5,0},{8,13},{9,12},{12,9},{13,8},{2,7},{3,6},{6... | collective-permute-start | bytes 589832 | tf_op jit(solution)/shard_map/ppermute | solution.py:574
  108.8 21.7 %collective-permute-start.15 = (bf16[384,256]{1,0:T(8,128)(2,1)S(1)}, bf16[384,256]{1,0:T(8,128)(2,1)S(1)}, u32[]{:S(2)}, u32[]{:S(2)}) collective-permute-start(bf16[384,256]{1,0:T(8,128)(2,1)S(1)} %get-tuple-element.49), channel_id=1, source_target_pairs={{0,13},{1,12},{4,9},{5,8},{8,5},{9,4},{12,1},{13,0},{2,15},{3,14},... | collective-permute-start | bytes 589832 | tf_op jit(solution)/shard_map/ppermute | solution.py:574
  111.0 21.1 %collective-permute-start.17 = (bf16[384,256]{1,0:T(8,128)(2,1)S(1)}, bf16[384,256]{1,0:T(8,128)(2,1)S(1)}, u32[]{:S(2)}, u32[]{:S(2)}) collective-permute-start(bf16[384,256]{1,0:T(8,128)(2,1)S(1)} %get-tuple-element.50.refs_0_), channel_id=1, source_target_pairs={{0,2},{2,0},{1,3},{3,1},{4,6},{6,4},{5,7},{7,5},{8,10},{10,8},{9,1... | collective-permute-start | bytes 589832 | tf_op jit(solution)/shard_map/ppermute | solution.py:423
  117.1 15.5 %collective-permute-start.21 = (bf16[384,256]{1,0:T(8,128)(2,1)S(1)}, bf16[384,256]{1,0:T(8,128)(2,1)S(1)}, u32[]{:S(2)}, u32[]{:S(2)}) collective-permute-start(bf16[384,256]{1,0:T(8,128)(2,1)S(1)} %collective-permute-done.20.refs_4_), channel_id=1, source_target_pairs={{0,2},{2,0},{1,3},{3,1},{4,6},{6,4},{5,7},{7,5},{8,10},{10,8},{9,1... | collective-permute-start | bytes 589832 | tf_op jit(solution)/shard_map/ppermute | solution.py:423
  124.9 33.0 %collective-permute-start.31 = (bf16[512,512]{1,0:T(8,128)(2,1)S(1)}, bf16[512,512]{1,0:T(8,128)(2,1)S(1)}, u32[]{:S(2)}, u32[]{:S(2)}) collective-permute-start(bf16[512,512]{1,0:T(8,128)(2,1)S(1)} %collective-permute-done.28.refs_9_), channel_id=1, source_target_pairs={{1,0},{0,1},{3,2},{2,3},{5,4},{4,5},{7,6},{6,7},{9,8},{8,9},{11,10... | collective-permute-start | bytes 1572872 | tf_op jit(solution)/shard_map/ppermute | solution.py:492
  130.0 7.8 %collective-permute-start.19 = (bf16[384,256]{1,0:T(8,128)(2,1)S(1)}, bf16[384,256]{1,0:T(8,128)(2,1)S(1)}, u32[]{:S(2)}, u32[]{:S(2)}) collective-permute-start(bf16[384,256]{1,0:T(8,128)(2,1)S(1)} %collective-permute-done.18.refs_2_), channel_id=1, source_target_pairs={{0,2},{2,0},{1,3},{3,1},{4,6},{6,4},{5,7},{7,5},{8,10},{10,8},{9,1... | collective-permute-start | bytes 589832 | tf_op jit(solution)/shard_map/ppermute | solution.py:423
  130.6 11.5 %collective-permute-start.23 = (bf16[384,256]{1,0:T(8,128)(2,1)S(1)}, bf16[384,256]{1,0:T(8,128)(2,1)S(1)}, u32[]{:S(2)}, u32[]{:S(2)}) collective-permute-start(bf16[384,256]{1,0:T(8,128)(2,1)S(1)} %collective-permute-done.22.refs_6_), channel_id=1, source_target_pairs={{0,2},{2,0},{1,3},{3,1},{4,6},{6,4},{5,7},{7,5},{8,10},{10,8},{9,1... | collective-permute-start | bytes 589832 | tf_op jit(solution)/shard_map/ppermute | solution.py:423
  132.1 14.2 %collective-permute-start.25 = (bf16[384,256]{1,0:T(8,128)(2,1)S(1)}, bf16[384,256]{1,0:T(8,128)(2,1)S(1)}, u32[]{:S(2)}, u32[]{:S(2)}) collective-permute-start(bf16[384,256]{1,0:T(8,128)(2,1)S(1)} %collective-permute-done.24.refs_8_), channel_id=1, source_target_pairs={{0,2},{2,0},{1,3},{3,1},{4,6},{6,4},{5,7},{7,5},{8,10},{10,8},{9,1... | collective-permute-start | bytes 589832 | tf_op jit(solution)/shard_map/ppermute | solution.py:423
  132.6 17.9 %collective-permute-start.27 = (bf16[384,256]{1,0:T(8,128)(2,1)S(1)}, bf16[384,256]{1,0:T(8,128)(2,1)S(1)}, u32[]{:S(2)}, u32[]{:S(2)}) collective-permute-start(bf16[384,256]{1,0:T(8,128)(2,1)S(1)} %collective-permute-done.26.refs_10_), channel_id=1, source_target_pairs={{0,2},{2,0},{1,3},{3,1},{4,6},{6,4},{5,7},{7,5},{8,10},{10,8},{9,1... | collective-permute-start | bytes 589832 | tf_op jit(solution)/shard_map/ppermute | solution.py:423
  137.8 18.9 %collective-permute-start.32 = (bf16[512,256]{1,0:T(8,128)(2,1)S(1)}, bf16[512,256]{1,0:T(8,128)(2,1)S(1)}, u32[]{:S(2)}, u32[]{:S(2)}) collective-permute-start(bf16[512,256]{1,0:T(8,128)(2,1)S(1)} %collective-permute-done.29.refs_10_), channel_id=1, source_target_pairs={{1,0},{0,1},{3,2},{2,3},{5,4},{4,5},{7,6},{6,7},{9,8},{8,9},{11,10... | collective-permute-start | bytes 786440 | tf_op jit(solution)/shard_map/ppermute | solution.py:492
  142.0 14.7 %collective-permute-start.14 = (bf16[384,256]{1,0:T(8,128)(2,1)S(1)}, bf16[384,256]{1,0:T(8,128)(2,1)S(1)}, u32[]{:S(2)}, u32[]{:S(2)}) collective-permute-start(bf16[384,256]{1,0:T(8,128)(2,1)S(1)} %collective-permute-done.13.refs_12_), channel_id=1, source_target_pairs={{0,2},{2,0},{1,3},{3,1},{4,6},{6,4},{5,7},{7,5},{8,10},{10,8},{9,1... | collective-permute-start | bytes 589832 | tf_op jit(solution)/shard_map/ppermute | solution.py:423
  146.2 11.7 %collective-permute-start.16 = (bf16[384,256]{1,0:T(8,128)(2,1)S(1)}, bf16[384,256]{1,0:T(8,128)(2,1)S(1)}, u32[]{:S(2)}, u32[]{:S(2)}) collective-permute-start(bf16[384,256]{1,0:T(8,128)(2,1)S(1)} %collective-permute-done.15.refs_13_), channel_id=1, source_target_pairs={{0,2},{2,0},{1,3},{3,1},{4,6},{6,4},{5,7},{7,5},{8,10},{10,8},{9,1... | collective-permute-start | bytes 589832 | tf_op jit(solution)/shard_map/ppermute | solution.py:423
  150.5 6.2 %collective-permute-start.33 = (bf16[128,512]{1,0:T(8,128)(2,1)S(1)}, bf16[128,512]{1,0:T(8,128)(2,1)S(1)}, u32[]{:S(2)}, u32[]{:S(2)}) collective-permute-start(bf16[128,512]{1,0:T(8,128)(2,1)S(1)} %collective-permute-done.30.refs_11_), channel_id=1, source_target_pairs={{1,0},{0,1},{3,2},{2,3},{5,4},{4,5},{7,6},{6,7},{9,8},{8,9},{11,10... | collective-permute-start | bytes 393224 | tf_op jit(solution)/shard_map/ppermute | solution.py:492
  150.5 7.5 %copy-start.1 = (bf16[1536,512]{1,0:T(8,128)(2,1)S(1)}, bf16[1536,512]{1,0:T(8,128)(2,1)}, u32[]{:S(2)}) copy-start(bf16[1536,512]{1,0:T(8,128)(2,1)} %refs_4_.1) | copy-start | bytes 4718596
  150.5 7.5 %copy-start.3 = (bf16[1024,512]{1,0:T(8,128)(2,1)S(1)}, bf16[1024,512]{1,0:T(8,128)(2,1)}, u32[]{:S(2)}) copy-start(bf16[1024,512]{1,0:T(8,128)(2,1)} %refs_8_.1) | copy-start | bytes 3145732
  150.5 7.5 %copy-start.8 = (f32[512]{0:T(512)S(1)}, f32[512]{0:T(512)}, u32[]{:S(2)}) copy-start(f32[512]{0:T(512)} %param.18) | copy-start | bytes 6148
  (1 other events, 0.7 us)
